TPU v7x, 32 devices: a whole 2x2x4 slice. The times are simulated.
32 devices in a mesh: lat: 4 (over y, x), lon: 8 (over z, core).
Axes of the slice: x: 2, y: 2, z: 4, core: 2. Of those that a mesh axis runs over, the one named last changes fastest.
Arguments:
- field: float32 [64, 2048, 128], P('lat', 'lon'), may hold values from -6 to 6
- ocean: int32 [64, 2048], P('lat', 'lon'), may hold values 0 or 1
- modes: int32 [16], replicated, may hold values from 1 to 1023, as said below
- spectral_weight: float32 [16, 2, 128, 128], P('lon'), may hold values from -0.375 to 0.375
- local_weight: float32 [128, 128], replicated, may hold values from -0.5 to 0.5
- layer_bias: float32 [128], replicated, may hold values from -4 to 4
- conv_weight: float32 [3, 3, 128, 128], replicated, may hold values from -0.1875 to 0.1875
- conv_bias: float32 [128], replicated, may hold values from -2 to 2
Outputs:
- decoded: float32 [64, 2048, 128], P('lat', 'lon')
Inputs may be any that keep to these rules, and one draw needn't show every extreme that they name: `modes`: distinct wavenumbers.
All inputs are finite; a program needn't handle non-finite values. No bound on the sum of `ocean` on one device may be relied on, other than what follows from the above.
Results may differ from a plain program's by a relative error of at most 0.0001.
Values sent between devices are 32-bit elements; how exact they have to be, the bound alone decides.
No kernel may reach another device: no remote copies, remote signals or barrier semaphores. Data moves between devices by JAX's collectives and lax.ppermute only.
A program may use at most 64 MiB of HBM per device.

v0:
```python
import math

import jax
import jax.numpy as jnp
from jax import lax
from jax.sharding import PartitionSpec as P

HIGH = lax.Precision.HIGHEST


def with_halo(block, sides, width, periodic):
    for axis, dim in sides:
        count = lax.axis_size(axis)
        forward = [(i, i + 1) for i in range(count - 1)]
        if periodic:
            forward.append((count - 1, 0))
        backward = [(target, source) for source, target in forward]
        low = lax.ppermute(
            lax.slice_in_dim(block, block.shape[dim] - width, None, axis=dim), axis, forward
        )
        high = lax.ppermute(lax.slice_in_dim(block, 0, width, axis=dim), axis, backward)
        block = jnp.concatenate([low, block, high], axis=dim)
    return block


def tables(mode_ids, lon_start, width, total_lon):
    lon_ids = lon_start + jnp.arange(width, dtype=jnp.int32)
    product = mode_ids[:, None] * lon_ids[None, :] % total_lon
    theta = product.astype(jnp.float32) * (2.0 * math.pi / total_lon)
    return (jnp.cos(theta), jnp.sin(theta))


def forward_terms(field, cosine, sine, total_lon):
    real_part = jnp.einsum("mj,ijc->mic", cosine, field, precision=HIGH) / math.sqrt(total_lon)
    imag_part = -jnp.einsum("mj,ijc->mic", sine, field, precision=HIGH) / math.sqrt(total_lon)
    return jnp.concatenate([real_part, imag_part], -1)


def mix_modes(coeffs, weights):
    w_real = weights[:, 0]
    w_imag = weights[:, 1]
    upper = jnp.concatenate([w_real, w_imag], -1)
    lower = jnp.concatenate([-w_imag, w_real], -1)
    blocks = jnp.concatenate([upper, lower], 1)
    return jnp.einsum("mic,mcd->mid", coeffs, blocks, precision=HIGH)


def inverse_terms(mixed, cosine, sine, channels):
    result = jnp.einsum("mj,mic->ijc", cosine, mixed[:, :, :channels], precision=HIGH)
    return result - jnp.einsum("mj,mic->ijc", sine, mixed[:, :, channels:], precision=HIGH)


def per_device(
    field, ocean, modes, spectral_weight, local_weight, layer_bias, conv_weight, conv_bias
):
    rows, width, channels = field.shape
    lon_count = lax.axis_size("lon")
    total_lon = width * lon_count
    total_modes = modes.shape[0]
    lon_start = lax.axis_index("lon") * width
    scale = 2.0 / math.sqrt(total_modes)
    cosine, sine = tables(modes, lon_start, width, total_lon)
    partial_coeffs = forward_terms(field, cosine, sine, total_lon)
    own_coeffs = lax.psum_scatter(partial_coeffs, "lon", scatter_dimension=0, tiled=True)
    own_mixed = mix_modes(own_coeffs, spectral_weight)
    mixed = lax.all_gather(own_mixed, "lon", axis=0, tiled=True)
    spectral = inverse_terms(mixed, cosine, sine, channels) * scale
    wet = ocean.astype(jnp.float32)[:, :, None]
    local = jnp.einsum("ijc,cd->ijd", field, local_weight, precision=HIGH)
    hidden = wet * jax.nn.gelu(spectral + local + layer_bias, approximate=True)
    with_rows = with_halo(hidden, (("lat", 0),), 1, False)
    padded = with_halo(with_rows, (("lon", 1),), 1, True)
    conv = jnp.zeros((rows, width, channels), jnp.float32)
    for row_tap in range(3):
        for col_tap in range(3):
            window = padded[row_tap : row_tap + rows, col_tap : col_tap + width]
            conv = conv + jnp.einsum(
                "ijc,cd->ijd", window, conv_weight[row_tap, col_tap], precision=HIGH
            )
    return wet * (conv + conv_bias)


def solution(mesh):
    in_specs = (
        P("lat", "lon", None),
        P("lat", "lon"),
        P(),
        P("lon", None, None, None),
        P(),
        P(),
        P(),
        P(),
    )
    out_specs = P("lat", "lon", None)
    return jax.shard_map(
        per_device, mesh=mesh, in_specs=in_specs, out_specs=out_specs, check_vma=False
    )
```

profile of v0, /device:TPU:0, one launch (start us, length us, event | category | flops | bytes accessed | tf_op | source)
XLA Modules:
  0.0 127.5 jit_solution(14861475375408570328)
XLA Ops:
  6.5 0.0 copy-start
  6.5 0.0 copy-start.11
  6.5 0.0 reduce-scatter.2.cloned.1.call-start
  6.5 1.6 %copy-done = f32[16,256,128]{2,1,0:T(8,128)S(1)} copy-done((f32[16,256,128]{2,1,0:T(8,128)S(1)}, f32[16,256,128]{2,1,0:T(8,128)}, u32[]{:S(2)}) %copy-start) | copy-done | bytes 2097176
  8.1 1.9 %fusion.70 = f32[16,16,128]{2,0,1:T(8,128)S(1)} fusion(f32[16,256,128]{2,1,0:T(8,128)S(1)} %copy-done, s32[256]{0:T(256)S(1)} %iota_add_fusion, s32[16]{0:T(128)} %param.10), kind=kOutput, calls=%fused_computation.82 | convolution fusion | flops 100720640 | bytes 2229312 | tf_op jit(solution)/shard_map/mj,ijc->mic/dot_general | solution.py:35
  10.0 0.0 copy-done.11
  10.0 0.0 copy-start.8
  10.0 0.0 copy-start.10
  10.0 0.0 copy-start.9
  10.1 1.2 fusion.73
  11.3 0.1 fusion.40
  11.4 0.7 pad_maximum_fusion.2
  12.1 0.0 reduce-scatter.2.cloned.1.call-update
  12.2 0.0 copy-done.8
  12.2 0.0 copy-done.10
  12.2 0.0 copy-done.9
  12.2 3.3 %fusion.55 = f32[16,256,128]{1,2,0:T(8,128)} fusion(f32[16,256,128]{2,1,0:T(8,128)S(1)} %copy-done, f32[128,128]{1,0:T(8,128)S(1)} %copy-done.9), kind=kOutput, calls=%fused_computation.62 | convolution fusion | flops 805306368 | bytes 4259840 | tf_op jit(solution)/shard_map/ijc,cd->ijd/dot_general | solution.py:69
  15.6 0.0 copy-start.13
  15.6 30.2 %reduce-scatter.2.cloned.1.call-done = f32[2,16,256]{2,1,0:T(8,128)} async-done(((f32[16,16,256]{2,1,0:T(8,128)}), f32[2,16,256]{2,1,0:T(8,128)}) %reduce-scatter.2.cloned.1.call-update) | async-done | bytes 32784 | tf_op jit(solution)/shard_map/reduce_scatter | solution.py:64
  45.8 0.0 copy-start.6
  45.8 1.2 fusion.29
  47.1 14.2 %all_gather.3 = f32[16,16,256]{2,1,0:T(8,128)S(1)} all-gather(f32[2,16,256]{2,1,0:T(8,128)S(1)} %fusion.29), channel_id=1, replica_groups=mesh['lat'=4,'lon'=8] {'lon'}, dimensions={0}, use_global_device_ids=true | all-gather | bytes 294912 | tf_op jit(solution)/shard_map/all_gather | solution.py:66
  61.2 1.9 %fusion.38 = f32[16,128,256]{2,1,0:T(8,128)S(1)} fusion(f32[16,16,128]{2,1,0:T(8,128)S(1)} %get-tuple-element.12, s32[256]{0:T(256)S(1)} %iota_add_fusion, s32[16]{0:T(128)S(1)} %copy-done.11), kind=kOutput, calls=%fused_computation.45 | convolution fusion | flops 100720640 | bytes 2229312 | tf_op jit(solution)/shard_map/mj,mic->ijc/dot_general | solution.py:49
  63.2 0.0 copy-done.13
  63.2 0.0 copy-done.6
  63.2 2.8 %fusion.15 = f32[16,256,128]{1,2,0:T(8,128)S(1)} fusion(f32[16,256,128]{1,2,0:T(8,128)S(1)} %copy-done.6, f32[16,128,256]{2,1,0:T(8,128)S(1)} %fusion.38, f32[128]{0:T(128)S(1)} %copy-done.13, f32[16,256]{1,0:T(8,128)S(1)} %convert_element_type.6, f32[16,16,128]{2,1,0:T(8,128)S(1)} %get-tuple-element.11, s32[256]{0:T(256)S(1)} %iota_add_fusion, ...), kind=kOutput, calls=%fused_computation.19 | convolution fusion | flops 107536384 | bytes 6440512 | tf_op jit(solution)/shard_map/mj,mic->ijc/dot_general | solution.py:50
  66.0 0.0 copy-start.1
  66.1 3.4 %collective-permute-start = (f32[1,256,128]{1,2,0:T(8,128)S(1)}, f32[1,256,128]{1,2,0:T(8,128)S(1)}, u32[]{:S(2)}, u32[]{:S(2)}) collective-permute-start(f32[1,256,128]{1,2,0:T(8,128)S(1)} %get-tuple-element.9), channel_id=1, source_target_pairs={{0,8},{8,16},{16,24},{1,9},{9,17},{17,25},{2,10},{10,18},{18,26},{... | collective-permute-start | bytes 393224 | tf_op jit(solution)/shard_map/ppermute | solution.py:18
  69.5 1.5 %collective-permute-start.1 = (f32[1,256,128]{1,2,0:T(8,128)S(1)}, f32[1,256,128]{1,2,0:T(8,128)S(1)}, u32[]{:S(2)}, u32[]{:S(2)}) collective-permute-start(f32[1,256,128]{1,2,0:T(8,128)S(1)} %get-tuple-element.10), channel_id=1, source_target_pairs={{8,0},{16,8},{24,16},{9,1},{17,9},{25,17},{10,2},{18,10},{26,18},{... | collective-permute-start | bytes 393224 | tf_op jit(solution)/shard_map/ppermute | solution.py:21
  71.0 4.2 %fusion.49 = f32[16,256,128]{1,2,0:T(8,128)} fusion(f32[16,256,128]{1,2,0:T(8,128)S(1)} %fusion.15, f32[3,3,128,128]{3,2,1,0:T(8,128)} %param.14), kind=kOutput, calls=%fused_computation.56 | convolution fusion | flops 805306368 | bytes 4259840 | tf_op jit(solution)/shard_map/ijc,cd->ijd/dot_general | solution.py:77
  75.1 0.0 collective-permute-done
  75.1 2.3 %collective-permute-done.1 = f32[1,256,128]{1,2,0:T(8,128)S(1)} collective-permute-done((f32[1,256,128]{1,2,0:T(8,128)S(1)}, f32[1,256,128]{1,2,0:T(8,128)S(1)}, u32[]{:S(2)}, u32[]{:S(2)}) %collective-permute-start.1) | collective-permute-done | bytes 131104 | tf_op jit(solution)/shard_map/ppermute | solution.py:21
  77.5 0.0 copy-done.1
  77.5 0.2 pad_maximum_fusion.1
  77.7 1.4 %fusion.101 = (f32[18,1,128]{1,2,0:T(8,128)S(1)}, f32[18,1,128]{1,2,0:T(8,128)}) fusion(f32[18,256,128]{1,2,0:T(8,128)S(1)} %pad_maximum_fusion.1), kind=kLoop, calls=%fused_computation.110 | loop fusion | bytes 36864 | tf_op jit(solution)/shard_map/slice | solution.py:21
  79.2 2.2 %copy.38 = f32[18,1,128]{2,1,0:T(1,128)} copy(f32[18,1,128]{1,2,0:T(8,128)} %get-tuple-element.8) | data formatting | bytes 18432 | tf_op jit(solution)/shard_map/slice | solution.py:19
  81.4 0.0 collective-permute-start.2
  81.4 0.9 copy.44
  82.3 0.0 copy-start.2
  82.3 3.5 %collective-permute-start.3 = (f32[18,1,128]{2,1,0:T(1,128)}, f32[18,1,128]{2,1,0:T(1,128)}, u32[]{:S(2)}, u32[]{:S(2)}) collective-permute-start(f32[18,1,128]{2,1,0:T(1,128)} %copy.44), channel_id=1, source_target_pairs={{1,0},{2,1},{3,2},{4,3},{5,4},{6,5},{7,6},{0,7},{9,8},{10,9},{11,1... | collective-permute-start | bytes 27656 | tf_op jit(solution)/shard_map/ppermute | solution.py:21
  85.9 4.8 %fusion = f32[16,256,128]{1,2,0:T(8,128)} fusion(f32[16,256,128]{1,2,0:T(8,128)} %copy-done.1, f32[1,256,128]{1,2,0:T(8,128)S(1)} %collective-permute-done, f32[3,3,128,128]{3,2,1,0:T(8,128)} %param.14), kind=kOutput, calls=%fused_computation.4 | convolution fusion | flops 805863424 | bytes 4390912 | tf_op jit(solution)/shard_map/ijc,cd->ijd/dot_general | solution.py:77
  90.7 0.0 copy-done.2
  90.7 4.2 %fusion.4 = f32[16,256,128]{1,2,0:T(8,128)} fusion(f32[1,256,128]{1,2,0:T(8,128)S(1)} %collective-permute-done.1, f32[16,256,128]{1,2,0:T(8,128)S(1)} %copy-done.2, f32[3,3,128,128]{3,2,1,0:T(8,128)} %param.14), kind=kOutput, calls=%fused_computation.8 | convolution fusion | flops 805863424 | bytes 4390912 | tf_op jit(solution)/shard_map/ijc,cd->ijd/dot_general | solution.py:77
  94.9 0.0 collective-permute-done.2
  94.9 1.1 copy.39
  96.0 0.0 collective-permute-done.3
  96.0 2.1 %copy.45 = f32[18,1,128]{1,2,0:T(8,128)} copy(f32[18,1,128]{2,1,0:T(1,128)} %collective-permute-done.3) | data formatting | bytes 18432 | tf_op jit(solution)/shard_map/ppermute | solution.py:21
  98.1 3.7 %pad_maximum_fusion = (f32[18,257,128]{1,2,0:T(8,128)S(1)}, f32[18,257,128]{1,2,0:T(8,128)S(1)}) fusion(f32[18,1,128]{1,2,0:T(8,128)} %copy.45, f32[1,256,128]{1,2,0:T(8,128)S(1)} %collective-permute-done.1, f32[16,256,128]{1,2,0:T(8,128)} %copy-done.1, f32[1,256,128]{1,2,0:T(8,128)S(1)} %collective-permute-done, f32[18,1,128]{1,2,0:T(8,128)S(1)} %copy.39), kind=kLoop, calls=%fused_computation.1 | loop fusion | flops 3552768 | bytes 7114752 | tf_op jit(solution)/shard_map/concatenate | solution.py:22
  101.9 0.0 copy-done.7
  101.9 2.0 %fusion.18 = f32[16,256,128]{1,2,0:T(8,128)S(1)} fusion(f32[18,257,128]{1,2,0:T(8,128)S(1)} %get-tuple-element.6, f32[3,3,128,128]{3,2,1,0:T(8,128)S(1)} %copy-done.7), kind=kOutput, calls=%fused_computation.22 | convolution fusion | flops 805306368 | bytes 4259840 | tf_op jit(solution)/shard_map/ijc,cd->ijd/dot_general | solution.py:77
  103.9 2.0 %fusion.22 = f32[16,256,128]{1,2,0:T(8,128)S(1)} fusion(f32[18,257,128]{1,2,0:T(8,128)S(1)} %get-tuple-element.6, f32[3,3,128,128]{3,2,1,0:T(8,128)S(1)} %copy-done.7), kind=kOutput, calls=%fused_computation.26 | convolution fusion | flops 805306368 | bytes 4259840 | tf_op jit(solution)/shard_map/ijc,cd->ijd/dot_general | solution.py:77
  105.9 2.3 %fusion.20 = f32[16,256,128]{1,2,0:T(8,128)S(1)} fusion(f32[18,257,128]{1,2,0:T(8,128)S(1)} %get-tuple-element.5, f32[3,3,128,128]{3,2,1,0:T(8,128)S(1)} %copy-done.7), kind=kOutput, calls=%fused_computation.24 | convolution fusion | flops 805306368 | bytes 4259840 | tf_op jit(solution)/shard_map/ijc,cd->ijd/dot_general | solution.py:77
  108.2 0.0 copy-start.5
  108.2 2.3 %fusion.24 = f32[16,256,128]{1,2,0:T(8,128)S(1)} fusion(f32[18,257,128]{1,2,0:T(8,128)S(1)} %get-tuple-element.5, f32[3,3,128,128]{3,2,1,0:T(8,128)S(1)} %copy-done.7), kind=kOutput, calls=%fused_computation.28 | convolution fusion | flops 805306368 | bytes 4259840 | tf_op jit(solution)/shard_map/ijc,cd->ijd/dot_general | solution.py:77
  110.6 0.0 copy-start.3
  110.6 0.0 copy-start.4
  110.6 0.0 copy-start.12
  110.6 2.0 %fusion.26 = f32[16,256,128]{1,2,0:T(8,128)S(1)} fusion(f32[18,257,128]{1,2,0:T(8,128)S(1)} %get-tuple-element.6, f32[3,3,128,128]{3,2,1,0:T(8,128)S(1)} %copy-done.7), kind=kOutput, calls=%fused_computation.30 | convolution fusion | flops 805306368 | bytes 4259840 | tf_op jit(solution)/shard_map/ijc,cd->ijd/dot_general | solution.py:77
  112.6 0.0 copy-done.5
  112.6 0.0 copy-done.3
  112.6 0.2 copy-done.4
  112.8 0.0 copy-done.12
  112.8 5.0 %add_multiply_fusion = f32[16,256,128]{1,2,0:T(8,128)} fusion(f32[16,256,128]{1,2,0:T(8,128)S(1)} %copy-done.5, f32[16,256,128]{1,2,0:T(8,128)S(1)} %fusion.18, f32[16,256,128]{1,2,0:T(8,128)S(1)} %fusion.20, f32[16,256,128]{1,2,0:T(8,128)S(1)} %copy-done.3, f32[16,256,128]{1,2,0:T(8,128)S(1)} %fusion.22, f32[16,256,128]{1,2,0:T(8,128)S(1)} %fusion.24, ...), kind=kOutput, calls=%fused_computation.34 | convolution fusion | flops 810549248 | bytes 21053952 | tf_op jit(solution)/shard_map/ijc,cd->ijd/dot_general | solution.py:77
  117.8 2.9 %copy.60 = f32[16,256,128]{2,1,0:T(8,128)} copy(f32[16,256,128]{1,2,0:T(8,128)} %add_multiply_fusion) | data formatting | bytes 4194304 | tf_op jit(solution)/shard_map/mul | solution.py:80
  (7 shorter events, 0.1 us)
Async XLA Ops:
  6.5 1.6 %copy-start = (f32[16,256,128]{2,1,0:T(8,128)S(1)}, f32[16,256,128]{2,1,0:T(8,128)}, u32[]{:S(2)}) copy-start(f32[16,256,128]{2,1,0:T(8,128)} %param.8) | copy-start | bytes 6291460
  6.5 3.5 %copy-start.11 = (s32[16]{0:T(128)S(1)}, s32[16]{0:T(128)}, u32[]{:S(2)}) copy-start(s32[16]{0:T(128)} %param.10) | copy-start | bytes 196
  6.5 39.3 %reduce-scatter.2.cloned.1.call-start = ((), (), s32[]{:S(2)}) async-start(), calls=%async_computation.1 | async-start | bytes 294912 | tf_op jit(solution)/shard_map/reduce_scatter | solution.py:64
  10.0 2.1 %copy-start.8 = (f32[2,2,128,128]{3,2,1,0:T(8,128)S(1)}, f32[2,2,128,128]{3,2,1,0:T(8,128)}, u32[]{:S(2)}) copy-start(f32[2,2,128,128]{3,2,1,0:T(8,128)} %param.11) | copy-start | bytes 786436
  10.0 2.2 %copy-start.10 = (s32[16,256]{1,0:T(8,128)S(1)}, s32[16,256]{1,0:T(8,128)}, u32[]{:S(2)}) copy-start(s32[16,256]{1,0:T(8,128)} %param.9) | copy-start | bytes 49156
  10.0 2.2 %copy-start.9 = (f32[128,128]{1,0:T(8,128)S(1)}, f32[128,128]{1,0:T(8,128)}, u32[]{:S(2)}) copy-start(f32[128,128]{1,0:T(8,128)} %param.12) | copy-start | bytes 196612
  15.6 47.6 %copy-start.13 = (f32[128]{0:T(128)S(1)}, f32[128]{0:T(128)}, u32[]{:S(2)}) copy-start(f32[128]{0:T(128)} %param.13) | copy-start | bytes 1540
  45.8 17.4 %copy-start.6 = (f32[16,256,128]{1,2,0:T(8,128)S(1)}, f32[16,256,128]{1,2,0:T(8,128)}, u32[]{:S(2)}) copy-start(f32[16,256,128]{1,2,0:T(8,128)} %fusion.55) | copy-start | bytes 6291460
  66.0 11.5 %copy-start.1 = (f32[16,256,128]{1,2,0:T(8,128)}, f32[16,256,128]{1,2,0:T(8,128)S(1)}, u32[]{:S(2)}) copy-start(f32[16,256,128]{1,2,0:T(8,128)S(1)} %fusion.15) | copy-start | bytes 6291460
  66.1 9.1 %collective-permute-start = (f32[1,256,128]{1,2,0:T(8,128)S(1)}, f32[1,256,128]{1,2,0:T(8,128)S(1)}, u32[]{:S(2)}, u32[]{:S(2)}) collective-permute-start(f32[1,256,128]{1,2,0:T(8,128)S(1)} %get-tuple-element.9), channel_id=1, source_target_pairs={{0,8},{8,16},{16,24},{1,9},{9,17},{17,25},{2,10},{10,18},{18,26},{... | collective-permute-start | bytes 393224 | tf_op jit(solution)/shard_map/ppermute | solution.py:18
  69.5 8.0 %collective-permute-start.1 = (f32[1,256,128]{1,2,0:T(8,128)S(1)}, f32[1,256,128]{1,2,0:T(8,128)S(1)}, u32[]{:S(2)}, u32[]{:S(2)}) collective-permute-start(f32[1,256,128]{1,2,0:T(8,128)S(1)} %get-tuple-element.10), channel_id=1, source_target_pairs={{8,0},{16,8},{24,16},{9,1},{17,9},{25,17},{10,2},{18,10},{26,18},{... | collective-permute-start | bytes 393224 | tf_op jit(solution)/shard_map/ppermute | solution.py:21
  81.4 13.5 %collective-permute-start.2 = (f32[18,1,128]{2,1,0:T(1,128)}, f32[18,1,128]{2,1,0:T(1,128)}, u32[]{:S(2)}, u32[]{:S(2)}) collective-permute-start(f32[18,1,128]{2,1,0:T(1,128)} %copy.38), channel_id=1, source_target_pairs={{0,1},{1,2},{2,3},{3,4},{4,5},{5,6},{6,7},{7,0},{8,9},{9,10},{10,1... | collective-permute-start | bytes 27656 | tf_op jit(solution)/shard_map/ppermute | solution.py:18
  82.3 8.4 %copy-start.2 = (f32[16,256,128]{1,2,0:T(8,128)S(1)}, f32[16,256,128]{1,2,0:T(8,128)}, u32[]{:S(2)}) copy-start(f32[16,256,128]{1,2,0:T(8,128)} %copy-done.1) | copy-start | bytes 6291460
  82.3 13.7 %collective-permute-start.3 = (f32[18,1,128]{2,1,0:T(1,128)}, f32[18,1,128]{2,1,0:T(1,128)}, u32[]{:S(2)}, u32[]{:S(2)}) collective-permute-start(f32[18,1,128]{2,1,0:T(1,128)} %copy.44), channel_id=1, source_target_pairs={{1,0},{2,1},{3,2},{4,3},{5,4},{6,5},{7,6},{0,7},{9,8},{10,9},{11,1... | collective-permute-start | bytes 27656 | tf_op jit(solution)/shard_map/ppermute | solution.py:21
  98.1 3.7 %copy-start.7 = (f32[3,3,128,128]{3,2,1,0:T(8,128)S(1)}, f32[3,3,128,128]{3,2,1,0:T(8,128)}, u32[]{:S(2)}) copy-start(f32[3,3,128,128]{3,2,1,0:T(8,128)} %param.14) | copy-start | bytes 1769476
  108.2 4.4 %copy-start.5 = (f32[16,256,128]{1,2,0:T(8,128)S(1)}, f32[16,256,128]{1,2,0:T(8,128)}, u32[]{:S(2)}) copy-start(f32[16,256,128]{1,2,0:T(8,128)} %fusion.4) | copy-start | bytes 6291460
  110.6 2.1 %copy-start.3 = (f32[16,256,128]{1,2,0:T(8,128)S(1)}, f32[16,256,128]{1,2,0:T(8,128)}, u32[]{:S(2)}) copy-start(f32[16,256,128]{1,2,0:T(8,128)} %fusion.49) | copy-start | bytes 6291460
  110.6 2.2 %copy-start.4 = (f32[16,256,128]{1,2,0:T(8,128)S(1)}, f32[16,256,128]{1,2,0:T(8,128)}, u32[]{:S(2)}) copy-start(f32[16,256,128]{1,2,0:T(8,128)} %fusion) | copy-start | bytes 6291460
  110.6 2.2 %copy-start.12 = (f32[128]{0:T(128)S(1)}, f32[128]{0:T(128)}, u32[]{:S(2)}) copy-start(f32[128]{0:T(128)} %param.15) | copy-start | bytes 1540
Sparse Core Ops, SparseCore 0:
  12.3 33.4 reduce-scatter.1
where the time goes:
time: 128 us
  matrix products  41.4 us (32%)
  waiting for transfers between devices  32.6 us (25%)
  blocking collectives  14.2 us (11%)
  between operations  13.7 us (11%)
  local copies, waits for them, and re-layouts  12.5 us (10%)
  starting transfers between devices  8.41 us (7%)
  other arithmetic  4.8 us (4%)
    reduce_scatter x1, waiting for transfers between devices, per_device(): lax.psum_scatter(partial_coeffs, 'lon', scatter_dimension=0, tiled=True)  30.2 us
    dot_general x9, matrix products, per_device(): jnp.einsum('ijc,cd->ijd', window, conv_weight[row_tap, col_tap], precisio...  28.9 us
    all_gather x1, blocking collectives, per_device(): mixed = lax.all_gather(own_mixed, 'lon', axis=0, tiled=True)  14.2 us
    ppermute x2, starting transfers between devices, with_halo(): lax.ppermute(lax.slice_in_dim(block, 0, width, axis=dim), axis, backward)  5.01 us
    concatenate x2, other arithmetic, with_halo(): block = jnp.concatenate([low, block, high], axis=dim)  3.95 us
    ppermute x2, starting transfers between devices, with_halo(): lax.ppermute(lax.slice_in_dim(block, block.shape[dim] - width, None, axis...  3.4 us
    dot_general x1, matrix products, per_device(): local = jnp.einsum('ijc,cd->ijd', field, local_weight, precision=HIGH)  3.35 us
    mul x1, local copies, waits for them, and re-layouts, per_device(): return wet * (conv + conv_bias)  2.88 us
  transfers between devices with their start and end apart: 5, of which 2 were waited for; matrix products, arithmetic and copies ran while one was open for 15% of the time, Pallas kernels for 0%

commit v1 on v0

v1 whole, which is shorter than its diff:
```python
import functools
import math

import jax
import jax.numpy as jnp
from jax import lax
from jax.experimental import pallas as pl
from jax.experimental.pallas import tpu as pltpu
from jax.sharding import PartitionSpec as P

LANES = 128
TAIL = 16
MIB = 1 << 20
F32 = jnp.float32
BF16 = jnp.bfloat16


def flip_of(distance, chips):
    return 1 if distance in (1, chips - 1) else 0


def chip_moves(distance, chips, flip):
    return [
        (2 * chip + core, 2 * ((chip + distance) % chips) + (core ^ flip))
        for chip in range(chips)
        for core in range(2)
    ]


def pair_moves(chips):
    return [(device, device ^ 1) for device in range(2 * chips)]


def distances(chips):
    return [1, chips - 1] + list(range(2, chips - 1))


def split(x):
    high = x.astype(BF16)
    return high, (x - high.astype(F32)).astype(BF16)


def dot(a, b):
    return lax.dot_general(a, b, (((1,), (0,)), ((), ())), preferred_element_type=F32)


def fill(blocks, depth):
    missing = depth - sum(block.shape[0] for block in blocks)
    if missing:
        blocks = blocks + [jnp.zeros((missing,) + blocks[0].shape[1:], blocks[0].dtype)]
    return jnp.concatenate(blocks, 0)


def angles(mode_list, lon, total_lon):
    row = lax.broadcasted_iota(jnp.int32, lon.shape, 0)
    ids = jnp.zeros(lon.shape, jnp.int32)
    for index, mode in enumerate(mode_list):
        ids = jnp.where(row == index, mode, ids)
    product = ids * lon
    if total_lon & (total_lon - 1):
        product = lax.rem(product, total_lon)
    else:
        product = product & (total_lon - 1)
    return product.astype(F32) * (2.0 * math.pi / total_lon)


def forward_kernel(
    chips, per, total_lon, where_ref, modes_hbm, field_hbm, ocean_hbm, give_ref, keep_ref, away_ref,
    modes_ref, field_ref, ocean_ref, small_sem, field_sem,
):
    rows, width, channels = field_ref.shape
    chunks = field_sem.shape[0]
    step = rows // chunks
    first_copy = pltpu.make_async_copy(modes_hbm, modes_ref, small_sem.at[0])
    first_copy.start()
    copies = []
    for k in range(chunks):
        part = pl.ds(k * step, step)
        copies.append(pltpu.make_async_copy(field_hbm.at[part], field_ref.at[part], field_sem.at[k]))
        copies[-1].start()
    ocean_copy = pltpu.make_async_copy(ocean_hbm, ocean_ref, small_sem.at[1])
    ocean_copy.start()
    here = where_ref[0]
    chip, core = here // 2, lax.rem(here, 2)
    first_copy.wait()
    mode_list = []
    for flipped in range(2):
        for d in range(chips):
            owner = 2 * lax.rem(chip + d, chips)
            owner = owner + lax.rem(core + flipped + flip_of(d, chips), 2)
            mode_list += [modes_ref[owner * per + t] for t in range(per)]
    count = len(mode_list)
    half = count // 2
    lon = here * width + lax.broadcasted_iota(jnp.int32, (count, width), 1)
    theta = angles(mode_list, lon, total_lon)
    scale = 1.0 / math.sqrt(total_lon)
    table = jnp.concatenate([jnp.cos(theta) * scale, -jnp.sin(theta) * scale], 0)
    lhs = jnp.concatenate(split(table), 0)
    for i in range(rows):
        if i % step == 0:
            copies[i // step].wait()
        rhs = jnp.concatenate(split(field_ref[i]), 1)
        product = dot(lhs, rhs)
        total = product[: 2 * count] + product[2 * count :]
        total = total[:, :channels] + total[:, channels:]
        keep_ref[:half, i, :channels] = total[:half]
        give_ref[:half, i, :channels] = total[half:count]
        keep_ref[:half, i, channels:] = total[count : count + half]
        give_ref[:half, i, channels:] = total[count + half :]
    ocean_copy.wait()
    last = field_ref[:, width - 1, :]
    first = field_ref[:, 0, :]
    land = ocean_ref[...].astype(F32)
    last_wet = jnp.broadcast_to(land[:, width - 1 : width], (rows, channels))
    first_wet = jnp.broadcast_to(land[:, :1], (rows, channels))
    near_is_last = core == 0
    give_ref[half, :, :channels] = jnp.where(near_is_last, last, first)
    give_ref[half, :, channels:] = jnp.where(near_is_last, last_wet, first_wet)
    away_ref[0, :, :channels] = jnp.where(near_is_last, first, last)
    away_ref[0, :, channels:] = jnp.where(near_is_last, first_wet, last_wet)


def prepare_kernel(
    chips, per, total_lon, width, where_ref, modes_ref, local_ref, conv_ref, spectral_ref,
    trig_ref, local_out, w1_ref, w2_ref, w3_ref, mix_ref,
):
    channels = local_ref.shape[0]
    wide = 2 * channels
    for t in range(per):
        real, imag = spectral_ref[t, 0], spectral_ref[t, 1]
        top = jnp.concatenate(split(jnp.concatenate([real, imag], 1)), 1)
        low = jnp.concatenate(split(jnp.concatenate([-imag, real], 1)), 1)
        mix_ref[t * wide : t * wide + channels, :] = top
        mix_ref[t * wide + channels : (t + 1) * wide, :] = low
    here = where_ref[0]
    chip, core = here // 2, lax.rem(here, 2)
    mode_list = []
    for flipped in range(2):
        for d in [0] + distances(chips):
            source = 2 * lax.rem(chip - d + chips, chips) + lax.rem(core + flipped, 2)
            mode_list += [modes_ref[source * per + t] for t in range(per)]
    count = len(mode_list)
    block = width + TAIL
    padded = -(-block // LANES) * LANES
    place = lax.broadcasted_iota(jnp.int32, (count, padded), 1)
    place = jnp.where(place == block - 1, -1, place)
    lon = here * width + place + total_lon
    lon = jnp.where(lon >= total_lon, lon - total_lon, lon)
    lon = jnp.where(lon >= total_lon, lon - total_lon, lon)
    theta = angles(mode_list, lon, total_lon)
    scale = 2.0 / math.sqrt(count)
    table = jnp.concatenate([jnp.cos(theta) * scale, -jnp.sin(theta) * scale], 0)
    high, low = split(table)
    high, low = high.astype(F32), low.astype(F32)
    depth = trig_ref.shape[1]
    stacked = fill([high, low, high], depth)
    trig_ref[...] = stacked.T[:block].astype(BF16)
    local_out[...] = jnp.concatenate(split(local_ref[...]), 1)
    for col in range(3):
        left = slice(col * channels, (col + 1) * channels)
        right = slice((3 + col) * channels, (4 + col) * channels)
        for row in range(2):
            at = slice(row * channels, (row + 1) * channels)
            top, bottom = split(conv_ref[row, col])
            w1_ref[at, left] = top
            w1_ref[at, right] = bottom
            w3_ref[at, left] = top
        top, bottom = split(conv_ref[2, col])
        w2_ref[:channels, left] = top
        w2_ref[:channels, right] = bottom
        w2_ref[channels:, left] = top
        w2_ref[channels:, right] = jnp.zeros_like(top)


def gelu(x):
    inner = math.sqrt(2.0 / math.pi) * (x + 0.044715 * (x * x * x))
    return x * (0.5 * (1.0 + jnp.tanh(inner)))


def mix_kernel(per, rows, *refs):
    summed_ref, *part_refs, mix_ref, out_ref = refs
    wide = summed_ref.shape[1]
    for t in range(per):
        at = slice(t * rows, (t + 1) * rows)
        total = summed_ref[at, :]
        for part in part_refs:
            total = total + part[at, :]
        high, low = split(total)
        weights = mix_ref[t * wide : (t + 1) * wide, :]
        y = dot(high, weights)
        out_ref[at, :] = y[:, :wide] + y[:, wide:] + dot(low, weights[:, :wide])


def hidden_kernel(
    per, where_ref, field_ref, got_ref, west_ref, east_ref, ocean_ref, mixed_ref, trig_ref, local_ref, bias_ref,
    high_ref, low_ref, edge_ref,
):
    rows, width, channels = field_ref.shape
    block = width + TAIL
    depth = trig_ref.shape[1]
    wet = ocean_ref[...].astype(F32).T
    empty = jnp.zeros((depth, channels), BF16)
    trig = trig_ref[...]
    local = local_ref[...]
    south = lax.rem(where_ref[0], 2) == 0
    even = lax.rem(where_ref[1], 2)
    near = got_ref[got_ref.shape[0] - rows :, :]
    left = jnp.where(south, west_ref[per * rows :, :], near)
    right = jnp.where(south, near, east_ref[per * rows :, :])
    place = lax.broadcasted_iota(jnp.int32, (TAIL, 2 * channels), 0)
    for i in range(rows):
        tail = jnp.where(place == TAIL - 1, left[i : i + 1], jnp.where(place == 0, right[i : i + 1], 0.0))
        x = jnp.concatenate([field_ref[i], tail[:, :channels]], 0)
        x_high, x_low = split(x)
        mixed = jnp.concatenate([mixed_ref[:, i, :channels], mixed_ref[:, i, channels:]], 0)
        m_high, m_low = split(mixed)
        lower = fill([m_high, m_high, m_low], depth)
        rhs = jnp.concatenate([local, jnp.concatenate([lower, empty], 1)], 0)
        lhs = jnp.concatenate([x_high, trig], 1)
        y = dot(lhs, rhs)
        y = y[:, :channels] + y[:, channels:] + dot(x_low, local[:, :channels])
        y = gelu(y + bias_ref[...])
        mask = jnp.concatenate(
            [jnp.broadcast_to(wet[:, i : i + 1], (width, channels)), tail[:, channels:]], 0
        )
        y = y * mask
        h_high, h_low = split(y)
        high_ref[i * block : (i + 1) * block, :] = h_high
        low_ref[i * block : (i + 1) * block, :] = h_low
        if i == 0:
            edge_ref[1 - even] = y
        if i == rows - 1:
            edge_ref[even] = y


def conv_rows(a1, a2, a3, w1, w2, w3, channels, block, count):
    n = 3 * channels
    y = dot(a1, w1) + dot(a2, w2)
    z = y[:, :n] + y[:, n:] + dot(a3, w3)
    out = []
    for r in range(count):
        t = z[r * block : (r + 1) * block]
        west = pltpu.roll(t[:, :channels], 1, 0)
        east = pltpu.roll(t[:, 2 * channels :], block - 1, 0)
        out.append((west + t[:, channels : 2 * channels] + east)[: block - TAIL])
    return out


def inner_kernel(high_ref, low_ref, ocean_ref, bias_ref, w1_ref, w2_ref, w3_ref, out_ref, buf_ref, wet_ref, sem_ref):
    rows, width = ocean_ref.shape
    channels = high_ref.shape[1]
    block = width + TAIL
    wet = ocean_ref[...].astype(F32).T
    for g in range((rows - 2) // 2):
        i = 1 + 2 * g

        def at(ref, first):
            return ref[first * block : (first + 2) * block, :]

        a1 = jnp.concatenate([at(high_ref, i - 1), at(high_ref, i)], 1)
        a2 = jnp.concatenate([at(high_ref, i + 1), at(low_ref, i + 1)], 1)
        a3 = jnp.concatenate([at(low_ref, i - 1), at(low_ref, i)], 1)
        res = conv_rows(a1, a2, a3, w1_ref[...], w2_ref[...], w3_ref[...], channels, block, 2)
        for r in range(2):
            buf_ref[2 * g + r] = (res[r] + bias_ref[...]) * wet[:, i + r : i + r + 1]
        pltpu.make_async_copy(buf_ref.at[pl.ds(2 * g, 2)], out_ref.at[pl.ds(i, 2)], sem_ref.at[g]).start()
    for g in range((rows - 2) // 2):
        pltpu.make_async_copy(buf_ref.at[pl.ds(2 * g, 2)], out_ref.at[pl.ds(1 + 2 * g, 2)], sem_ref.at[g]).wait()


def outer_kernel(
    where_ref, high_ref, low_ref, first_ref, second_ref, ocean_ref, bias_ref, w1_ref, w2_ref, w3_ref, in_ref, out_ref, buf_ref, sem_ref
):
    rows, width = ocean_ref.shape
    channels = high_ref.shape[1]
    block = width + TAIL
    wet = ocean_ref[...].astype(F32).T

    def at(ref, row):
        return ref[row * block : (row + 1) * block, :]

    even = lax.rem(where_ref[1], 2) == 0
    up_high, up_low = split(jnp.where(even, second_ref[0], first_ref[0]))
    down_high, down_low = split(jnp.where(even, first_ref[0], second_ref[0]))
    top = [(up_high, up_low)] + [(at(high_ref, r), at(low_ref, r)) for r in (0, 1)]
    bottom = [(at(high_ref, r), at(low_ref, r)) for r in (rows - 2, rows - 1)] + [(down_high, down_low)]

    def stack(k, part):
        return jnp.concatenate([top[k][part], bottom[k][part]], 0)

    a1 = jnp.concatenate([stack(0, 0), stack(1, 0)], 1)
    a2 = jnp.concatenate([stack(2, 0), stack(2, 1)], 1)
    a3 = jnp.concatenate([stack(0, 1), stack(1, 1)], 1)
    res = conv_rows(a1, a2, a3, w1_ref[...], w2_ref[...], w3_ref[...], channels, block, 2)
    copies = []
    for r, row in enumerate((0, rows - 1)):
        buf_ref[r] = (res[r] + bias_ref[...]) * wet[:, row : row + 1]
        copy = pltpu.make_async_copy(buf_ref.at[pl.ds(r, 1)], out_ref.at[pl.ds(row, 1)], sem_ref.at[r])
        copy.start()
        copies.append(copy)
    for copy in copies:
        copy.wait()


def vmem():
    return pl.BlockSpec(memory_space=pltpu.VMEM)


def smem():
    return pl.BlockSpec(memory_space=pltpu.SMEM)


def struct(shape, dtype=F32):
    return jax.ShapeDtypeStruct(shape, dtype)


def params(mib):
    return pltpu.CompilerParams(vmem_limit_bytes=mib * MIB)


def per_device(
    field, ocean, modes, spectral_weight, local_weight, layer_bias, conv_weight, conv_bias
):
    rows, width, channels = field.shape
    devices = lax.axis_size("lon")
    chips = devices // 2
    bands = lax.axis_size("lat")
    where = jnp.stack([lax.axis_index("lon"), lax.axis_index("lat")]).astype(jnp.int32)
    total_lon = width * devices
    total_modes = modes.shape[0]
    per = total_modes // devices
    half = chips * per
    block = width + TAIL
    steps = distances(chips)
    wide = 2 * channels
    chunks = 4

    give, keep, away = pl.pallas_call(
        functools.partial(forward_kernel, chips, per, total_lon),
        out_shape=(
            struct((half + 1, rows, wide)),
            struct((half, rows, wide)),
            struct((1, rows, wide)),
        ),
        in_specs=[smem()] + [pl.BlockSpec(memory_space=pltpu.MemorySpace.HBM)] * 3,
        out_specs=(vmem(), vmem(), vmem()),
        scratch_shapes=[
            pltpu.SMEM((total_modes,), jnp.int32),
            pltpu.VMEM((rows, width, channels), F32),
            pltpu.VMEM((rows, width), jnp.int32),
            pltpu.SemaphoreType.DMA((2,)),
            pltpu.SemaphoreType.DMA((chunks,)),
        ],
        compiler_params=params(16),
        name="forward",
    )(where, *[pltpu.with_memory_space_constraint(x, pltpu.MemorySpace.HBM) for x in (modes, field, ocean)])
    give = give.reshape((half + 1) * rows, wide)
    keep = keep.reshape(half * rows, wide)
    away = away.reshape(rows, wide)

    depth = -(-6 * total_modes // LANES) * LANES
    trig, local, w1, w2, w3, mix = pl.pallas_call(
        functools.partial(prepare_kernel, chips, per, total_lon, width),
        out_shape=(
            struct((block, depth), BF16),
            struct((channels, 2 * channels), BF16),
            struct((2 * channels, 6 * channels), BF16),
            struct((2 * channels, 6 * channels), BF16),
            struct((2 * channels, 3 * channels), BF16),
            struct((per * wide, 2 * wide), BF16),
        ),
        in_specs=[smem(), smem(), vmem(), vmem(), vmem()],
        out_specs=(vmem(),) * 6,
        compiler_params=params(16),
        name="prepare",
    )(where, modes, local_weight, conv_weight, spectral_weight)

    got = lax.ppermute(give, "lon", pair_moves(chips))
    summed = keep + got[: half * rows]
    size = per * rows
    parts = {}
    for d in steps:
        send = summed[d * size : (d + 1) * size]
        flip = flip_of(d, chips)
        if flip:
            send = jnp.concatenate([send, away])
        parts[d] = lax.ppermute(send, "lon", chip_moves(d, chips, flip))

    own_mixed = pl.pallas_call(
        functools.partial(mix_kernel, per, rows),
        out_shape=struct((size, wide)),
        in_specs=[vmem()] * (len(steps) + 2),
        out_specs=vmem(),
        compiler_params=params(8),
        name="mix",
    )(summed, *[parts[d] for d in steps], mix)
    gathered = [own_mixed]
    for d in steps:
        gathered.append(lax.ppermute(own_mixed, "lon", chip_moves(d, chips, 0)))
    gathered = jnp.concatenate(gathered)
    other = lax.ppermute(gathered, "lon", pair_moves(chips))
    mixed = jnp.concatenate([gathered, other]).reshape(total_modes, rows, wide)

    high, low, edge = pl.pallas_call(
        functools.partial(hidden_kernel, per),
        out_shape=(
            struct((rows * block, channels), BF16),
            struct((rows * block, channels), BF16),
            struct((2, block, channels)),
        ),
        in_specs=[smem()] + [vmem()] * 9,
        out_specs=(vmem(),) * 3,
        compiler_params=params(24),
        name="hidden",
    )(where, field, got, parts[1], parts[chips - 1], ocean, mixed, trig, local, layer_bias.reshape(1, channels))

    evens = [(i, i + 1) for i in range(0, bands - 1, 2)]
    odds = [(i, i + 1) for i in range(1, bands - 1, 2)]
    first = lax.ppermute(edge[:1], "lat", evens + [(b, a) for a, b in evens])
    second = lax.ppermute(edge[1:], "lat", odds + [(b, a) for a, b in odds])
    bias = conv_bias.reshape(1, channels)
    flops = 2 * 9 * 3 * rows * width * channels * channels
    inner = pl.pallas_call(
        inner_kernel,
        out_shape=struct((rows, width, channels)),
        in_specs=[vmem()] * 7,
        out_specs=pl.BlockSpec(memory_space=pl.ANY),
        scratch_shapes=[
            pltpu.VMEM((rows - 2, width, channels), F32),
            pltpu.VMEM((rows, width), F32),
            pltpu.SemaphoreType.DMA(((rows - 2) // 2,)),
        ],
        compiler_params=params(32),
        cost_estimate=pl.CostEstimate(flops=flops, transcendentals=0, bytes_accessed=4 * field.size),
        name="inner",
    )(high, low, ocean, bias, w1, w2, w3)
    return pl.pallas_call(
        outer_kernel,
        out_shape=struct((rows, width, channels)),
        in_specs=[smem()] + [vmem()] * 9 + [pl.BlockSpec(memory_space=pl.ANY)],
        out_specs=pl.BlockSpec(memory_space=pl.ANY),
        scratch_shapes=[
            pltpu.VMEM((2, width, channels), F32),
            pltpu.SemaphoreType.DMA((2,)),
        ],
        input_output_aliases={10: 0},
        compiler_params=params(32),
        name="outer",
    )(where, high, low, first, second, ocean, bias, w1, w2, w3, inner)


def solution(mesh):
    in_specs = (
        P("lat", "lon", None),
        P("lat", "lon"),
        P(),
        P("lon", None, None, None),
        P(),
        P(),
        P(),
        P(),
    )
    out_specs = P("lat", "lon", None)
    return jax.shard_map(
        per_device, mesh=mesh, in_specs=in_specs, out_specs=out_specs, check_vma=False
    )
```

time: 128 us -> 42.2 us (0.33)
  matrix products: 41.4 us -> 0 us
  waiting for transfers between devices: 32.6 us -> 12.8 us
  blocking collectives: 14.2 us -> 0 us
  between operations: 13.7 us -> 0.18 us
  Pallas kernels: 0 us -> 13.4 us
  local copies, waits for them, and re-layouts: 12.5 us -> 0.1 us
  starting transfers between devices: 8.41 us -> 15.5 us
  other arithmetic: 4.8 us -> 0.11 us
    dot_general x15 -> x0, matrix products: 41.4 us -> none  [the longest x9 28.9 us: per_device(): jnp.einsum('ijc,cd->ijd', window, conv_weight[row_tap, col_tap], precisio...]
    reduce_scatter x1 -> x0, waiting for transfers between devices: 30.2 us -> none  [per_device(): lax.psum_scatter(partial_coeffs, 'lon', scatter_dimension=0, tiled=True)]
    all_gather x1 -> x0, blocking collectives: 14.2 us -> none  [per_device(): mixed = lax.all_gather(own_mixed, 'lon', axis=0, tiled=True)]
    pallas_call x0 -> x6, Pallas kernels: none -> 13.4 us  [the longest x1 5.18 us: per_device(): pl.pallas_call(inner_kernel, out_shape=struct((rows, width, channels)), i...]
    ppermute x4 -> x10, waiting for transfers between devices: 2.35 us -> 12.8 us  [the longest x3 5.7 us: per_device(): gathered.append(lax.ppermute(own_mixed, 'lon', chip_moves(d, chips, 0)))]
    ppermute x4 -> x10, starting transfers between devices: 8.41 us -> 15.5 us  [the longest x3 5.73 us: per_device(): parts[d] = lax.ppermute(send, 'lon', chip_moves(d, chips, flip))]
    concatenate x3 -> x2, other arithmetic: 4.68 us -> 0.02 us  [the longest x1 0.01 us: per_device(): gathered = jnp.concatenate(gathered)]
    slice x5 -> x2, local copies, waits for them, and re-layouts: 4.65 us -> 0.03 us  [the longest x1 0.02 us: per_device(): second = lax.ppermute(edge[1:], 'lat', odds + [(b, a) for a, b in odds])]
  transfers between devices with their start and end apart: 5 -> 10, of which waited for: 2 -> 8; matrix products, arithmetic and copies ran while one was open for 15% -> 0% of each run, Pallas kernels for 0% -> 14%
where the time goes in v1:
time: 42.2 us; the launch traced here: 42.1 us
  starting transfers between devices  15.5 us (37%)
  Pallas kernels  13.4 us (32%)
  waiting for transfers between devices  12.8 us (30%)
    ppermute x3, starting transfers between devices, per_device(): parts[d] = lax.ppermute(send, 'lon', chip_moves(d, chips, flip))  5.73 us
    ppermute x3, waiting for transfers between devices, per_device(): gathered.append(lax.ppermute(own_mixed, 'lon', chip_moves(d, chips, 0)))  5.7 us
    pallas_call x1, Pallas kernels, per_device(): pl.pallas_call(inner_kernel, out_shape=struct((rows, width, channels)), i...  5.18 us
    ppermute x1, starting transfers between devices, per_device(): first = lax.ppermute(edge[:1], 'lat', evens + [(b, a) for a, b in evens])  4.29 us
    ppermute x3, starting transfers between devices, per_device(): gathered.append(lax.ppermute(own_mixed, 'lon', chip_moves(d, chips, 0)))  4.17 us
    ppermute x3, waiting for transfers between devices, per_device(): parts[d] = lax.ppermute(send, 'lon', chip_moves(d, chips, flip))  3.43 us
    pallas_call x1, Pallas kernels, per_device(): pl.pallas_call(functools.partial(forward_kernel, chips, per, total_lon),...  2.63 us
    pallas_call x1, Pallas kernels, per_device(): pl.pallas_call(functools.partial(hidden_kernel, per), out_shape=(struct((...  2.37 us
  transfers between devices with their start and end apart: 10, of which 8 were waited for; matrix products, arithmetic and copies ran while one was open for 0% of the time, Pallas kernels for 14%

profile of v1, /device:TPU:0, one launch (start us, length us, event | category | flops | bytes accessed | tf_op | source)
XLA Modules:
  0.0 42.1 jit_solution(16503183074519430832)
XLA Ops:
  0.0 0.0 copy-start.5
  0.0 0.0 copy-start.1
  0.0 0.0 copy-start.4
  0.0 0.0 copy-start.2
  0.0 0.1 pad_add_fusion.where_ref
  0.1 2.6 %forward.1 = (f32[9,16,256]{2,1,0:T(8,128)S(1)}, f32[8,16,256]{2,1,0:T(8,128)S(1)}, f32[1,16,256]{2,1,0:T(8,128)S(1)}) custom-call(s32[2]{0:T(128)S(1)} %pad_add_fusion.where_ref, s32[16]{0:T(128)} %modes_ref.1, f32[16,256,128]{2,1,0:T(8,128)} %field_ref.1, s32[16,256]{1,0:T(8,128)} %ocean_ref.5), custom_call_target="tpu_custom_call" | custom-call | tf_op jit(solution)/shard_map/forward/pallas_call | solution.py:338
  2.7 0.0 copy-start
  2.7 0.0 copy-start.3
  2.7 0.0 copy-start.6
  2.8 0.6 %collective-permute-start = (f32[144,256]{1,0:T(8,128)S(1)}, f32[144,256]{1,0:T(8,128)S(1)}, u32[]{:S(2)}, u32[]{:S(2)}) collective-permute-start(f32[144,256]{1,0:T(8,128)S(1)} %bitcast.14), channel_id=1, source_target_pairs={{0,1},{1,0},{2,3},{3,2},{4,5},{5,4},{6,7},{7,6},{8,9},{9,8},{10,11... | collective-permute-start | bytes 442376 | tf_op jit(solution)/shard_map/ppermute | solution.py:378
  3.3 1.0 %collective-permute-done.got_ref = f32[144,256]{1,0:T(8,128)S(1)} collective-permute-done((f32[144,256]{1,0:T(8,128)S(1)}, f32[144,256]{1,0:T(8,128)S(1)}, u32[]{:S(2)}, u32[]{:S(2)}) %collective-permute-start) | collective-permute-done | bytes 147488 | tf_op jit(solution)/shard_map/ppermute | solution.py:378
  4.4 4.8 %collective-permute-start.2 = (f32[48,256]{1,0:T(8,128)S(1)}, f32[48,256]{1,0:T(8,128)S(1)}, u32[]{:S(2)}, u32[]{:S(2)}) collective-permute-start(f32[48,256]{1,0:T(8,128)S(1)} %get-tuple-element.34), channel_id=1, source_target_pairs={{0,7},{1,6},{2,1},{3,0},{4,3},{5,2},{6,5},{7,4},{8,15},{9,14},{10,... | collective-permute-start | bytes 147464 | tf_op jit(solution)/shard_map/ppermute | solution.py:387
  9.1 0.0 collective-permute-start.1
  9.1 1.0 %collective-permute-start.3 = (f32[32,256]{1,0:T(8,128)S(1)}, f32[32,256]{1,0:T(8,128)S(1)}, u32[]{:S(2)}, u32[]{:S(2)}) collective-permute-start(f32[32,256]{1,0:T(8,128)S(1)} %get-tuple-element.31), channel_id=1, source_target_pairs={{0,4},{1,5},{2,6},{3,7},{4,0},{5,1},{6,2},{7,3},{8,12},{9,13},{10,... | collective-permute-start | bytes 98312 | tf_op jit(solution)/shard_map/ppermute | solution.py:387
  10.1 0.0 copy-done.5
  10.1 0.0 copy-done.1
  10.1 0.0 copy-done.4
  10.1 0.0 copy-done.2
  10.1 0.9 %prepare.1 = (bf16[272,128]{1,0:T(8,128)(2,1)S(1)}, bf16[128,256]{1,0:T(8,128)(2,1)S(1)}, bf16[256,768]{1,0:T(8,128)(2,1)S(1)}, bf16[256,768]{1,0:T(8,128)(2,1)S...) custom-call(s32[2]{0:T(128)S(1)} %pad_add_fusion.where_ref, s32[16]{0:T(128)S(1)} %copy-done.5, ...), custom_call_target="tpu_custom_call" | custom-call | tf_op jit(solution)/shard_map/prepare/pallas_call | solution.py:362
  11.1 2.9 %collective-permute-done.3.refs_3_ = f32[32,256]{1,0:T(8,128)S(1)} collective-permute-done((f32[32,256]{1,0:T(8,128)S(1)}, f32[32,256]{1,0:T(8,128)S(1)}, u32[]{:S(2)}, u32[]{:S(2)}) %collective-permute-start.3) | collective-permute-done | bytes 32800 | tf_op jit(solution)/shard_map/ppermute | solution.py:387
  14.0 0.0 collective-permute-done.2.refs_2_.east_ref
  14.0 0.5 %collective-permute-done.1.refs_1_.west_ref = f32[48,256]{1,0:T(8,128)S(1)} collective-permute-done((f32[48,256]{1,0:T(8,128)S(1)}, f32[48,256]{1,0:T(8,128)S(1)}, u32[]{:S(2)}, u32[]{:S(2)}) %collective-permute-start.1) | collective-permute-done | bytes 49184 | tf_op jit(solution)/shard_map/ppermute | solution.py:387
  14.5 0.2 mix.1
  14.7 0.0 copy-start.7
  14.7 1.7 %collective-permute-start.6 = (f32[32,256]{1,0:T(8,128)S(1)}, f32[32,256]{1,0:T(8,128)S(1)}, u32[]{:S(2)}, u32[]{:S(2)}) collective-permute-start(f32[32,256]{1,0:T(8,128)S(1)} %mix.1), channel_id=1, source_target_pairs={{0,4},{1,5},{2,6},{3,7},{4,0},{5,1},{6,2},{7,3},{8,12},{9,13},{10,... | collective-permute-start | bytes 98312 | tf_op jit(solution)/shard_map/ppermute | solution.py:399
  16.4 2.4 %collective-permute-start.5 = (f32[32,256]{1,0:T(8,128)S(1)}, f32[32,256]{1,0:T(8,128)S(1)}, u32[]{:S(2)}, u32[]{:S(2)}) collective-permute-start(f32[32,256]{1,0:T(8,128)S(1)} %mix.1), channel_id=1, source_target_pairs={{0,6},{1,7},{2,0},{3,1},{4,2},{5,3},{6,4},{7,5},{8,14},{9,15},{10,... | collective-permute-start | bytes 98312 | tf_op jit(solution)/shard_map/ppermute | solution.py:399
  18.9 0.0 collective-permute-start.4
  18.9 1.0 %collective-permute-done.6 = f32[32,256]{1,0:T(8,128)S(1)} collective-permute-done((f32[32,256]{1,0:T(8,128)S(1)}, f32[32,256]{1,0:T(8,128)S(1)}, u32[]{:S(2)}, u32[]{:S(2)}) %collective-permute-start.6) | collective-permute-done | bytes 32800 | tf_op jit(solution)/shard_map/ppermute | solution.py:399
  19.8 0.6 %collective-permute-done.5 = f32[32,256]{1,0:T(8,128)S(1)} collective-permute-done((f32[32,256]{1,0:T(8,128)S(1)}, f32[32,256]{1,0:T(8,128)S(1)}, u32[]{:S(2)}, u32[]{:S(2)}) %collective-permute-start.5) | collective-permute-done | bytes 32800 | tf_op jit(solution)/shard_map/ppermute | solution.py:399
  20.5 4.1 %collective-permute-done.4 = f32[32,256]{1,0:T(8,128)S(1)} collective-permute-done((f32[32,256]{1,0:T(8,128)S(1)}, f32[32,256]{1,0:T(8,128)S(1)}, u32[]{:S(2)}, u32[]{:S(2)}) %collective-permute-start.4) | collective-permute-done | bytes 32800 | tf_op jit(solution)/shard_map/ppermute | solution.py:399
  24.6 0.1 collective-permute-start.7
  24.7 1.3 %collective-permute-done.7 = f32[128,256]{1,0:T(8,128)S(1)} collective-permute-done((f32[128,256]{1,0:T(8,128)S(1)}, f32[128,256]{1,0:T(8,128)S(1)}, u32[]{:S(2)}, u32[]{:S(2)}) %collective-permute-start.7) | collective-permute-done | bytes 131104 | tf_op jit(solution)/shard_map/ppermute | solution.py:401
  26.0 0.0 copy-done
  26.0 0.0 copy-done.3
  26.1 0.0 copy-done.6
  26.1 2.4 %hidden.1 = (bf16[4352,128]{1,0:T(8,128)(2,1)S(1)}, bf16[4352,128]{1,0:T(8,128)(2,1)S(1)}, f32[2,272,128]{2,1,0:T(8,128)S(1)}) custom-call(s32[2]{0:T(128)S(1)} %pad_add_fusion.where_ref, f32[16,256,128]{2,1,0:T(8,128)S(1)} %copy-done, f32[144,256]{1,0:T(8,128)S(1)} %collective-permute-done.got_ref, f32[48,256]{1,0:T(8,128)S(1)} %collective-permute-done.1.refs_1_.west_ref, ...), custom_call_target="tpu_custom_call" | custom-call | tf_op jit(solution)/shard_map/hidden/pallas_call | solution.py:404
  28.5 0.7 %collective-permute-start.9 = (f32[1,272,128]{2,1,0:T(8,128)S(1)}, f32[1,272,128]{2,1,0:T(8,128)S(1)}, u32[]{:S(2)}, u32[]{:S(2)}) collective-permute-start(f32[1,272,128]{2,1,0:T(8,128)S(1)} %get-tuple-element.29), channel_id=1, source_target_pairs={{8,16},{16,8},{9,17},{17,9},{10,18},{18,10},{11,19},{19,11},{12,20... | collective-permute-start | bytes 417800 | tf_op jit(solution)/shard_map/ppermute | solution.py:420
  29.1 4.3 %collective-permute-start.8 = (f32[1,272,128]{2,1,0:T(8,128)S(1)}, f32[1,272,128]{2,1,0:T(8,128)S(1)}, u32[]{:S(2)}, u32[]{:S(2)}) collective-permute-start(f32[1,272,128]{2,1,0:T(8,128)S(1)} %get-tuple-element.30), channel_id=1, source_target_pairs={{0,8},{16,24},{8,0},{24,16},{1,9},{17,25},{9,1},{25,17},{2,10},{18... | collective-permute-start | bytes 417800 | tf_op jit(solution)/shard_map/ppermute | solution.py:419
  33.4 0.0 copy-done.7
  33.4 5.2 %inner.1.in_ref = f32[16,256,128]{2,1,0:T(8,128)} custom-call(bf16[4352,128]{1,0:T(8,128)(2,1)S(1)} %get-tuple-element.23.high_ref, bf16[4352,128]{1,0:T(8,128)(2,1)S(1)} %get-tuple-element.24.low_ref, s32[16,256]{1,0:T(8,128)S(1)} %copy-done.3, f32[1,128]{1,0:T(1,128)S(1)} %bitcast.12, bf16[256,768]{1,0:T(8,128)(2,1)S(1)} %get-tuple-element.26.w1_ref, ...), custom_call_target="tpu_custom_call" | custom-call | flops 3623878656 | bytes 2097152 | tf_op jit(solution)/shard_map/inner/pallas_call | solution.py:423
  38.6 0.0 collective-permute-done.9.second_ref
  38.6 1.4 %collective-permute-done.8.first_ref = f32[1,272,128]{2,1,0:T(8,128)S(1)} collective-permute-done((f32[1,272,128]{2,1,0:T(8,128)S(1)}, f32[1,272,128]{2,1,0:T(8,128)S(1)}, u32[]{:S(2)}, u32[]{:S(2)}) %collective-permute-start.8) | collective-permute-done | bytes 139296 | tf_op jit(solution)/shard_map/ppermute | solution.py:419
  40.0 2.1 %outer.1 = f32[16,256,128]{2,1,0:T(8,128)} custom-call(s32[2]{0:T(128)S(1)} %pad_add_fusion.where_ref, bf16[4352,128]{1,0:T(8,128)(2,1)S(1)} %get-tuple-element.23.high_ref, bf16[4352,128]{1,0:T(8,128)(2,1)S(1)} %get-tuple-element.24.low_ref, f32[1,272,128]{2,1,0:T(8,128)S(1)} %collective-permute-done.8.first_ref, ...), custom_call_target="tpu_custom_call", output_to_operand_aliasing={{}: (10, {})} | custom-call | tf_op jit(solution)/shard_map/outer/pallas_call | solution.py:437
  (10 shorter events, 0.1 us)
Async XLA Ops:
  0.0 10.1 %copy-start.5 = (s32[16]{0:T(128)S(1)}, s32[16]{0:T(128)}, u32[]{:S(2)}) copy-start(s32[16]{0:T(128)} %modes_ref.1) | copy-start | bytes 196
  0.0 10.1 %copy-start.1 = (f32[3,3,128,128]{3,2,1,0:T(8,128)S(1)}, f32[3,3,128,128]{3,2,1,0:T(8,128)}, u32[]{:S(2)}) copy-start(f32[3,3,128,128]{3,2,1,0:T(8,128)} %conv_ref.1) | copy-start | bytes 1769476
  0.0 10.1 %copy-start.4 = (f32[128,128]{1,0:T(8,128)S(1)}, f32[128,128]{1,0:T(8,128)}, u32[]{:S(2)}) copy-start(f32[128,128]{1,0:T(8,128)} %local_ref.1) | copy-start | bytes 196612
  0.0 10.1 %copy-start.2 = (f32[2,2,128,128]{3,2,1,0:T(8,128)S(1)}, f32[2,2,128,128]{3,2,1,0:T(8,128)}, u32[]{:S(2)}) copy-start(f32[2,2,128,128]{3,2,1,0:T(8,128)} %spectral_ref.1) | copy-start | bytes 786436
  2.7 23.3 %copy-start = (f32[16,256,128]{2,1,0:T(8,128)S(1)}, f32[16,256,128]{2,1,0:T(8,128)}, u32[]{:S(2)}) copy-start(f32[16,256,128]{2,1,0:T(8,128)} %field_ref.1) | copy-start | bytes 6291460
  2.7 23.3 %copy-start.3 = (s32[16,256]{1,0:T(8,128)S(1)}, s32[16,256]{1,0:T(8,128)}, u32[]{:S(2)}) copy-start(s32[16,256]{1,0:T(8,128)} %ocean_ref.5) | copy-start | bytes 49156
  2.7 23.3 %copy-start.6 = (f32[128]{0:T(128)S(1)}, f32[128]{0:T(128)}, u32[]{:S(2)}) copy-start(f32[128]{0:T(128)} %param.13) | copy-start | bytes 1540
  2.8 1.6 %collective-permute-start = (f32[144,256]{1,0:T(8,128)S(1)}, f32[144,256]{1,0:T(8,128)S(1)}, u32[]{:S(2)}, u32[]{:S(2)}) collective-permute-start(f32[144,256]{1,0:T(8,128)S(1)} %bitcast.14), channel_id=1, source_target_pairs={{0,1},{1,0},{2,3},{3,2},{4,5},{5,4},{6,7},{7,6},{8,9},{9,8},{10,11... | collective-permute-start | bytes 442376 | tf_op jit(solution)/shard_map/ppermute | solution.py:378
  4.4 9.6 %collective-permute-start.2 = (f32[48,256]{1,0:T(8,128)S(1)}, f32[48,256]{1,0:T(8,128)S(1)}, u32[]{:S(2)}, u32[]{:S(2)}) collective-permute-start(f32[48,256]{1,0:T(8,128)S(1)} %get-tuple-element.34), channel_id=1, source_target_pairs={{0,7},{1,6},{2,1},{3,0},{4,3},{5,2},{6,5},{7,4},{8,15},{9,14},{10,... | collective-permute-start | bytes 147464 | tf_op jit(solution)/shard_map/ppermute | solution.py:387
  9.1 5.3 %collective-permute-start.1 = (f32[48,256]{1,0:T(8,128)S(1)}, f32[48,256]{1,0:T(8,128)S(1)}, u32[]{:S(2)}, u32[]{:S(2)}) collective-permute-start(f32[48,256]{1,0:T(8,128)S(1)} %get-tuple-element.35), channel_id=1, source_target_pairs={{0,3},{1,2},{2,5},{3,4},{4,7},{5,6},{6,1},{7,0},{8,11},{9,10},{10,... | collective-permute-start | bytes 147464 | tf_op jit(solution)/shard_map/ppermute | solution.py:387
  9.1 4.8 %collective-permute-start.3 = (f32[32,256]{1,0:T(8,128)S(1)}, f32[32,256]{1,0:T(8,128)S(1)}, u32[]{:S(2)}, u32[]{:S(2)}) collective-permute-start(f32[32,256]{1,0:T(8,128)S(1)} %get-tuple-element.31), channel_id=1, source_target_pairs={{0,4},{1,5},{2,6},{3,7},{4,0},{5,1},{6,2},{7,3},{8,12},{9,13},{10,... | collective-permute-start | bytes 98312 | tf_op jit(solution)/shard_map/ppermute | solution.py:387
  14.7 18.7 %copy-start.7 = (f32[128]{0:T(128)S(1)}, f32[128]{0:T(128)}, u32[]{:S(2)}) copy-start(f32[128]{0:T(128)} %param.15) | copy-start | bytes 1540
  14.7 5.1 %collective-permute-start.6 = (f32[32,256]{1,0:T(8,128)S(1)}, f32[32,256]{1,0:T(8,128)S(1)}, u32[]{:S(2)}, u32[]{:S(2)}) collective-permute-start(f32[32,256]{1,0:T(8,128)S(1)} %mix.1), channel_id=1, source_target_pairs={{0,4},{1,5},{2,6},{3,7},{4,0},{5,1},{6,2},{7,3},{8,12},{9,13},{10,... | collective-permute-start | bytes 98312 | tf_op jit(solution)/shard_map/ppermute | solution.py:399
  16.4 4.0 %collective-permute-start.5 = (f32[32,256]{1,0:T(8,128)S(1)}, f32[32,256]{1,0:T(8,128)S(1)}, u32[]{:S(2)}, u32[]{:S(2)}) collective-permute-start(f32[32,256]{1,0:T(8,128)S(1)} %mix.1), channel_id=1, source_target_pairs={{0,6},{1,7},{2,0},{3,1},{4,2},{5,3},{6,4},{7,5},{8,14},{9,15},{10,... | collective-permute-start | bytes 98312 | tf_op jit(solution)/shard_map/ppermute | solution.py:399
  18.9 5.7 %collective-permute-start.4 = (f32[32,256]{1,0:T(8,128)S(1)}, f32[32,256]{1,0:T(8,128)S(1)}, u32[]{:S(2)}, u32[]{:S(2)}) collective-permute-start(f32[32,256]{1,0:T(8,128)S(1)} %mix.1), channel_id=1, source_target_pairs={{0,2},{1,3},{2,4},{3,5},{4,6},{5,7},{6,0},{7,1},{8,10},{9,11},{10,... | collective-permute-start | bytes 98312 | tf_op jit(solution)/shard_map/ppermute | solution.py:399
  24.6 1.4 %collective-permute-start.7 = (f32[128,256]{1,0:T(8,128)S(1)}, f32[128,256]{1,0:T(8,128)S(1)}, u32[]{:S(2)}, u32[]{:S(2)}) collective-permute-start(f32[128,256]{1,0:T(8,128)S(1)} %pad_maximum_fusion), channel_id=1, source_target_pairs={{0,1},{1,0},{2,3},{3,2},{4,5},{5,4},{6,7},{7,6},{8,9},{9,8},{10,11... | collective-permute-start | bytes 393224 | tf_op jit(solution)/shard_map/ppermute | solution.py:401
  28.5 10.2 %collective-permute-start.9 = (f32[1,272,128]{2,1,0:T(8,128)S(1)}, f32[1,272,128]{2,1,0:T(8,128)S(1)}, u32[]{:S(2)}, u32[]{:S(2)}) collective-permute-start(f32[1,272,128]{2,1,0:T(8,128)S(1)} %get-tuple-element.29), channel_id=1, source_target_pairs={{8,16},{16,8},{9,17},{17,9},{10,18},{18,10},{11,19},{19,11},{12,20... | collective-permute-start | bytes 417800 | tf_op jit(solution)/shard_map/ppermute | solution.py:420
  29.1 10.9 %collective-permute-start.8 = (f32[1,272,128]{2,1,0:T(8,128)S(1)}, f32[1,272,128]{2,1,0:T(8,128)S(1)}, u32[]{:S(2)}, u32[]{:S(2)}) collective-permute-start(f32[1,272,128]{2,1,0:T(8,128)S(1)} %get-tuple-element.30), channel_id=1, source_target_pairs={{0,8},{16,24},{8,0},{24,16},{1,9},{17,25},{9,1},{25,17},{2,10},{18... | collective-permute-start | bytes 417800 | tf_op jit(solution)/shard_map/ppermute | solution.py:419

commit v2 on v1

v2 whole, which is shorter than its diff:
```python
import functools
import math

import jax
import jax.numpy as jnp
from jax import lax
from jax.experimental import pallas as pl
from jax.experimental.pallas import tpu as pltpu
from jax.sharding import PartitionSpec as P

LANES = 128
TAIL = 16
MIB = 1 << 20
DRY = -(2.0**36)
F32 = jnp.float32
BF16 = jnp.bfloat16


def flip_of(distance, chips):
    return 1 if distance in (1, chips - 1) else 0


def chip_moves(distance, chips, flip):
    return [
        (2 * chip + core, 2 * ((chip + distance) % chips) + (core ^ flip))
        for chip in range(chips)
        for core in range(2)
    ]


def pair_moves(chips):
    return [(device, device ^ 1) for device in range(2 * chips)]


def distances(chips):
    return [1, chips - 1] + list(range(2, chips - 1))


def gather_source(chip, distance, chips):
    if chips & (chips - 1):
        return lax.rem(chip - distance + chips, chips)
    return chip ^ distance


def gather_moves(distance, chips):
    if chips & (chips - 1):
        return chip_moves(distance, chips, 0)
    return [
        (2 * chip + core, 2 * (chip ^ distance) + core) for chip in range(chips) for core in range(2)
    ]


def split(x):
    high = x.astype(BF16)
    return high, (x - high.astype(F32)).astype(BF16)


def dot(a, b):
    return lax.dot_general(a, b, (((1,), (0,)), ((), ())), preferred_element_type=F32)


def fill(blocks, depth):
    missing = depth - sum(block.shape[0] for block in blocks)
    if missing:
        blocks = blocks + [jnp.zeros((missing,) + blocks[0].shape[1:], blocks[0].dtype)]
    return jnp.concatenate(blocks, 0)


def angles(mode_list, lon, total_lon):
    row = lax.broadcasted_iota(jnp.int32, lon.shape, 0)
    ids = jnp.zeros(lon.shape, jnp.int32)
    for index, mode in enumerate(mode_list):
        ids = jnp.where(row == index, mode, ids)
    product = ids * lon
    if total_lon & (total_lon - 1):
        product = lax.rem(product, total_lon)
    else:
        product = product & (total_lon - 1)
    return product.astype(F32) * (2.0 * math.pi / total_lon)


def forward_kernel(
    chips, per, total_lon, modes_hbm, field_hbm, ocean_hbm, give_ref, keep_ref, away_ref,
    modes_ref, field_ref, ocean_ref, small_sem, field_sem,
):
    rows, width, channels = field_ref.shape
    chunks = field_sem.shape[0]
    step = rows // chunks
    first_copy = pltpu.make_async_copy(modes_hbm, modes_ref, small_sem.at[0])
    first_copy.start()
    copies = []
    for k in range(chunks):
        part = pl.ds(k * step, step)
        copies.append(pltpu.make_async_copy(field_hbm.at[part], field_ref.at[part], field_sem.at[k]))
        copies[-1].start()
    ocean_copy = pltpu.make_async_copy(ocean_hbm, ocean_ref, small_sem.at[1])
    ocean_copy.start()
    here = lax.axis_index("lon")
    chip, core = here // 2, lax.rem(here, 2)
    first_copy.wait()
    mode_list = []
    for flipped in range(2):
        for d in range(chips):
            owner = 2 * lax.rem(chip + d, chips)
            owner = owner + lax.rem(core + flipped + flip_of(d, chips), 2)
            mode_list += [modes_ref[owner * per + t] for t in range(per)]
    count = len(mode_list)
    half = count // 2
    lon = here * width + lax.broadcasted_iota(jnp.int32, (count, width), 1)
    theta = angles(mode_list, lon, total_lon)
    scale = 1.0 / math.sqrt(total_lon)
    table = jnp.concatenate([jnp.cos(theta) * scale, -jnp.sin(theta) * scale], 0)
    lhs = jnp.concatenate(split(table), 0)
    for i in range(rows):
        if i % step == 0:
            copies[i // step].wait()
        rhs = jnp.concatenate(split(field_ref[i]), 1)
        product = dot(lhs, rhs)
        total = product[: 2 * count] + product[2 * count :]
        total = total[:, :channels] + total[:, channels:]
        keep_ref[:half, i, :channels] = total[:half]
        give_ref[:half, i, :channels] = total[half:count]
        keep_ref[:half, i, channels:] = total[count : count + half]
        give_ref[:half, i, channels:] = total[count + half :]
    ocean_copy.wait()
    last = field_ref[:, width - 1, :]
    first = field_ref[:, 0, :]
    land = ocean_ref[...].astype(F32)
    last_wet = jnp.broadcast_to(land[:, width - 1 : width], (rows, channels))
    first_wet = jnp.broadcast_to(land[:, :1], (rows, channels))
    near_is_last = core == 0
    give_ref[half, :, :channels] = jnp.where(near_is_last, last, first)
    give_ref[half, :, channels:] = jnp.where(near_is_last, last_wet, first_wet)
    away_ref[0, :, :channels] = jnp.where(near_is_last, first, last)
    away_ref[0, :, channels:] = jnp.where(near_is_last, first_wet, last_wet)


def prepare_kernel(
    chips, per, total_lon, modes_ref, local_ref, spectral_ref, ocean_ref, trig_ref, local_out, mix_ref
):
    channels = local_ref.shape[0]
    rows, width = ocean_ref.shape
    wide = 2 * channels
    for t in range(per):
        real, imag = spectral_ref[t, 0], spectral_ref[t, 1]
        top = jnp.concatenate(split(jnp.concatenate([real, imag], 1)), 1)
        low = jnp.concatenate(split(jnp.concatenate([-imag, real], 1)), 1)
        mix_ref[t * wide : t * wide + channels, :] = top
        mix_ref[t * wide + channels : (t + 1) * wide, :] = low
    here = lax.axis_index("lon")
    chip, core = here // 2, lax.rem(here, 2)
    mode_list = []
    for flipped in range(2):
        for d in range(chips):
            source = 2 * gather_source(chip, d, chips) + lax.rem(core + flipped, 2)
            mode_list += [modes_ref[source * per + t] for t in range(per)]
    count = len(mode_list)
    block = width + TAIL
    padded = -(-block // LANES) * LANES
    place = lax.broadcasted_iota(jnp.int32, (count, padded), 1)
    place = jnp.where(place == block - 1, -1, place)
    lon = here * width + place + total_lon
    lon = jnp.where(lon >= total_lon, lon - total_lon, lon)
    lon = jnp.where(lon >= total_lon, lon - total_lon, lon)
    theta = angles(mode_list, lon, total_lon)
    scale = 2.0 / math.sqrt(count)
    table = jnp.concatenate([jnp.cos(theta) * scale, -jnp.sin(theta) * scale], 0)
    high, low = split(table)
    high, low = high.astype(F32), low.astype(F32)
    land = 1.0 - ocean_ref[...].astype(F32)
    land = jnp.concatenate([land, jnp.ones((rows, padded - width), F32)], 1)
    ones = jnp.where(lax.broadcasted_iota(jnp.int32, (8, padded), 0) < 3, 1.0, 0.0)
    stacked = fill([high, low, high, land, ones], trig_ref.shape[1])
    trig_ref[...] = stacked.T[:block].astype(BF16)
    local_out[...] = jnp.concatenate(split(local_ref[...]), 1)


def filter_kernel(conv_ref, out_ref):
    channels = conv_ref.shape[2]
    for col in range(3):
        left = slice(col * channels, (col + 1) * channels)
        right = slice((3 + col) * channels, (4 + col) * channels)
        low, mid, up = (conv_ref[row, col] for row in range(3))
        outer = 0.5 * (low + up)
        for k, taps in enumerate((low, outer + 0.5 * mid, outer - 0.5 * mid, up, mid)):
            top, bottom = split(taps)
            out_ref[k, :channels, left] = top
            out_ref[k, :channels, right] = bottom
            out_ref[k, channels:, left] = top
            out_ref[k, channels:, right] = jnp.zeros_like(top)


def gelu(x):
    inner = math.sqrt(2.0 / math.pi) * (x + 0.044715 * (x * x * x))
    return x * (0.5 * (1.0 + jnp.tanh(inner)))


def mix_kernel(per, rows, *refs):
    summed_ref, *part_refs, mix_ref, out_ref = refs
    wide = summed_ref.shape[1]
    for t in range(per):
        at = slice(t * rows, (t + 1) * rows)
        total = summed_ref[at, :]
        for part in part_refs:
            total = total + part[at, :]
        high, low = split(total)
        weights = mix_ref[t * wide : (t + 1) * wide, :]
        y = dot(high, weights)
        out_ref[at, :] = y[:, :wide] + y[:, wide:] + dot(low, weights[:, :wide])


def hidden_kernel(
    per, field_ref, got_ref, west_ref, east_ref, mixed_ref, trig_ref, local_ref, bias_ref,
    hidden_ref, edge_ref,
):
    rows, width, channels = field_ref.shape
    block = width + TAIL
    count = mixed_ref.shape[0]
    depth = trig_ref.shape[1]
    empty = jnp.zeros((depth, channels), BF16)
    local = local_ref[...]
    south = lax.rem(lax.axis_index("lon"), 2) == 0
    even = lax.rem(lax.axis_index("lat"), 2)
    near = got_ref[got_ref.shape[0] - rows :, :]
    left = jnp.where(south, west_ref[per * rows :, :], near)
    right = jnp.where(south, near, east_ref[per * rows :, :])
    place = lax.broadcasted_iota(jnp.int32, (TAIL, channels), 0)
    first = 6 * count
    lane = lax.broadcasted_iota(jnp.int32, (rows, depth), 1)
    mine = lane == first + lax.broadcasted_iota(jnp.int32, (rows, depth), 0)
    dry = [jnp.sum(jnp.where(mine, 1.0 - side[:, channels : channels + 1], 0.0), 0, keepdims=True) for side in (left, right)]
    tail_place = lax.broadcasted_iota(jnp.int32, (TAIL, depth), 0)
    tail_lane = lax.broadcasted_iota(jnp.int32, (TAIL, depth), 1)
    is_land = (tail_lane >= first) & (tail_lane < first + rows)
    end = trig_ref[width:, :].astype(F32)
    end = jnp.where(is_land & (tail_place == TAIL - 1), dry[0], end)
    end = jnp.where(is_land & (tail_place == 0), dry[1], end)
    trig = jnp.concatenate([trig_ref[:width, :], end.astype(BF16)], 0)
    b_high, b_mid = split(bias_ref[...])
    rest = bias_ref[...] - b_high.astype(F32) - b_mid.astype(F32)
    shape8 = (8, channels)
    row8 = lax.broadcasted_iota(jnp.int32, shape8, 0)
    bias8 = jnp.where(
        row8 == 0, b_high.astype(F32), jnp.where(row8 == 1, b_mid.astype(F32), jnp.where(row8 == 2, rest, 0.0))
    ).astype(F32)
    select = lax.broadcasted_iota(jnp.int32, (rows, channels), 0)
    for i in range(rows):
        side = jnp.where(
            place == TAIL - 1, left[i : i + 1, :channels], jnp.where(place == 0, right[i : i + 1, :channels], 0.0)
        )
        x = jnp.concatenate([field_ref[i], side], 0)
        x_high, x_low = split(x)
        mixed = jnp.concatenate([mixed_ref[:, i, :channels], mixed_ref[:, i, channels:]], 0)
        m_high, m_low = split(mixed)
        cut = jnp.where(select == i, DRY, 0.0)
        extra = jnp.concatenate([cut, bias8], 0).astype(BF16)
        spare = depth - first - extra.shape[0]
        extra = jnp.concatenate([extra, jnp.zeros((spare, channels), BF16)], 0)
        lower = jnp.concatenate([m_high, m_high, m_low, extra], 0)
        rhs = jnp.concatenate([local, jnp.concatenate([lower, empty], 1)], 0)
        lhs = jnp.concatenate([x_high, trig], 1)
        y = dot(lhs, rhs)
        y = gelu(y[:, :channels] + y[:, channels:] + dot(x_low, local[:, :channels]))
        hidden_ref[i * block : (i + 1) * block, :] = y
        if i == 0:
            edge_ref[1 - even] = y
        if i == rows - 1:
            edge_ref[even] = y


def columns(t, channels, keep):
    west = pltpu.roll(t[:, :channels], 1, 0)
    east = pltpu.roll(t[:, 2 * channels :], t.shape[0] - 1, 0)
    return (west + t[:, channels : 2 * channels] + east)[:keep]


def product(parts, weights, channels):
    lhs = jnp.concatenate([jnp.concatenate(split(part), 1) for part in parts], 0)
    y = dot(lhs, weights)
    return y[:, : 3 * channels] + y[:, 3 * channels :]


def inner_kernel(groups, hidden_ref, ocean_ref, bias_ref, filter_ref, out_ref):
    _, width = ocean_ref.shape
    channels = hidden_ref.shape[1]
    block = width + TAIL
    wet = ocean_ref[...].astype(F32).T
    for group in groups:
        terms = [[], [], [], []]
        for first in group:
            d = [hidden_ref[(first - 1 + k) * block : (first + k) * block, :] for k in range(4)]
            terms[0].append(d[0] - d[2])
            terms[1].append(d[1] + d[2])
            terms[2].append(d[2] - d[1])
            terms[3].append(d[1] - d[3])
        m = [product(terms[k], filter_ref[k], channels) for k in range(4)]
        pair = (m[0] + m[1] + m[2], m[1] - m[2] - m[3])
        for g, first in enumerate(group):
            for r in range(2):
                t = columns(pair[r][g * block : (g + 1) * block], channels, width)
                row = first + r
                out_ref[row - 1] = (t + bias_ref[...]) * wet[:, row : row + 1]


def outer_kernel(
    hidden_ref, first_ref, second_ref, ocean_ref, bias_ref, filter_ref, inner_ref, out_ref, buf_ref, sem_ref
):
    rows, width = ocean_ref.shape
    channels = hidden_ref.shape[1]
    block = width + TAIL
    middle = pltpu.make_async_copy(inner_ref, out_ref.at[pl.ds(1, rows - 2)], sem_ref.at[2])
    middle.start()
    wet = ocean_ref[...].astype(F32).T

    def at(row):
        return hidden_ref[row * block : (row + 1) * block, :]

    even = lax.rem(lax.axis_index("lat"), 2) == 0
    above = jnp.where(even, second_ref[0], first_ref[0])
    below = jnp.where(even, first_ref[0], second_ref[0])
    z = product([at(0), at(rows - 1)], filter_ref[4], channels)
    z = z + product([at(1), below], filter_ref[3], channels)
    z = z + product([above, at(rows - 2)], filter_ref[0], channels)
    copies = [middle]
    for r, row in enumerate((0, rows - 1)):
        t = columns(z[r * block : (r + 1) * block], channels, width)
        buf_ref[r] = (t + bias_ref[...]) * wet[:, row : row + 1]
        copy = pltpu.make_async_copy(buf_ref.at[pl.ds(r, 1)], out_ref.at[pl.ds(row, 1)], sem_ref.at[r])
        copy.start()
        copies.append(copy)
    for copy in copies:
        copy.wait()


def vmem():
    return pl.BlockSpec(memory_space=pltpu.VMEM)


def smem():
    return pl.BlockSpec(memory_space=pltpu.SMEM)


def struct(shape, dtype=F32):
    return jax.ShapeDtypeStruct(shape, dtype)


def params(mib):
    return pltpu.CompilerParams(vmem_limit_bytes=mib * MIB)


def per_device(
    field, ocean, modes, spectral_weight, local_weight, layer_bias, conv_weight, conv_bias
):
    rows, width, channels = field.shape
    devices = lax.axis_size("lon")
    chips = devices // 2
    bands = lax.axis_size("lat")
    total_lon = width * devices
    total_modes = modes.shape[0]
    per = total_modes // devices
    half = chips * per
    block = width + TAIL
    steps = distances(chips)
    wide = 2 * channels
    chunks = 2

    give, keep, away = pl.pallas_call(
        functools.partial(forward_kernel, chips, per, total_lon),
        out_shape=(
            struct((half + 1, rows, wide)),
            struct((half, rows, wide)),
            struct((1, rows, wide)),
        ),
        in_specs=[pl.BlockSpec(memory_space=pltpu.MemorySpace.HBM)] * 3,
        out_specs=(vmem(), vmem(), vmem()),
        scratch_shapes=[
            pltpu.SMEM((total_modes,), jnp.int32),
            pltpu.VMEM((rows, width, channels), F32),
            pltpu.VMEM((rows, width), jnp.int32),
            pltpu.SemaphoreType.DMA((2,)),
            pltpu.SemaphoreType.DMA((chunks,)),
        ],
        compiler_params=params(16),
        name="forward",
    )(*[pltpu.with_memory_space_constraint(x, pltpu.MemorySpace.HBM) for x in (modes, field, ocean)])
    give = give.reshape((half + 1) * rows, wide)
    keep = keep.reshape(half * rows, wide)
    away = away.reshape(rows, wide)

    depth = -(-(6 * total_modes + rows + 8) // LANES) * LANES
    trig, local, mix = pl.pallas_call(
        functools.partial(prepare_kernel, chips, per, total_lon),
        out_shape=(
            struct((block, depth), BF16),
            struct((channels, 2 * channels), BF16),
            struct((per * wide, 2 * wide), BF16),
        ),
        in_specs=[smem(), vmem(), vmem(), vmem()],
        out_specs=(vmem(),) * 3,
        compiler_params=params(16),
        name="prepare",
    )(modes, local_weight, spectral_weight, ocean)
    filters = pl.pallas_call(
        filter_kernel,
        out_shape=struct((5, 2 * channels, 6 * channels), BF16),
        in_specs=[vmem()],
        out_specs=vmem(),
        compiler_params=params(16),
        name="filters",
    )(conv_weight)

    got = lax.ppermute(give, "lon", pair_moves(chips))
    summed = keep + got[: half * rows]
    size = per * rows
    parts = {}
    for d in steps:
        send = summed[d * size : (d + 1) * size]
        flip = flip_of(d, chips)
        if flip:
            send = jnp.concatenate([send, away])
        parts[d] = lax.ppermute(send, "lon", chip_moves(d, chips, flip))

    own_mixed = pl.pallas_call(
        functools.partial(mix_kernel, per, rows),
        out_shape=struct((size, wide)),
        in_specs=[vmem()] * (len(steps) + 2),
        out_specs=vmem(),
        compiler_params=params(8),
        name="mix",
    )(summed, *[parts[d] for d in steps], mix)
    gathered = [own_mixed]
    for d in range(1, chips):
        gathered.append(lax.ppermute(own_mixed, "lon", gather_moves(d, chips)))
    gathered = jnp.concatenate(gathered)
    other = lax.ppermute(gathered, "lon", pair_moves(chips))
    mixed = jnp.concatenate([gathered, other]).reshape(total_modes, rows, wide)

    hidden, edge = pl.pallas_call(
        functools.partial(hidden_kernel, per),
        out_shape=(struct((rows * block, channels)), struct((2, block, channels))),
        in_specs=[vmem()] * 8,
        out_specs=(vmem(),) * 2,
        compiler_params=params(24),
        name="hidden",
    )(field, got, parts[1], parts[chips - 1], mixed, trig, local, layer_bias.reshape(1, channels))

    evens = [(i, i + 1) for i in range(0, bands - 1, 2)]
    odds = [(i, i + 1) for i in range(1, bands - 1, 2)]
    first = lax.ppermute(edge[:1], "lat", evens + [(b, a) for a, b in evens])
    second = lax.ppermute(edge[1:], "lat", odds + [(b, a) for a, b in odds])
    bias = conv_bias.reshape(1, channels)
    firsts = list(range(1, rows - 1, 2))
    groups = [firsts[k : k + 2] for k in range(0, len(firsts), 2)]
    if len(groups) > 1 and len(groups[-1]) == 1:
        groups[-2:] = [groups[-2] + groups[-1]]
    flops = 2 * 6 * 4 * rows * width * channels * channels
    inner = pl.pallas_call(
        functools.partial(inner_kernel, groups),
        out_shape=struct((rows - 2, width, channels)),
        in_specs=[vmem()] * 4,
        out_specs=vmem(),
        compiler_params=params(24),
        cost_estimate=pl.CostEstimate(flops=flops, transcendentals=0, bytes_accessed=4 * field.size),
        name="inner",
    )(hidden, ocean, bias, filters)
    return pl.pallas_call(
        outer_kernel,
        out_shape=struct((rows, width, channels)),
        in_specs=[vmem()] * 7,
        out_specs=pl.BlockSpec(memory_space=pl.ANY),
        scratch_shapes=[
            pltpu.VMEM((2, width, channels), F32),
            pltpu.SemaphoreType.DMA((3,)),
        ],
        compiler_params=params(24),
        name="outer",
    )(hidden, first, second, ocean, bias, filters, inner)


def solution(mesh):
    in_specs = (
        P("lat", "lon", None),
        P("lat", "lon"),
        P(),
        P("lon", None, None, None),
        P(),
        P(),
        P(),
        P(),
    )
    out_specs = P("lat", "lon", None)
    return jax.shard_map(
        per_device, mesh=mesh, in_specs=in_specs, out_specs=out_specs, check_vma=False
    )
```

time: 42.2 us -> 38.2 us (0.905)
  Pallas kernels: 13.4 us -> 9.84 us
  waiting for transfers between devices: 12.8 us -> 12.2 us
    ppermute x3, waiting for transfers between devices: 5.7 us -> 3.7 us  [per_device(): gathered.append(lax.ppermute(own_mixed, 'lon', gather_moves(d, chips)))]
    ppermute x1, waiting for transfers between devices: 1.4 us -> 2.94 us  [per_device(): first = lax.ppermute(edge[:1], 'lat', evens + [(b, a) for a, b in evens])]
    pallas_call x2 -> x3, Pallas kernels: 6.09 us -> 4.7 us  [the longest x1 3.64 us: per_device(): pl.pallas_call(functools.partial(inner_kernel, groups), out_shape=struct(...]
    pallas_call x1, Pallas kernels: 2.37 us -> 1.36 us  [per_device(): pl.pallas_call(functools.partial(hidden_kernel, per), out_shape=(struct((...]
    pallas_call x1, Pallas kernels: 2.63 us -> 2.04 us  [per_device(): pl.pallas_call(functools.partial(forward_kernel, chips, per, total_lon),...]
    pallas_call x1, Pallas kernels: 2.06 us -> 1.52 us  [per_device(): pl.pallas_call(outer_kernel, out_shape=struct((rows, width, channels)), i...]
  transfers between devices with their start and end apart: 10 -> 10, of which waited for: 8 -> 7; matrix products, arithmetic and copies ran while one was open for 0% -> 0% of each run, Pallas kernels for 14% -> 12%
where the time goes in v2:
time: 38.2 us; the launch traced here: 38.1 us
  starting transfers between devices  15.7 us (41%)
  waiting for transfers between devices  12.2 us (32%)
  Pallas kernels  9.84 us (26%)
    ppermute x3, starting transfers between devices, per_device(): parts[d] = lax.ppermute(send, 'lon', chip_moves(d, chips, flip))  5.74 us
    ppermute x3, starting transfers between devices, per_device(): gathered.append(lax.ppermute(own_mixed, 'lon', gather_moves(d, chips)))  4.39 us
    ppermute x1, starting transfers between devices, per_device(): first = lax.ppermute(edge[:1], 'lat', evens + [(b, a) for a, b in evens])  4.29 us
    ppermute x3, waiting for transfers between devices, per_device(): gathered.append(lax.ppermute(own_mixed, 'lon', gather_moves(d, chips)))  3.7 us
    pallas_call x1, Pallas kernels, per_device(): pl.pallas_call(functools.partial(inner_kernel, groups), out_shape=struct(...  3.64 us
    ppermute x3, waiting for transfers between devices, per_device(): parts[d] = lax.ppermute(send, 'lon', chip_moves(d, chips, flip))  3.25 us
    ppermute x1, waiting for transfers between devices, per_device(): first = lax.ppermute(edge[:1], 'lat', evens + [(b, a) for a, b in evens])  2.94 us
    pallas_call x1, Pallas kernels, per_device(): pl.pallas_call(functools.partial(forward_kernel, chips, per, total_lon),...  2.04 us
  transfers between devices with their start and end apart: 10, of which 7 were waited for; matrix products, arithmetic and copies ran while one was open for 0% of the time, Pallas kernels for 12%

profile of v2, /device:TPU:0, one launch (start us, length us, event | category | flops | bytes accessed | tf_op | source)
XLA Modules:
  0.0 38.1 jit_solution(10384763350767361146)
XLA Ops:
  0.0 0.0 copy-start.1
  0.0 2.0 %forward.1 = (f32[9,16,256]{2,1,0:T(8,128)S(1)}, f32[8,16,256]{2,1,0:T(8,128)S(1)}, f32[1,16,256]{2,1,0:T(8,128)S(1)}) custom-call(s32[16]{0:T(128)} %modes_ref.1, f32[16,256,128]{2,1,0:T(8,128)} %field_ref.1, s32[16,256]{1,0:T(8,128)} %ocean_ref.5), custom_call_target="tpu_custom_call" | custom-call | tf_op jit(solution)/shard_map/forward/pallas_call | solution.py:367
  2.1 0.0 copy-start.2
  2.1 0.0 copy-start.3
  2.1 0.0 copy-start.4
  2.1 0.0 copy-start.5
  2.1 0.6 %collective-permute-start = (f32[144,256]{1,0:T(8,128)S(1)}, f32[144,256]{1,0:T(8,128)S(1)}, u32[]{:S(2)}, u32[]{:S(2)}) collective-permute-start(f32[144,256]{1,0:T(8,128)S(1)} %bitcast.12), channel_id=1, source_target_pairs={{0,1},{1,0},{2,3},{3,2},{4,5},{5,4},{6,7},{7,6},{8,9},{9,8},{10,11... | collective-permute-start | bytes 442376 | tf_op jit(solution)/shard_map/ppermute | solution.py:412
  2.7 1.0 %collective-permute-done.got_ref = f32[144,256]{1,0:T(8,128)S(1)} collective-permute-done((f32[144,256]{1,0:T(8,128)S(1)}, f32[144,256]{1,0:T(8,128)S(1)}, u32[]{:S(2)}, u32[]{:S(2)}) %collective-permute-start) | collective-permute-done | bytes 147488 | tf_op jit(solution)/shard_map/ppermute | solution.py:412
  3.7 4.8 %collective-permute-start.2 = (f32[48,256]{1,0:T(8,128)S(1)}, f32[48,256]{1,0:T(8,128)S(1)}, u32[]{:S(2)}, u32[]{:S(2)}) collective-permute-start(f32[48,256]{1,0:T(8,128)S(1)} %get-tuple-element.26), channel_id=1, source_target_pairs={{0,7},{1,6},{2,1},{3,0},{4,3},{5,2},{6,5},{7,4},{8,15},{9,14},{10,... | collective-permute-start | bytes 147464 | tf_op jit(solution)/shard_map/ppermute | solution.py:421
  8.5 0.0 collective-permute-start.1
  8.5 0.0 copy-start
  8.5 0.0 copy-start.6
  8.5 1.0 %collective-permute-start.3 = (f32[32,256]{1,0:T(8,128)S(1)}, f32[32,256]{1,0:T(8,128)S(1)}, u32[]{:S(2)}, u32[]{:S(2)}) collective-permute-start(f32[32,256]{1,0:T(8,128)S(1)} %get-tuple-element.23), channel_id=1, source_target_pairs={{0,4},{1,5},{2,6},{3,7},{4,0},{5,1},{6,2},{7,3},{8,12},{9,13},{10,... | collective-permute-start | bytes 98312 | tf_op jit(solution)/shard_map/ppermute | solution.py:421
  9.5 0.0 copy-done.1
  9.5 0.3 filters.1.filter_ref
  9.8 0.0 copy-done.2
  9.8 0.0 copy-done.3
  9.8 0.0 copy-done.4
  9.8 0.0 copy-done.5
  9.8 0.8 %prepare.1 = (bf16[272,128]{1,0:T(8,128)(2,1)S(1)}, bf16[128,256]{1,0:T(8,128)(2,1)S(1)}, bf16[512,512]{1,0:T(8,128)(2,1)S(1)}) custom-call(s32[16]{0:T(128)S(1)} %copy-done.5, f32[128,128]{1,0:T(8,128)S(1)} %copy-done.4, f32[2,2,128,128]{3,2,1,0:T(8,128)S(1)} %copy-done.2, s32[16,256]{1,0:T(8,128)S(1)} %copy-done.3), custom_call_target="tpu_custom_call" | custom-call | tf_op jit(solution)/shard_map/prepare/pallas_call | solution.py:391
  10.6 2.7 %collective-permute-done.3.refs_3_ = f32[32,256]{1,0:T(8,128)S(1)} collective-permute-done((f32[32,256]{1,0:T(8,128)S(1)}, f32[32,256]{1,0:T(8,128)S(1)}, u32[]{:S(2)}, u32[]{:S(2)}) %collective-permute-start.3) | collective-permute-done | bytes 32800 | tf_op jit(solution)/shard_map/ppermute | solution.py:421
  13.3 0.0 collective-permute-done.2.refs_2_.east_ref
  13.3 0.5 %collective-permute-done.1.refs_1_.west_ref = f32[48,256]{1,0:T(8,128)S(1)} collective-permute-done((f32[48,256]{1,0:T(8,128)S(1)}, f32[48,256]{1,0:T(8,128)S(1)}, u32[]{:S(2)}, u32[]{:S(2)}) %collective-permute-start.1) | collective-permute-done | bytes 49184 | tf_op jit(solution)/shard_map/ppermute | solution.py:421
  13.8 0.2 mix.1
  14.0 0.0 copy-start.7
  14.0 3.3 %collective-permute-start.6 = (f32[32,256]{1,0:T(8,128)S(1)}, f32[32,256]{1,0:T(8,128)S(1)}, u32[]{:S(2)}, u32[]{:S(2)}) collective-permute-start(f32[32,256]{1,0:T(8,128)S(1)} %mix.1), channel_id=1, source_target_pairs={{0,6},{1,7},{2,4},{3,5},{4,2},{5,3},{6,0},{7,1},{8,14},{9,15},{10,... | collective-permute-start | bytes 98312 | tf_op jit(solution)/shard_map/ppermute | solution.py:433
  17.3 0.0 collective-permute-start.5
  17.3 1.1 %collective-permute-start.4 = (f32[32,256]{1,0:T(8,128)S(1)}, f32[32,256]{1,0:T(8,128)S(1)}, u32[]{:S(2)}, u32[]{:S(2)}) collective-permute-start(f32[32,256]{1,0:T(8,128)S(1)} %mix.1), channel_id=1, source_target_pairs={{0,2},{1,3},{2,0},{3,1},{4,6},{5,7},{6,4},{7,5},{8,10},{9,11},{10,... | collective-permute-start | bytes 98312 | tf_op jit(solution)/shard_map/ppermute | solution.py:433
  18.4 1.8 %collective-permute-done.6 = f32[32,256]{1,0:T(8,128)S(1)} collective-permute-done((f32[32,256]{1,0:T(8,128)S(1)}, f32[32,256]{1,0:T(8,128)S(1)}, u32[]{:S(2)}, u32[]{:S(2)}) %collective-permute-start.6) | collective-permute-done | bytes 32800 | tf_op jit(solution)/shard_map/ppermute | solution.py:433
  20.2 1.9 %collective-permute-done.5 = f32[32,256]{1,0:T(8,128)S(1)} collective-permute-done((f32[32,256]{1,0:T(8,128)S(1)}, f32[32,256]{1,0:T(8,128)S(1)}, u32[]{:S(2)}, u32[]{:S(2)}) %collective-permute-start.5) | collective-permute-done | bytes 32800 | tf_op jit(solution)/shard_map/ppermute | solution.py:433
  22.1 0.0 collective-permute-done.4
  22.1 0.1 collective-permute-start.7
  22.3 1.3 %collective-permute-done.7 = f32[128,256]{1,0:T(8,128)S(1)} collective-permute-done((f32[128,256]{1,0:T(8,128)S(1)}, f32[128,256]{1,0:T(8,128)S(1)}, u32[]{:S(2)}, u32[]{:S(2)}) %collective-permute-start.7) | collective-permute-done | bytes 131104 | tf_op jit(solution)/shard_map/ppermute | solution.py:435
  23.6 0.0 copy-done
  23.6 0.0 copy-done.6
  23.6 1.4 %hidden.1 = (f32[4352,128]{1,0:T(8,128)S(1)}, f32[2,272,128]{2,1,0:T(8,128)S(1)}) custom-call(f32[16,256,128]{2,1,0:T(8,128)S(1)} %copy-done, f32[144,256]{1,0:T(8,128)S(1)} %collective-permute-done.got_ref, f32[48,256]{1,0:T(8,128)S(1)} %collective-permute-done.1.refs_1_.west_ref, f32[48,256]{1,0:T(8,128)S(1)} %collective-permute-done.2.refs_2_.east_ref, ...), custom_call_target="tpu_custom_call" | custom-call | tf_op jit(solution)/shard_map/hidden/pallas_call | solution.py:438
  25.0 0.7 %collective-permute-start.9 = (f32[1,272,128]{2,1,0:T(8,128)S(1)}, f32[1,272,128]{2,1,0:T(8,128)S(1)}, u32[]{:S(2)}, u32[]{:S(2)}) collective-permute-start(f32[1,272,128]{2,1,0:T(8,128)S(1)} %get-tuple-element.21), channel_id=1, source_target_pairs={{8,16},{16,8},{9,17},{17,9},{10,18},{18,10},{11,19},{19,11},{12,20... | collective-permute-start | bytes 417800 | tf_op jit(solution)/shard_map/ppermute | solution.py:450
  25.7 4.3 %collective-permute-start.8 = (f32[1,272,128]{2,1,0:T(8,128)S(1)}, f32[1,272,128]{2,1,0:T(8,128)S(1)}, u32[]{:S(2)}, u32[]{:S(2)}) collective-permute-start(f32[1,272,128]{2,1,0:T(8,128)S(1)} %get-tuple-element.22), channel_id=1, source_target_pairs={{0,8},{16,24},{8,0},{24,16},{1,9},{17,25},{9,1},{25,17},{2,10},{18... | collective-permute-start | bytes 417800 | tf_op jit(solution)/shard_map/ppermute | solution.py:449
  30.0 0.0 copy-done.7
  30.0 3.6 %inner.1.inner_ref = f32[14,256,128]{2,1,0:T(8,128)S(1)} custom-call(f32[4352,128]{1,0:T(8,128)S(1)} %get-tuple-element.19.hidden_ref, s32[16,256]{1,0:T(8,128)S(1)} %copy-done.3, f32[1,128]{1,0:T(1,128)S(1)} %bitcast.10, bf16[5,256,768]{2,1,0:T(8,128)(2,1)S(1)} %filters.1.filter_ref), custom_call_target="tpu_custom_call" | custom-call | flops 3221225472 | bytes 2097152 | tf_op jit(solution)/shard_map/inner/pallas_call | solution.py:457
  33.6 0.0 collective-permute-done.9.second_ref
  33.6 2.9 %collective-permute-done.8.first_ref = f32[1,272,128]{2,1,0:T(8,128)S(1)} collective-permute-done((f32[1,272,128]{2,1,0:T(8,128)S(1)}, f32[1,272,128]{2,1,0:T(8,128)S(1)}, u32[]{:S(2)}, u32[]{:S(2)}) %collective-permute-start.8) | collective-permute-done | bytes 139296 | tf_op jit(solution)/shard_map/ppermute | solution.py:449
  36.6 1.5 %outer.1 = f32[16,256,128]{2,1,0:T(8,128)} custom-call(f32[4352,128]{1,0:T(8,128)S(1)} %get-tuple-element.19.hidden_ref, f32[1,272,128]{2,1,0:T(8,128)S(1)} %collective-permute-done.8.first_ref, f32[1,272,128]{2,1,0:T(8,128)S(1)} %collective-permute-done.9.second_ref, s32[16,256]{1,0:T(8,128)S(1)} %copy-done.3, f32[1,128]{1,0:T(1,128)S(1)} %bitcast.11, ...), custom_call_target="tpu_custom_call" | custom-call | tf_op jit(solution)/shard_map/outer/pallas_call | solution.py:466
  (10 shorter events, 0.1 us)
Async XLA Ops:
  0.0 9.5 %copy-start.1 = (f32[3,3,128,128]{3,2,1,0:T(8,128)S(1)}, f32[3,3,128,128]{3,2,1,0:T(8,128)}, u32[]{:S(2)}) copy-start(f32[3,3,128,128]{3,2,1,0:T(8,128)} %conv_ref.1) | copy-start | bytes 1769476
  2.1 7.7 %copy-start.2 = (f32[2,2,128,128]{3,2,1,0:T(8,128)S(1)}, f32[2,2,128,128]{3,2,1,0:T(8,128)}, u32[]{:S(2)}) copy-start(f32[2,2,128,128]{3,2,1,0:T(8,128)} %spectral_ref.1) | copy-start | bytes 786436
  2.1 7.7 %copy-start.3 = (s32[16,256]{1,0:T(8,128)S(1)}, s32[16,256]{1,0:T(8,128)}, u32[]{:S(2)}) copy-start(s32[16,256]{1,0:T(8,128)} %ocean_ref.5) | copy-start | bytes 49156
  2.1 7.7 %copy-start.4 = (f32[128,128]{1,0:T(8,128)S(1)}, f32[128,128]{1,0:T(8,128)}, u32[]{:S(2)}) copy-start(f32[128,128]{1,0:T(8,128)} %local_ref.1) | copy-start | bytes 196612
  2.1 7.7 %copy-start.5 = (s32[16]{0:T(128)S(1)}, s32[16]{0:T(128)}, u32[]{:S(2)}) copy-start(s32[16]{0:T(128)} %modes_ref.1) | copy-start | bytes 196
  2.1 1.6 %collective-permute-start = (f32[144,256]{1,0:T(8,128)S(1)}, f32[144,256]{1,0:T(8,128)S(1)}, u32[]{:S(2)}, u32[]{:S(2)}) collective-permute-start(f32[144,256]{1,0:T(8,128)S(1)} %bitcast.12), channel_id=1, source_target_pairs={{0,1},{1,0},{2,3},{3,2},{4,5},{5,4},{6,7},{7,6},{8,9},{9,8},{10,11... | collective-permute-start | bytes 442376 | tf_op jit(solution)/shard_map/ppermute | solution.py:412
  3.7 9.6 %collective-permute-start.2 = (f32[48,256]{1,0:T(8,128)S(1)}, f32[48,256]{1,0:T(8,128)S(1)}, u32[]{:S(2)}, u32[]{:S(2)}) collective-permute-start(f32[48,256]{1,0:T(8,128)S(1)} %get-tuple-element.26), channel_id=1, source_target_pairs={{0,7},{1,6},{2,1},{3,0},{4,3},{5,2},{6,5},{7,4},{8,15},{9,14},{10,... | collective-permute-start | bytes 147464 | tf_op jit(solution)/shard_map/ppermute | solution.py:421
  8.5 5.3 %collective-permute-start.1 = (f32[48,256]{1,0:T(8,128)S(1)}, f32[48,256]{1,0:T(8,128)S(1)}, u32[]{:S(2)}, u32[]{:S(2)}) collective-permute-start(f32[48,256]{1,0:T(8,128)S(1)} %get-tuple-element.27), channel_id=1, source_target_pairs={{0,3},{1,2},{2,5},{3,4},{4,7},{5,6},{6,1},{7,0},{8,11},{9,10},{10,... | collective-permute-start | bytes 147464 | tf_op jit(solution)/shard_map/ppermute | solution.py:421
  8.5 15.1 %copy-start = (f32[16,256,128]{2,1,0:T(8,128)S(1)}, f32[16,256,128]{2,1,0:T(8,128)}, u32[]{:S(2)}) copy-start(f32[16,256,128]{2,1,0:T(8,128)} %field_ref.1) | copy-start | bytes 6291460
  8.5 15.1 %copy-start.6 = (f32[128]{0:T(128)S(1)}, f32[128]{0:T(128)}, u32[]{:S(2)}) copy-start(f32[128]{0:T(128)} %param.13) | copy-start | bytes 1540
  8.5 4.8 %collective-permute-start.3 = (f32[32,256]{1,0:T(8,128)S(1)}, f32[32,256]{1,0:T(8,128)S(1)}, u32[]{:S(2)}, u32[]{:S(2)}) collective-permute-start(f32[32,256]{1,0:T(8,128)S(1)} %get-tuple-element.23), channel_id=1, source_target_pairs={{0,4},{1,5},{2,6},{3,7},{4,0},{5,1},{6,2},{7,3},{8,12},{9,13},{10,... | collective-permute-start | bytes 98312 | tf_op jit(solution)/shard_map/ppermute | solution.py:421
  14.0 15.9 %copy-start.7 = (f32[128]{0:T(128)S(1)}, f32[128]{0:T(128)}, u32[]{:S(2)}) copy-start(f32[128]{0:T(128)} %param.15) | copy-start | bytes 1540
  14.0 6.2 %collective-permute-start.6 = (f32[32,256]{1,0:T(8,128)S(1)}, f32[32,256]{1,0:T(8,128)S(1)}, u32[]{:S(2)}, u32[]{:S(2)}) collective-permute-start(f32[32,256]{1,0:T(8,128)S(1)} %mix.1), channel_id=1, source_target_pairs={{0,6},{1,7},{2,4},{3,5},{4,2},{5,3},{6,0},{7,1},{8,14},{9,15},{10,... | collective-permute-start | bytes 98312 | tf_op jit(solution)/shard_map/ppermute | solution.py:433
  17.3 4.8 %collective-permute-start.5 = (f32[32,256]{1,0:T(8,128)S(1)}, f32[32,256]{1,0:T(8,128)S(1)}, u32[]{:S(2)}, u32[]{:S(2)}) collective-permute-start(f32[32,256]{1,0:T(8,128)S(1)} %mix.1), channel_id=1, source_target_pairs={{0,4},{1,5},{2,6},{3,7},{4,0},{5,1},{6,2},{7,3},{8,12},{9,13},{10,... | collective-permute-start | bytes 98312 | tf_op jit(solution)/shard_map/ppermute | solution.py:433
  17.3 4.8 %collective-permute-start.4 = (f32[32,256]{1,0:T(8,128)S(1)}, f32[32,256]{1,0:T(8,128)S(1)}, u32[]{:S(2)}, u32[]{:S(2)}) collective-permute-start(f32[32,256]{1,0:T(8,128)S(1)} %mix.1), channel_id=1, source_target_pairs={{0,2},{1,3},{2,0},{3,1},{4,6},{5,7},{6,4},{7,5},{8,10},{9,11},{10,... | collective-permute-start | bytes 98312 | tf_op jit(solution)/shard_map/ppermute | solution.py:433
  22.1 1.4 %collective-permute-start.7 = (f32[128,256]{1,0:T(8,128)S(1)}, f32[128,256]{1,0:T(8,128)S(1)}, u32[]{:S(2)}, u32[]{:S(2)}) collective-permute-start(f32[128,256]{1,0:T(8,128)S(1)} %pad_maximum_fusion), channel_id=1, source_target_pairs={{0,1},{1,0},{2,3},{3,2},{4,5},{5,4},{6,7},{7,6},{8,9},{9,8},{10,11... | collective-permute-start | bytes 393224 | tf_op jit(solution)/shard_map/ppermute | solution.py:435
  25.0 8.6 %collective-permute-start.9 = (f32[1,272,128]{2,1,0:T(8,128)S(1)}, f32[1,272,128]{2,1,0:T(8,128)S(1)}, u32[]{:S(2)}, u32[]{:S(2)}) collective-permute-start(f32[1,272,128]{2,1,0:T(8,128)S(1)} %get-tuple-element.21), channel_id=1, source_target_pairs={{8,16},{16,8},{9,17},{17,9},{10,18},{18,10},{11,19},{19,11},{12,20... | collective-permute-start | bytes 417800 | tf_op jit(solution)/shard_map/ppermute | solution.py:450
  25.7 10.9 %collective-permute-start.8 = (f32[1,272,128]{2,1,0:T(8,128)S(1)}, f32[1,272,128]{2,1,0:T(8,128)S(1)}, u32[]{:S(2)}, u32[]{:S(2)}) collective-permute-start(f32[1,272,128]{2,1,0:T(8,128)S(1)} %get-tuple-element.22), channel_id=1, source_target_pairs={{0,8},{16,24},{8,0},{24,16},{1,9},{17,25},{9,1},{25,17},{2,10},{18... | collective-permute-start | bytes 417800 | tf_op jit(solution)/shard_map/ppermute | solution.py:449

commit v3 on v2

--- a/solution.py
+++ b/solution.py
@@ -16,38 +16,18 @@
 BF16 = jnp.bfloat16
 
 
-def flip_of(distance, chips):
-    return 1 if distance in (1, chips - 1) else 0
+def flip_of(distance):
+    return 1 if distance & (distance + 1) == 0 and distance else 0
 
 
 def chip_moves(distance, chips, flip):
     return [
-        (2 * chip + core, 2 * ((chip + distance) % chips) + (core ^ flip))
-        for chip in range(chips)
-        for core in range(2)
+        (2 * chip + core, 2 * (chip ^ distance) + (core ^ flip)) for chip in range(chips) for core in range(2)
     ]
 
 
 def pair_moves(chips):
     return [(device, device ^ 1) for device in range(2 * chips)]
-
-
-def distances(chips):
-    return [1, chips - 1] + list(range(2, chips - 1))
-
-
-def gather_source(chip, distance, chips):
-    if chips & (chips - 1):
-        return lax.rem(chip - distance + chips, chips)
-    return chip ^ distance
-
-
-def gather_moves(distance, chips):
-    if chips & (chips - 1):
-        return chip_moves(distance, chips, 0)
-    return [
-        (2 * chip + core, 2 * (chip ^ distance) + core) for chip in range(chips) for core in range(2)
-    ]
 
 
 def split(x):
@@ -80,7 +60,7 @@
 
 
 def forward_kernel(
-    chips, per, total_lon, modes_hbm, field_hbm, ocean_hbm, give_ref, keep_ref, away_ref,
+    chips, per, total_lon, modes_hbm, field_hbm, ocean_hbm, give_ref, keep_ref, away_ref, first_ref, second_ref,
     modes_ref, field_ref, ocean_ref, small_sem, field_sem,
 ):
     rows, width, channels = field_ref.shape
@@ -101,8 +81,7 @@
     mode_list = []
     for flipped in range(2):
         for d in range(chips):
-            owner = 2 * lax.rem(chip + d, chips)
-            owner = owner + lax.rem(core + flipped + flip_of(d, chips), 2)
+            owner = 2 * (chip ^ d) + lax.rem(core + flipped + flip_of(d), 2)
             mode_list += [modes_ref[owner * per + t] for t in range(per)]
     count = len(mode_list)
     half = count // 2
@@ -128,6 +107,12 @@
     land = ocean_ref[...].astype(F32)
     last_wet = jnp.broadcast_to(land[:, width - 1 : width], (rows, channels))
     first_wet = jnp.broadcast_to(land[:, :1], (rows, channels))
+    even = lax.rem(lax.axis_index("lat"), 2) == 0
+    for out, at_end in ((first_ref, even), (second_ref, ~even)):
+        out[:width, :] = jnp.where(at_end, field_ref[rows - 1], field_ref[0])
+        row = jnp.where(at_end, land[rows - 1 :], land[:1])
+        pieces = [row[:, k : k + channels] for k in range(0, width, channels)]
+        out[width:, :] = fill(pieces, out.shape[0] - width)
     near_is_last = core == 0
     give_ref[half, :, :channels] = jnp.where(near_is_last, last, first)
     give_ref[half, :, channels:] = jnp.where(near_is_last, last_wet, first_wet)
@@ -152,7 +137,7 @@
     mode_list = []
     for flipped in range(2):
         for d in range(chips):
-            source = 2 * gather_source(chip, d, chips) + lax.rem(core + flipped, 2)
+            source = 2 * (chip ^ d) + lax.rem(core + flipped, 2)
             mode_list += [modes_ref[source * per + t] for t in range(per)]
     count = len(mode_list)
     block = width + TAIL
@@ -180,7 +165,7 @@
     for col in range(3):
         left = slice(col * channels, (col + 1) * channels)
         right = slice((3 + col) * channels, (4 + col) * channels)
-        low, mid, up = (conv_ref[row, col] for row in range(3))
+        low, mid, up = (0.5 * conv_ref[row, col] for row in range(3))
         outer = 0.5 * (low + up)
         for k, taps in enumerate((low, outer + 0.5 * mid, outer - 0.5 * mid, up, mid)):
             top, bottom = split(taps)
@@ -190,9 +175,51 @@
             out_ref[k, channels:, right] = jnp.zeros_like(top)
 
 
-def gelu(x):
-    inner = math.sqrt(2.0 / math.pi) * (x + 0.044715 * (x * x * x))
-    return x * (0.5 * (1.0 + jnp.tanh(inner)))
+def twice_gelu(x):
+    slope = math.sqrt(2.0 / math.pi)
+    return x * (1.0 + jnp.tanh(x * (slope + (slope * 0.044715) * (x * x))))
+
+
+def hidden_rows(x, mixed, cut, trig, local, bias, channels):
+    depth = trig.shape[1]
+    x_high, x_low = split(x)
+    m_high, m_low = split(mixed)
+    lower = fill([m_high, m_high, m_low, jnp.concatenate([cut, bias], 0).astype(BF16)], depth)
+    rhs = jnp.concatenate([lower, jnp.zeros((depth, channels), BF16)], 1)
+    rhs = jnp.concatenate([local, rhs], 0)
+    y = dot(jnp.concatenate([x_high, trig], 1), rhs)
+    return twice_gelu(y[:, :channels] + y[:, channels:] + dot(x_low, local[:, :channels]))
+
+
+def bias_rows(bias_ref):
+    high, mid = split(bias_ref[...])
+    high, mid = high.astype(F32), mid.astype(F32)
+    row = lax.broadcasted_iota(jnp.int32, (8, high.shape[1]), 0)
+    rest = jnp.where(row == 2, bias_ref[...] - high - mid, 0.0)
+    return jnp.where(row == 0, high, jnp.where(row == 1, mid, rest))
+
+
+def side_columns(chips, per, rows, got_ref, far_refs):
+    here = lax.axis_index("lon")
+    chip, south = here // 2, lax.rem(here, 2) == 0
+    other = lax.rem(jnp.where(south, chip + chips - 1, chip + 1), chips)
+    far = far_refs[0][per * rows :, :]
+    masks = [d for d in range(chips) if flip_of(d)]
+    for d, ref in zip(masks[1:], far_refs[1:]):
+        far = jnp.where((chip ^ other) == d, ref[per * rows :, :], far)
+    near = got_ref[got_ref.shape[0] - rows :, :]
+    return jnp.where(south, far, near), jnp.where(south, near, far)
+
+
+def edges_kernel(chips, per, got_ref, mixed_ref, *refs):
+    *far_refs, first_ref, second_ref = refs
+    count, rows, _ = mixed_ref.shape
+    left, right = side_columns(chips, per, rows, got_ref, far_refs)
+    even = lax.rem(lax.axis_index("lat"), 2) == 0
+    for out, at_end in ((first_ref, even), (second_ref, ~even)):
+        out[:count, :] = jnp.where(at_end, mixed_ref[:, rows - 1, :], mixed_ref[:, 0, :])
+        sides = [jnp.where(at_end, side[rows - 1 :], side[:1]) for side in (left, right)]
+        out[count:, :] = fill(sides, out.shape[0] - count)
 
 
 def mix_kernel(per, rows, *refs):
@@ -209,26 +236,22 @@
         out_ref[at, :] = y[:, :wide] + y[:, wide:] + dot(low, weights[:, :wide])
 
 
-def hidden_kernel(
-    per, field_ref, got_ref, west_ref, east_ref, mixed_ref, trig_ref, local_ref, bias_ref,
-    hidden_ref, edge_ref,
-):
+def hidden_kernel(chips, per, field_ref, got_ref, mixed_ref, trig_ref, local_ref, bias_ref, *refs):
+    *far_refs, hidden_ref = refs
     rows, width, channels = field_ref.shape
     block = width + TAIL
     count = mixed_ref.shape[0]
     depth = trig_ref.shape[1]
-    empty = jnp.zeros((depth, channels), BF16)
     local = local_ref[...]
-    south = lax.rem(lax.axis_index("lon"), 2) == 0
-    even = lax.rem(lax.axis_index("lat"), 2)
-    near = got_ref[got_ref.shape[0] - rows :, :]
-    left = jnp.where(south, west_ref[per * rows :, :], near)
-    right = jnp.where(south, near, east_ref[per * rows :, :])
+    left, right = side_columns(chips, per, rows, got_ref, far_refs)
     place = lax.broadcasted_iota(jnp.int32, (TAIL, channels), 0)
     first = 6 * count
     lane = lax.broadcasted_iota(jnp.int32, (rows, depth), 1)
     mine = lane == first + lax.broadcasted_iota(jnp.int32, (rows, depth), 0)
-    dry = [jnp.sum(jnp.where(mine, 1.0 - side[:, channels : channels + 1], 0.0), 0, keepdims=True) for side in (left, right)]
+    dry = [
+        jnp.sum(jnp.where(mine, 1.0 - side[:, channels : channels + 1], 0.0), 0, keepdims=True)
+        for side in (left, right)
+    ]
     tail_place = lax.broadcasted_iota(jnp.int32, (TAIL, depth), 0)
     tail_lane = lax.broadcasted_iota(jnp.int32, (TAIL, depth), 1)
     is_land = (tail_lane >= first) & (tail_lane < first + rows)
@@ -236,36 +259,16 @@
     end = jnp.where(is_land & (tail_place == TAIL - 1), dry[0], end)
     end = jnp.where(is_land & (tail_place == 0), dry[1], end)
     trig = jnp.concatenate([trig_ref[:width, :], end.astype(BF16)], 0)
-    b_high, b_mid = split(bias_ref[...])
-    rest = bias_ref[...] - b_high.astype(F32) - b_mid.astype(F32)
-    shape8 = (8, channels)
-    row8 = lax.broadcasted_iota(jnp.int32, shape8, 0)
-    bias8 = jnp.where(
-        row8 == 0, b_high.astype(F32), jnp.where(row8 == 1, b_mid.astype(F32), jnp.where(row8 == 2, rest, 0.0))
-    ).astype(F32)
+    bias = bias_rows(bias_ref)
     select = lax.broadcasted_iota(jnp.int32, (rows, channels), 0)
     for i in range(rows):
         side = jnp.where(
             place == TAIL - 1, left[i : i + 1, :channels], jnp.where(place == 0, right[i : i + 1, :channels], 0.0)
         )
         x = jnp.concatenate([field_ref[i], side], 0)
-        x_high, x_low = split(x)
         mixed = jnp.concatenate([mixed_ref[:, i, :channels], mixed_ref[:, i, channels:]], 0)
-        m_high, m_low = split(mixed)
         cut = jnp.where(select == i, DRY, 0.0)
-        extra = jnp.concatenate([cut, bias8], 0).astype(BF16)
-        spare = depth - first - extra.shape[0]
-        extra = jnp.concatenate([extra, jnp.zeros((spare, channels), BF16)], 0)
-        lower = jnp.concatenate([m_high, m_high, m_low, extra], 0)
-        rhs = jnp.concatenate([local, jnp.concatenate([lower, empty], 1)], 0)
-        lhs = jnp.concatenate([x_high, trig], 1)
-        y = dot(lhs, rhs)
-        y = gelu(y[:, :channels] + y[:, channels:] + dot(x_low, local[:, :channels]))
-        hidden_ref[i * block : (i + 1) * block, :] = y
-        if i == 0:
-            edge_ref[1 - even] = y
-        if i == rows - 1:
-            edge_ref[even] = y
+        hidden_ref[i * block : (i + 1) * block, :] = hidden_rows(x, mixed, cut, trig, local, bias, channels)
 
 
 def columns(t, channels, keep):
@@ -303,7 +306,8 @@
 
 
 def outer_kernel(
-    hidden_ref, first_ref, second_ref, ocean_ref, bias_ref, filter_ref, inner_ref, out_ref, buf_ref, sem_ref
+    bands, hidden_ref, early_first, early_second, late_first, late_second, trig_ref, local_ref, layer_ref,
+    ocean_ref, bias_ref, filter_ref, inner_ref, out_ref, buf_ref, sem_ref,
 ):
     rows, width = ocean_ref.shape
     channels = hidden_ref.shape[1]
@@ -311,13 +315,33 @@
     middle = pltpu.make_async_copy(inner_ref, out_ref.at[pl.ds(1, rows - 2)], sem_ref.at[2])
     middle.start()
     wet = ocean_ref[...].astype(F32).T
+    layer = bias_rows(layer_ref)
+    no_cut = jnp.zeros((rows, channels), F32)
+    place = lax.broadcasted_iota(jnp.int32, (TAIL, channels), 0)
+
+    def neighbour(early, late):
+        count = late.shape[0] - 8
+        left, right = late[count : count + 1, :], late[count + 1 : count + 2, :]
+
+        def tail(lanes):
+            return jnp.where(place == TAIL - 1, left[:, lanes], jnp.where(place == 0, right[:, lanes], 0.0))
+
+        flags = early[width:, :].T
+        pieces = [jnp.broadcast_to(flags[:, k : k + 1], (channels, channels)) for k in range(width // channels)]
+        mask = jnp.concatenate(pieces + [tail(slice(channels, None))], 0)
+        x = jnp.concatenate([early[:width, :], tail(slice(0, channels))], 0)
+        mixed = jnp.concatenate([late[:count, :channels], late[:count, channels:]], 0)
+        return mask * hidden_rows(x, mixed, no_cut, trig_ref[...], local_ref[...], layer, channels)
 
     def at(row):
         return hidden_ref[row * block : (row + 1) * block, :]
 
-    even = lax.rem(lax.axis_index("lat"), 2) == 0
-    above = jnp.where(even, second_ref[0], first_ref[0])
-    below = jnp.where(even, first_ref[0], second_ref[0])
+    band = lax.axis_index("lat")
+    even = lax.rem(band, 2) == 0
+    one = neighbour(early_first, late_first)
+    two = neighbour(early_second, late_second)
+    above = jnp.where(band == 0, 0.0, jnp.where(even, two, one))
+    below = jnp.where(band == bands - 1, 0.0, jnp.where(even, one, two))
     z = product([at(0), at(rows - 1)], filter_ref[4], channels)
     z = z + product([at(1), below], filter_ref[3], channels)
     z = z + product([above, at(rows - 2)], filter_ref[0], channels)
@@ -360,19 +384,21 @@
     per = total_modes // devices
     half = chips * per
     block = width + TAIL
-    steps = distances(chips)
+    steps = list(range(1, chips))
     wide = 2 * channels
     chunks = 2
 
-    give, keep, away = pl.pallas_call(
+    give, keep, away, early_first, early_second = pl.pallas_call(
         functools.partial(forward_kernel, chips, per, total_lon),
         out_shape=(
             struct((half + 1, rows, wide)),
             struct((half, rows, wide)),
             struct((1, rows, wide)),
+            struct((width + 8, channels)),
+            struct((width + 8, channels)),
         ),
         in_specs=[pl.BlockSpec(memory_space=pltpu.MemorySpace.HBM)] * 3,
-        out_specs=(vmem(), vmem(), vmem()),
+        out_specs=(vmem(),) * 5,
         scratch_shapes=[
             pltpu.SMEM((total_modes,), jnp.int32),
             pltpu.VMEM((rows, width, channels), F32),
@@ -415,10 +441,17 @@
     parts = {}
     for d in steps:
         send = summed[d * size : (d + 1) * size]
-        flip = flip_of(d, chips)
-        if flip:
+        if flip_of(d):
             send = jnp.concatenate([send, away])
-        parts[d] = lax.ppermute(send, "lon", chip_moves(d, chips, flip))
+        parts[d] = lax.ppermute(send, "lon", chip_moves(d, chips, flip_of(d)))
+    crossed = [parts[d] for d in steps if flip_of(d)]
+    evens = [(i, i + 1) for i in range(0, bands - 1, 2)]
+    odds = [(i, i + 1) for i in range(1, bands - 1, 2)]
+    if bands % 2 == 0 and bands > 2:
+        odds.append((0, bands - 1))
+    evens, odds = ([(a, b) for a, b in moves] + [(b, a) for a, b in moves] for moves in (evens, odds))
+    early_first = lax.ppermute(early_first, "lat", evens)
+    early_second = lax.ppermute(early_second, "lat", odds)
 
     own_mixed = pl.pallas_call(
         functools.partial(mix_kernel, per, rows),
@@ -429,25 +462,36 @@
         name="mix",
     )(summed, *[parts[d] for d in steps], mix)
     gathered = [own_mixed]
-    for d in range(1, chips):
-        gathered.append(lax.ppermute(own_mixed, "lon", gather_moves(d, chips)))
+    for d in steps:
+        gathered.append(lax.ppermute(own_mixed, "lon", chip_moves(d, chips, 0)))
     gathered = jnp.concatenate(gathered)
     other = lax.ppermute(gathered, "lon", pair_moves(chips))
     mixed = jnp.concatenate([gathered, other]).reshape(total_modes, rows, wide)
 
-    hidden, edge = pl.pallas_call(
-        functools.partial(hidden_kernel, per),
-        out_shape=(struct((rows * block, channels)), struct((2, block, channels))),
-        in_specs=[vmem()] * 8,
+    late = struct((total_modes + 8, wide))
+    late_first, late_second = pl.pallas_call(
+        functools.partial(edges_kernel, chips, per),
+        out_shape=(late, late),
+        in_specs=[vmem()] * (2 + len(crossed)),
         out_specs=(vmem(),) * 2,
+        compiler_params=params(8),
+        name="edges",
+    )(got, mixed, *crossed)
+    late_first = lax.ppermute(late_first, "lat", evens)
+    late_second = lax.ppermute(late_second, "lat", odds)
+    layer = layer_bias.reshape(1, channels)
+    hidden = pl.pallas_call(
+        functools.partial(hidden_kernel, chips, per),
+        out_shape=struct((rows * block, channels)),
+        in_specs=[vmem()] * (6 + len(crossed)),
+        out_specs=vmem(),
         compiler_params=params(24),
+        cost_estimate=pl.CostEstimate(
+            flops=6 * 256 * rows * width * channels, transcendentals=field.size, bytes_accessed=4 * field.size
+        ),
         name="hidden",
-    )(field, got, parts[1], parts[chips - 1], mixed, trig, local, layer_bias.reshape(1, channels))
-
-    evens = [(i, i + 1) for i in range(0, bands - 1, 2)]
-    odds = [(i, i + 1) for i in range(1, bands - 1, 2)]
-    first = lax.ppermute(edge[:1], "lat", evens + [(b, a) for a, b in evens])
-    second = lax.ppermute(edge[1:], "lat", odds + [(b, a) for a, b in odds])
+    )(field, got, mixed, trig, local, layer, *crossed)
+
     bias = conv_bias.reshape(1, channels)
     firsts = list(range(1, rows - 1, 2))
     groups = [firsts[k : k + 2] for k in range(0, len(firsts), 2)]
@@ -464,9 +508,9 @@
         name="inner",
     )(hidden, ocean, bias, filters)
     return pl.pallas_call(
-        outer_kernel,
+        functools.partial(outer_kernel, bands),
         out_shape=struct((rows, width, channels)),
-        in_specs=[vmem()] * 7,
+        in_specs=[vmem()] * 12,
         out_specs=pl.BlockSpec(memory_space=pl.ANY),
         scratch_shapes=[
             pltpu.VMEM((2, width, channels), F32),
@@ -474,7 +518,9 @@
         ],
         compiler_params=params(24),
         name="outer",
-    )(hidden, first, second, ocean, bias, filters, inner)
+    )(
+        hidden, early_first, early_second, late_first, late_second, trig, local, layer, ocean, bias, filters, inner
+    )
 
 
 def solution(mesh):

time: 38.2 us -> 32.8 us (0.86)
  waiting for transfers between devices: 12.2 us -> 6.35 us
    ppermute x8 -> x10, waiting for transfers between devices: 9.89 us -> 4.04 us  [the longest x3 4.03 us: per_device(): gathered.append(lax.ppermute(own_mixed, 'lon', chip_moves(d, chips, 0)))]
    pallas_call x2 -> x3, Pallas kernels: 2.89 us -> 3.22 us  [the longest x1 1.78 us: per_device(): pl.pallas_call(functools.partial(outer_kernel, bands), out_shape=struct((...]
    ppermute x8 -> x10, starting transfers between devices: 15.1 us -> 15.2 us  [the longest x3 5.41 us: per_device(): parts[d] = lax.ppermute(send, 'lon', chip_moves(d, chips, flip_of(d)))]
  transfers between devices with their start and end apart: 10 -> 12, of which waited for: 7 -> 4; matrix products, arithmetic and copies ran while one was open for 0% -> 0% of each run, Pallas kernels for 12% -> 20%
where the time goes in v3:
time: 32.8 us; the launch traced here: 32.7 us
  starting transfers between devices  15.8 us (48%)
  Pallas kernels  10.2 us (31%)
  waiting for transfers between devices  6.35 us (19%)
    ppermute x3, starting transfers between devices, per_device(): parts[d] = lax.ppermute(send, 'lon', chip_moves(d, chips, flip_of(d)))  5.41 us
    ppermute x3, starting transfers between devices, per_device(): gathered.append(lax.ppermute(own_mixed, 'lon', chip_moves(d, chips, 0)))  4.39 us
    ppermute x3, waiting for transfers between devices, per_device(): gathered.append(lax.ppermute(own_mixed, 'lon', chip_moves(d, chips, 0)))  4.03 us
    pallas_call x1, Pallas kernels, per_device(): pl.pallas_call(functools.partial(inner_kernel, groups), out_shape=struct(...  3.64 us
    pallas_call x1, Pallas kernels, per_device(): pl.pallas_call(functools.partial(forward_kernel, chips, per, total_lon),...  2.06 us
    pallas_call x1, Pallas kernels, per_device(): pl.pallas_call(functools.partial(outer_kernel, bands), out_shape=struct((...  1.78 us
    ppermute x1, starting transfers between devices, per_device(): early_first = lax.ppermute(early_first, 'lat', evens)  1.6 us
    ppermute x1, starting transfers between devices, per_device(): late_first = lax.ppermute(late_first, 'lat', evens)  1.56 us
  transfers between devices with their start and end apart: 12, of which 4 were waited for; matrix products, arithmetic and copies ran while one was open for 0% of the time, Pallas kernels for 20%

profile of v3, /device:TPU:0, one launch (start us, length us, event | category | flops | bytes accessed | tf_op | source)
XLA Modules:
  0.0 32.7 jit_solution(1755775151929535042)
XLA Ops:
  0.0 0.0 copy-start.1
  0.0 2.1 %forward.1 = (f32[9,16,256]{2,1,0:T(8,128)S(1)}, f32[8,16,256]{2,1,0:T(8,128)S(1)}, f32[1,16,256]{2,1,0:T(8,128)S(1)}, f32[264,128]{1,0:T(8,128)S(1)}, f32[264,128]{1,0:T(8,128)S(1)}) custom-call(s32[16]{0:T(128)} %modes_ref.1, f32[16,256,128]{2,1,0:T(8,128)} %field_ref.1, s32[16,256]{1,0:T(8,128)} %ocean_ref.5), custom_call_target="tpu_custom_call" | custom-call | tf_op jit(solution)/shard_map/forward/pallas_call | solution.py:391
  2.1 0.0 copy-start.2
  2.1 0.0 copy-start.3
  2.1 0.0 copy-start.4
  2.1 0.0 copy-start.5
  2.1 0.6 %collective-permute-start = (f32[144,256]{1,0:T(8,128)S(1)}, f32[144,256]{1,0:T(8,128)S(1)}, u32[]{:S(2)}, u32[]{:S(2)}) collective-permute-start(f32[144,256]{1,0:T(8,128)S(1)} %bitcast.14), channel_id=1, source_target_pairs={{0,1},{1,0},{2,3},{3,2},{4,5},{5,4},{6,7},{7,6},{8,9},{9,8},{10,11... | collective-permute-start | bytes 442376 | tf_op jit(solution)/shard_map/ppermute | solution.py:438
  2.7 1.0 %collective-permute-done.got_ref = f32[144,256]{1,0:T(8,128)S(1)} collective-permute-done((f32[144,256]{1,0:T(8,128)S(1)}, f32[144,256]{1,0:T(8,128)S(1)}, u32[]{:S(2)}, u32[]{:S(2)}) %collective-permute-start) | collective-permute-done | bytes 147488 | tf_op jit(solution)/shard_map/ppermute | solution.py:438
  3.7 4.8 %collective-permute-start.3 = (f32[48,256]{1,0:T(8,128)S(1)}, f32[48,256]{1,0:T(8,128)S(1)}, u32[]{:S(2)}, u32[]{:S(2)}) collective-permute-start(f32[48,256]{1,0:T(8,128)S(1)} %get-tuple-element.28), channel_id=1, source_target_pairs={{0,7},{1,6},{2,5},{3,4},{4,3},{5,2},{6,1},{7,0},{8,15},{9,14},{10,... | collective-permute-start | bytes 147464 | tf_op jit(solution)/shard_map/ppermute | solution.py:446
  8.5 0.0 collective-permute-start.1
  8.5 0.6 %collective-permute-start.2 = (f32[32,256]{1,0:T(8,128)S(1)}, f32[32,256]{1,0:T(8,128)S(1)}, u32[]{:S(2)}, u32[]{:S(2)}) collective-permute-start(f32[32,256]{1,0:T(8,128)S(1)} %get-tuple-element.26), channel_id=1, source_target_pairs={{0,4},{1,5},{2,6},{3,7},{4,0},{5,1},{6,2},{7,3},{8,12},{9,13},{10,... | collective-permute-start | bytes 98312 | tf_op jit(solution)/shard_map/ppermute | solution.py:446
  9.1 1.6 %collective-permute-start.8 = (f32[264,128]{1,0:T(8,128)S(1)}, f32[264,128]{1,0:T(8,128)S(1)}, u32[]{:S(2)}, u32[]{:S(2)}) collective-permute-start(f32[264,128]{1,0:T(8,128)S(1)} %get-tuple-element.21), channel_id=1, source_target_pairs={{0,8},{16,24},{8,0},{24,16},{1,9},{17,25},{9,1},{25,17},{2,10},{18... | collective-permute-start | bytes 405512 | tf_op jit(solution)/shard_map/ppermute | solution.py:453
  10.8 0.0 copy-start
  10.8 0.0 copy-start.6
  10.8 1.5 %collective-permute-start.9 = (f32[264,128]{1,0:T(8,128)S(1)}, f32[264,128]{1,0:T(8,128)S(1)}, u32[]{:S(2)}, u32[]{:S(2)}) collective-permute-start(f32[264,128]{1,0:T(8,128)S(1)} %get-tuple-element.22), channel_id=1, source_target_pairs={{8,16},{0,24},{16,8},{24,0},{9,17},{1,25},{17,9},{25,1},{10,18},{2... | collective-permute-start | bytes 405512 | tf_op jit(solution)/shard_map/ppermute | solution.py:454
  12.2 0.0 copy-done.1
  12.2 0.3 filters.1.filter_ref
  12.6 0.0 copy-done.2
  12.6 0.0 copy-done.3
  12.6 0.0 copy-done.4
  12.6 0.0 copy-done.5
  12.6 0.8 %prepare.1 = (bf16[272,128]{1,0:T(8,128)(2,1)S(1)}, bf16[128,256]{1,0:T(8,128)(2,1)S(1)}, bf16[512,512]{1,0:T(8,128)(2,1)S(1)}) custom-call(s32[16]{0:T(128)S(1)} %copy-done.5, f32[128,128]{1,0:T(8,128)S(1)} %copy-done.4, f32[2,2,128,128]{3,2,1,0:T(8,128)S(1)} %copy-done.2, s32[16,256]{1,0:T(8,128)S(1)} %copy-done.3), custom_call_target="tpu_custom_call" | custom-call | tf_op jit(solution)/shard_map/prepare/pallas_call | solution.py:417
  13.4 0.0 collective-permute-done.2.refs_2_
  13.4 0.0 collective-permute-done.3.refs_3_.refs_1_
  13.4 0.0 collective-permute-done.1.refs_1_.refs_0_
  13.4 0.2 mix.1
  13.6 3.6 %collective-permute-start.6 = (f32[32,256]{1,0:T(8,128)S(1)}, f32[32,256]{1,0:T(8,128)S(1)}, u32[]{:S(2)}, u32[]{:S(2)}) collective-permute-start(f32[32,256]{1,0:T(8,128)S(1)} %mix.1), channel_id=1, source_target_pairs={{0,6},{1,7},{2,4},{3,5},{4,2},{5,3},{6,0},{7,1},{8,14},{9,15},{10,... | collective-permute-start | bytes 98312 | tf_op jit(solution)/shard_map/ppermute | solution.py:466
  17.2 0.0 collective-permute-start.5
  17.3 0.8 %collective-permute-start.4 = (f32[32,256]{1,0:T(8,128)S(1)}, f32[32,256]{1,0:T(8,128)S(1)}, u32[]{:S(2)}, u32[]{:S(2)}) collective-permute-start(f32[32,256]{1,0:T(8,128)S(1)} %mix.1), channel_id=1, source_target_pairs={{0,2},{1,3},{2,0},{3,1},{4,6},{5,7},{6,4},{7,5},{8,10},{9,11},{10,... | collective-permute-start | bytes 98312 | tf_op jit(solution)/shard_map/ppermute | solution.py:466
  18.0 1.5 %collective-permute-done.6 = f32[32,256]{1,0:T(8,128)S(1)} collective-permute-done((f32[32,256]{1,0:T(8,128)S(1)}, f32[32,256]{1,0:T(8,128)S(1)}, u32[]{:S(2)}, u32[]{:S(2)}) %collective-permute-start.6) | collective-permute-done | bytes 32800 | tf_op jit(solution)/shard_map/ppermute | solution.py:466
  19.6 2.5 %collective-permute-done.5 = f32[32,256]{1,0:T(8,128)S(1)} collective-permute-done((f32[32,256]{1,0:T(8,128)S(1)}, f32[32,256]{1,0:T(8,128)S(1)}, u32[]{:S(2)}, u32[]{:S(2)}) %collective-permute-start.5) | collective-permute-done | bytes 32800 | tf_op jit(solution)/shard_map/ppermute | solution.py:466
  22.1 0.0 collective-permute-done.4
  22.1 0.1 collective-permute-start.7
  22.2 1.3 %collective-permute-done.7 = f32[128,256]{1,0:T(8,128)S(1)} collective-permute-done((f32[128,256]{1,0:T(8,128)S(1)}, f32[128,256]{1,0:T(8,128)S(1)}, u32[]{:S(2)}, u32[]{:S(2)}) %collective-permute-start.7) | collective-permute-done | bytes 131104 | tf_op jit(solution)/shard_map/ppermute | solution.py:468
  23.6 1.6 %collective-permute-start.10 = (f32[24,256]{1,0:T(8,128)S(1)}, f32[24,256]{1,0:T(8,128)S(1)}, u32[]{:S(2)}, u32[]{:S(2)}) collective-permute-start(f32[24,256]{1,0:T(8,128)S(1)} %get-tuple-element.23), channel_id=1, source_target_pairs={{0,8},{16,24},{8,0},{24,16},{1,9},{17,25},{9,1},{25,17},{2,10},{18... | collective-permute-start | bytes 73736 | tf_op jit(solution)/shard_map/ppermute | solution.py:480
  25.1 0.7 %collective-permute-start.11 = (f32[24,256]{1,0:T(8,128)S(1)}, f32[24,256]{1,0:T(8,128)S(1)}, u32[]{:S(2)}, u32[]{:S(2)}) collective-permute-start(f32[24,256]{1,0:T(8,128)S(1)} %get-tuple-element.24), channel_id=1, source_target_pairs={{8,16},{0,24},{16,8},{24,0},{9,17},{1,25},{17,9},{25,1},{10,18},{2... | collective-permute-start | bytes 73736 | tf_op jit(solution)/shard_map/ppermute | solution.py:481
  25.8 0.0 copy-done
  25.8 0.0 copy-done.6
  25.8 0.0 copy-start.7
  25.8 1.4 %hidden.1.hidden_ref = f32[4352,128]{1,0:T(8,128)S(1)} custom-call(f32[16,256,128]{2,1,0:T(8,128)S(1)} %copy-done, f32[144,256]{1,0:T(8,128)S(1)} %collective-permute-done.got_ref, f32[16,16,256]{2,1,0:T(8,128)S(1)} %bitcast.8, bf16[272,128]{1,0:T(8,128)(2,1)S(1)} %get-tuple-element.19.trig_ref, bf16[128,256]{1,0:T(8,128)(2,1)S(1)} %get-tuple-element.20.local_ref, ...), custom_call_target="tpu_custom_call" | custom-call | flops 805306368 | bytes 2097152 | tf_op jit(solution)/shard_map/hidden/pallas_call | solution.py:483
  27.2 0.0 copy-done.7
  27.2 3.6 %inner.1.inner_ref = f32[14,256,128]{2,1,0:T(8,128)S(1)} custom-call(f32[4352,128]{1,0:T(8,128)S(1)} %hidden.1.hidden_ref, s32[16,256]{1,0:T(8,128)S(1)} %copy-done.3, f32[1,128]{1,0:T(1,128)S(1)} %bitcast.12, bf16[5,256,768]{2,1,0:T(8,128)(2,1)S(1)} %filters.1.filter_ref), custom_call_target="tpu_custom_call" | custom-call | flops 3221225472 | bytes 2097152 | tf_op jit(solution)/shard_map/inner/pallas_call | solution.py:501
  30.9 0.0 collective-permute-done.8.early_first
  30.9 0.0 collective-permute-done.9.early_second
  30.9 0.0 collective-permute-done.10.late_first
  30.9 0.0 collective-permute-done.11.late_second
  30.9 1.8 %outer.1 = f32[16,256,128]{2,1,0:T(8,128)} custom-call(f32[4352,128]{1,0:T(8,128)S(1)} %hidden.1.hidden_ref, f32[264,128]{1,0:T(8,128)S(1)} %collective-permute-done.8.early_first, f32[264,128]{1,0:T(8,128)S(1)} %collective-permute-done.9.early_second, f32[24,256]{1,0:T(8,128)S(1)} %collective-permute-done.10.late_first, ...), custom_call_target="tpu_custom_call" | custom-call | tf_op jit(solution)/shard_map/outer/pallas_call | solution.py:510
  (10 shorter events, 0.1 us)
Async XLA Ops:
  0.0 12.2 %copy-start.1 = (f32[3,3,128,128]{3,2,1,0:T(8,128)S(1)}, f32[3,3,128,128]{3,2,1,0:T(8,128)}, u32[]{:S(2)}) copy-start(f32[3,3,128,128]{3,2,1,0:T(8,128)} %conv_ref.1) | copy-start | bytes 1769476
  2.1 10.5 %copy-start.2 = (f32[2,2,128,128]{3,2,1,0:T(8,128)S(1)}, f32[2,2,128,128]{3,2,1,0:T(8,128)}, u32[]{:S(2)}) copy-start(f32[2,2,128,128]{3,2,1,0:T(8,128)} %spectral_ref.1) | copy-start | bytes 786436
  2.1 10.5 %copy-start.3 = (s32[16,256]{1,0:T(8,128)S(1)}, s32[16,256]{1,0:T(8,128)}, u32[]{:S(2)}) copy-start(s32[16,256]{1,0:T(8,128)} %ocean_ref.5) | copy-start | bytes 49156
  2.1 10.5 %copy-start.4 = (f32[128,128]{1,0:T(8,128)S(1)}, f32[128,128]{1,0:T(8,128)}, u32[]{:S(2)}) copy-start(f32[128,128]{1,0:T(8,128)} %local_ref.1) | copy-start | bytes 196612
  2.1 10.5 %copy-start.5 = (s32[16]{0:T(128)S(1)}, s32[16]{0:T(128)}, u32[]{:S(2)}) copy-start(s32[16]{0:T(128)} %modes_ref.1) | copy-start | bytes 196
  2.1 1.6 %collective-permute-start = (f32[144,256]{1,0:T(8,128)S(1)}, f32[144,256]{1,0:T(8,128)S(1)}, u32[]{:S(2)}, u32[]{:S(2)}) collective-permute-start(f32[144,256]{1,0:T(8,128)S(1)} %bitcast.14), channel_id=1, source_target_pairs={{0,1},{1,0},{2,3},{3,2},{4,5},{5,4},{6,7},{7,6},{8,9},{9,8},{10,11... | collective-permute-start | bytes 442376 | tf_op jit(solution)/shard_map/ppermute | solution.py:438
  3.7 9.7 %collective-permute-start.3 = (f32[48,256]{1,0:T(8,128)S(1)}, f32[48,256]{1,0:T(8,128)S(1)}, u32[]{:S(2)}, u32[]{:S(2)}) collective-permute-start(f32[48,256]{1,0:T(8,128)S(1)} %get-tuple-element.28), channel_id=1, source_target_pairs={{0,7},{1,6},{2,5},{3,4},{4,3},{5,2},{6,1},{7,0},{8,15},{9,14},{10,... | collective-permute-start | bytes 147464 | tf_op jit(solution)/shard_map/ppermute | solution.py:446
  8.5 4.9 %collective-permute-start.1 = (f32[48,256]{1,0:T(8,128)S(1)}, f32[48,256]{1,0:T(8,128)S(1)}, u32[]{:S(2)}, u32[]{:S(2)}) collective-permute-start(f32[48,256]{1,0:T(8,128)S(1)} %get-tuple-element.29), channel_id=1, source_target_pairs={{0,3},{1,2},{2,1},{3,0},{4,7},{5,6},{6,5},{7,4},{8,11},{9,10},{10,... | collective-permute-start | bytes 147464 | tf_op jit(solution)/shard_map/ppermute | solution.py:446
  8.5 4.9 %collective-permute-start.2 = (f32[32,256]{1,0:T(8,128)S(1)}, f32[32,256]{1,0:T(8,128)S(1)}, u32[]{:S(2)}, u32[]{:S(2)}) collective-permute-start(f32[32,256]{1,0:T(8,128)S(1)} %get-tuple-element.26), channel_id=1, source_target_pairs={{0,4},{1,5},{2,6},{3,7},{4,0},{5,1},{6,2},{7,3},{8,12},{9,13},{10,... | collective-permute-start | bytes 98312 | tf_op jit(solution)/shard_map/ppermute | solution.py:446
  9.1 21.7 %collective-permute-start.8 = (f32[264,128]{1,0:T(8,128)S(1)}, f32[264,128]{1,0:T(8,128)S(1)}, u32[]{:S(2)}, u32[]{:S(2)}) collective-permute-start(f32[264,128]{1,0:T(8,128)S(1)} %get-tuple-element.21), channel_id=1, source_target_pairs={{0,8},{16,24},{8,0},{24,16},{1,9},{17,25},{9,1},{25,17},{2,10},{18... | collective-permute-start | bytes 405512 | tf_op jit(solution)/shard_map/ppermute | solution.py:453
  10.8 15.1 %copy-start = (f32[16,256,128]{2,1,0:T(8,128)S(1)}, f32[16,256,128]{2,1,0:T(8,128)}, u32[]{:S(2)}) copy-start(f32[16,256,128]{2,1,0:T(8,128)} %field_ref.1) | copy-start | bytes 6291460
  10.8 15.1 %copy-start.6 = (f32[128]{0:T(128)S(1)}, f32[128]{0:T(128)}, u32[]{:S(2)}) copy-start(f32[128]{0:T(128)} %param.13) | copy-start | bytes 1540
  10.8 20.1 %collective-permute-start.9 = (f32[264,128]{1,0:T(8,128)S(1)}, f32[264,128]{1,0:T(8,128)S(1)}, u32[]{:S(2)}, u32[]{:S(2)}) collective-permute-start(f32[264,128]{1,0:T(8,128)S(1)} %get-tuple-element.22), channel_id=1, source_target_pairs={{8,16},{0,24},{16,8},{24,0},{9,17},{1,25},{17,9},{25,1},{10,18},{2... | collective-permute-start | bytes 405512 | tf_op jit(solution)/shard_map/ppermute | solution.py:454
  13.6 5.9 %collective-permute-start.6 = (f32[32,256]{1,0:T(8,128)S(1)}, f32[32,256]{1,0:T(8,128)S(1)}, u32[]{:S(2)}, u32[]{:S(2)}) collective-permute-start(f32[32,256]{1,0:T(8,128)S(1)} %mix.1), channel_id=1, source_target_pairs={{0,6},{1,7},{2,4},{3,5},{4,2},{5,3},{6,0},{7,1},{8,14},{9,15},{10,... | collective-permute-start | bytes 98312 | tf_op jit(solution)/shard_map/ppermute | solution.py:466
  17.2 4.8 %collective-permute-start.5 = (f32[32,256]{1,0:T(8,128)S(1)}, f32[32,256]{1,0:T(8,128)S(1)}, u32[]{:S(2)}, u32[]{:S(2)}) collective-permute-start(f32[32,256]{1,0:T(8,128)S(1)} %mix.1), channel_id=1, source_target_pairs={{0,4},{1,5},{2,6},{3,7},{4,0},{5,1},{6,2},{7,3},{8,12},{9,13},{10,... | collective-permute-start | bytes 98312 | tf_op jit(solution)/shard_map/ppermute | solution.py:466
  17.3 4.8 %collective-permute-start.4 = (f32[32,256]{1,0:T(8,128)S(1)}, f32[32,256]{1,0:T(8,128)S(1)}, u32[]{:S(2)}, u32[]{:S(2)}) collective-permute-start(f32[32,256]{1,0:T(8,128)S(1)} %mix.1), channel_id=1, source_target_pairs={{0,2},{1,3},{2,0},{3,1},{4,6},{5,7},{6,4},{7,5},{8,10},{9,11},{10,... | collective-permute-start | bytes 98312 | tf_op jit(solution)/shard_map/ppermute | solution.py:466
  22.1 1.4 %collective-permute-start.7 = (f32[128,256]{1,0:T(8,128)S(1)}, f32[128,256]{1,0:T(8,128)S(1)}, u32[]{:S(2)}, u32[]{:S(2)}) collective-permute-start(f32[128,256]{1,0:T(8,128)S(1)} %pad_maximum_fusion), channel_id=1, source_target_pairs={{0,1},{1,0},{2,3},{3,2},{4,5},{5,4},{6,7},{7,6},{8,9},{9,8},{10,11... | collective-permute-start | bytes 393224 | tf_op jit(solution)/shard_map/ppermute | solution.py:468
  23.6 7.3 %collective-permute-start.10 = (f32[24,256]{1,0:T(8,128)S(1)}, f32[24,256]{1,0:T(8,128)S(1)}, u32[]{:S(2)}, u32[]{:S(2)}) collective-permute-start(f32[24,256]{1,0:T(8,128)S(1)} %get-tuple-element.23), channel_id=1, source_target_pairs={{0,8},{16,24},{8,0},{24,16},{1,9},{17,25},{9,1},{25,17},{2,10},{18... | collective-permute-start | bytes 73736 | tf_op jit(solution)/shard_map/ppermute | solution.py:480
  25.1 5.8 %collective-permute-start.11 = (f32[24,256]{1,0:T(8,128)S(1)}, f32[24,256]{1,0:T(8,128)S(1)}, u32[]{:S(2)}, u32[]{:S(2)}) collective-permute-start(f32[24,256]{1,0:T(8,128)S(1)} %get-tuple-element.24), channel_id=1, source_target_pairs={{8,16},{0,24},{16,8},{24,0},{9,17},{1,25},{17,9},{25,1},{10,18},{2... | collective-permute-start | bytes 73736 | tf_op jit(solution)/shard_map/ppermute | solution.py:481
  25.8 1.4 %copy-start.7 = (f32[128]{0:T(128)S(1)}, f32[128]{0:T(128)}, u32[]{:S(2)}) copy-start(f32[128]{0:T(128)} %param.15) | copy-start | bytes 1540

commit v4 on v3

--- a/solution.py
+++ b/solution.py
@@ -9,7 +9,7 @@
 from jax.sharding import PartitionSpec as P
 
 LANES = 128
-TAIL = 16
+TAIL = 8
 MIB = 1 << 20
 DRY = -(2.0**36)
 F32 = jnp.float32
@@ -51,7 +51,10 @@
     ids = jnp.zeros(lon.shape, jnp.int32)
     for index, mode in enumerate(mode_list):
         ids = jnp.where(row == index, mode, ids)
-    product = ids * lon
+    return turns(ids * lon, total_lon)
+
+
+def turns(product, total_lon):
     if total_lon & (total_lon - 1):
         product = lax.rem(product, total_lon)
     else:
@@ -61,7 +64,7 @@
 
 def forward_kernel(
     chips, per, total_lon, modes_hbm, field_hbm, ocean_hbm, give_ref, keep_ref, away_ref, first_ref, second_ref,
-    modes_ref, field_ref, ocean_ref, small_sem, field_sem,
+    high_ref, low_ref,     modes_ref, field_ref, ocean_ref, small_sem, field_sem,
 ):
     rows, width, channels = field_ref.shape
     chunks = field_sem.shape[0]
@@ -93,8 +96,10 @@
     for i in range(rows):
         if i % step == 0:
             copies[i // step].wait()
-        rhs = jnp.concatenate(split(field_ref[i]), 1)
-        product = dot(lhs, rhs)
+        high, low = split(field_ref[i])
+        high_ref[i] = high
+        low_ref[i] = low
+        product = dot(lhs, jnp.concatenate([high, low], 1))
         total = product[: 2 * count] + product[2 * count :]
         total = total[:, :channels] + total[:, channels:]
         keep_ref[:half, i, :channels] = total[:half]
@@ -134,12 +139,14 @@
         mix_ref[t * wide + channels : (t + 1) * wide, :] = low
     here = lax.axis_index("lon")
     chip, core = here // 2, lax.rem(here, 2)
-    mode_list = []
-    for flipped in range(2):
-        for d in range(chips):
-            source = 2 * (chip ^ d) + lax.rem(core + flipped, 2)
-            mode_list += [modes_ref[source * per + t] for t in range(per)]
-    count = len(mode_list)
+    count = modes_ref.shape[1]
+    spot = lax.broadcasted_iota(jnp.int32, (count, count), 0)
+    slot = lax.div(spot, per)
+    flipped, d = lax.div(slot, chips), lax.rem(slot, chips)
+    source = 2 * (chip ^ d) + (core ^ flipped)
+    wanted = source * per + lax.rem(spot, per)
+    hit = wanted == lax.broadcasted_iota(jnp.int32, (count, count), 1)
+    mine = jnp.sum(jnp.where(hit, modes_ref[...].astype(F32), 0.0), 1, keepdims=True).astype(jnp.int32)
     block = width + TAIL
     padded = -(-block // LANES) * LANES
     place = lax.broadcasted_iota(jnp.int32, (count, padded), 1)
@@ -147,7 +154,7 @@
     lon = here * width + place + total_lon
     lon = jnp.where(lon >= total_lon, lon - total_lon, lon)
     lon = jnp.where(lon >= total_lon, lon - total_lon, lon)
-    theta = angles(mode_list, lon, total_lon)
+    theta = turns(mine * lon, total_lon)
     scale = 2.0 / math.sqrt(count)
     table = jnp.concatenate([jnp.cos(theta) * scale, -jnp.sin(theta) * scale], 0)
     high, low = split(table)
@@ -180,15 +187,20 @@
     return x * (1.0 + jnp.tanh(x * (slope + (slope * 0.044715) * (x * x))))
 
 
-def hidden_rows(x, mixed, cut, trig, local, bias, channels):
+def hidden_pair(parts, mixed, cuts, trig, local, bias, channels):
     depth = trig.shape[1]
-    x_high, x_low = split(x)
-    m_high, m_low = split(mixed)
-    lower = fill([m_high, m_high, m_low, jnp.concatenate([cut, bias], 0).astype(BF16)], depth)
-    rhs = jnp.concatenate([lower, jnp.zeros((depth, channels), BF16)], 1)
-    rhs = jnp.concatenate([local, rhs], 0)
-    y = dot(jnp.concatenate([x_high, trig], 1), rhs)
-    return twice_gelu(y[:, :channels] + y[:, channels:] + dot(x_low, local[:, :channels]))
+    top = local[:, :channels]
+    none = jnp.zeros_like(top)
+    both = jnp.concatenate([jnp.concatenate([top, none], 1), jnp.concatenate([none, top], 1)], 0)
+    rest = dot(jnp.concatenate([parts[0][1], parts[1][1]], 1), both)
+    out = []
+    for r in range(2):
+        m_high, m_low = split(mixed[r])
+        lower = fill([m_high, m_high, m_low, jnp.concatenate([cuts[r], bias], 0).astype(BF16)], depth)
+        rhs = jnp.concatenate([lower, jnp.zeros((depth, channels), BF16)], 1)
+        y = dot(jnp.concatenate([parts[r][0], trig], 1), jnp.concatenate([local, rhs], 0))
+        out.append(twice_gelu(y[:, :channels] + y[:, channels:] + rest[:, r * channels : (r + 1) * channels]))
+    return out
 
 
 def bias_rows(bias_ref):
@@ -236,9 +248,9 @@
         out_ref[at, :] = y[:, :wide] + y[:, wide:] + dot(low, weights[:, :wide])
 
 
-def hidden_kernel(chips, per, field_ref, got_ref, mixed_ref, trig_ref, local_ref, bias_ref, *refs):
+def hidden_kernel(chips, per, high_ref, low_ref, got_ref, mixed_ref, trig_ref, local_ref, bias_ref, *refs):
     *far_refs, hidden_ref = refs
-    rows, width, channels = field_ref.shape
+    rows, width, channels = high_ref.shape
     block = width + TAIL
     count = mixed_ref.shape[0]
     depth = trig_ref.shape[1]
@@ -261,14 +273,19 @@
     trig = jnp.concatenate([trig_ref[:width, :], end.astype(BF16)], 0)
     bias = bias_rows(bias_ref)
     select = lax.broadcasted_iota(jnp.int32, (rows, channels), 0)
-    for i in range(rows):
-        side = jnp.where(
-            place == TAIL - 1, left[i : i + 1, :channels], jnp.where(place == 0, right[i : i + 1, :channels], 0.0)
-        )
-        x = jnp.concatenate([field_ref[i], side], 0)
-        mixed = jnp.concatenate([mixed_ref[:, i, :channels], mixed_ref[:, i, channels:]], 0)
-        cut = jnp.where(select == i, DRY, 0.0)
-        hidden_ref[i * block : (i + 1) * block, :] = hidden_rows(x, mixed, cut, trig, local, bias, channels)
+    for i in range(0, rows, 2):
+        parts, mixed, cuts = [], [], []
+        for r in (i, i + 1):
+            side = jnp.where(
+                place == TAIL - 1, left[r : r + 1, :channels], jnp.where(place == 0, right[r : r + 1, :channels], 0.0)
+            )
+            high, low = split(side)
+            parts.append((jnp.concatenate([high_ref[r], high], 0), jnp.concatenate([low_ref[r], low], 0)))
+            mixed.append(jnp.concatenate([mixed_ref[:, r, :channels], mixed_ref[:, r, channels:]], 0))
+            cuts.append(jnp.where(select == r, DRY, 0.0))
+        pair = hidden_pair(parts, mixed, cuts, trig, local, bias, channels)
+        for r in range(2):
+            hidden_ref[(i + r) * block : (i + r + 1) * block, :] = pair[r]
 
 
 def columns(t, channels, keep):
@@ -278,8 +295,7 @@
 
 
 def product(parts, weights, channels):
-    lhs = jnp.concatenate([jnp.concatenate(split(part), 1) for part in parts], 0)
-    y = dot(lhs, weights)
+    y = dot(jnp.concatenate(split(jnp.concatenate(parts, 0)), 1), weights)
     return y[:, : 3 * channels] + y[:, 3 * channels :]
 
 
@@ -310,7 +326,7 @@
     ocean_ref, bias_ref, filter_ref, inner_ref, out_ref, buf_ref, sem_ref,
 ):
     rows, width = ocean_ref.shape
-    channels = hidden_ref.shape[1]
+    channels = local_ref.shape[0]
     block = width + TAIL
     middle = pltpu.make_async_copy(inner_ref, out_ref.at[pl.ds(1, rows - 2)], sem_ref.at[2])
     middle.start()
@@ -331,17 +347,19 @@
         mask = jnp.concatenate(pieces + [tail(slice(channels, None))], 0)
         x = jnp.concatenate([early[:width, :], tail(slice(0, channels))], 0)
         mixed = jnp.concatenate([late[:count, :channels], late[:count, channels:]], 0)
-        return mask * hidden_rows(x, mixed, no_cut, trig_ref[...], local_ref[...], layer, channels)
+        return mask, split(x), mixed
+
+    band = lax.axis_index("lat")
+    even = lax.rem(band, 2) == 0
+    masks, parts, mixed = zip(neighbour(early_first, late_first), neighbour(early_second, late_second))
+    pair = hidden_pair(parts, mixed, (no_cut, no_cut), trig_ref[...], local_ref[...], layer, channels)
+    one, two = (mask * y for mask, y in zip(masks, pair))
+    above = jnp.where(band == 0, 0.0, jnp.where(even, two, one))
+    below = jnp.where(band == bands - 1, 0.0, jnp.where(even, one, two))
 
     def at(row):
         return hidden_ref[row * block : (row + 1) * block, :]
 
-    band = lax.axis_index("lat")
-    even = lax.rem(band, 2) == 0
-    one = neighbour(early_first, late_first)
-    two = neighbour(early_second, late_second)
-    above = jnp.where(band == 0, 0.0, jnp.where(even, two, one))
-    below = jnp.where(band == bands - 1, 0.0, jnp.where(even, one, two))
     z = product([at(0), at(rows - 1)], filter_ref[4], channels)
     z = z + product([at(1), below], filter_ref[3], channels)
     z = z + product([above, at(rows - 2)], filter_ref[0], channels)
@@ -358,10 +376,6 @@
 
 def vmem():
     return pl.BlockSpec(memory_space=pltpu.VMEM)
-
-
-def smem():
-    return pl.BlockSpec(memory_space=pltpu.SMEM)
 
 
 def struct(shape, dtype=F32):
@@ -388,7 +402,7 @@
     wide = 2 * channels
     chunks = 2
 
-    give, keep, away, early_first, early_second = pl.pallas_call(
+    give, keep, away, early_first, early_second, high, low = pl.pallas_call(
         functools.partial(forward_kernel, chips, per, total_lon),
         out_shape=(
             struct((half + 1, rows, wide)),
@@ -396,9 +410,11 @@
             struct((1, rows, wide)),
             struct((width + 8, channels)),
             struct((width + 8, channels)),
+            struct((rows, width, channels), BF16),
+            struct((rows, width, channels), BF16),
         ),
         in_specs=[pl.BlockSpec(memory_space=pltpu.MemorySpace.HBM)] * 3,
-        out_specs=(vmem(),) * 5,
+        out_specs=(vmem(),) * 7,
         scratch_shapes=[
             pltpu.SMEM((total_modes,), jnp.int32),
             pltpu.VMEM((rows, width, channels), F32),
@@ -421,11 +437,11 @@
             struct((channels, 2 * channels), BF16),
             struct((per * wide, 2 * wide), BF16),
         ),
-        in_specs=[smem(), vmem(), vmem(), vmem()],
+        in_specs=[vmem()] * 4,
         out_specs=(vmem(),) * 3,
         compiler_params=params(16),
         name="prepare",
-    )(modes, local_weight, spectral_weight, ocean)
+    )(modes.reshape(1, total_modes), local_weight, spectral_weight, ocean)
     filters = pl.pallas_call(
         filter_kernel,
         out_shape=struct((5, 2 * channels, 6 * channels), BF16),
@@ -483,14 +499,14 @@
     hidden = pl.pallas_call(
         functools.partial(hidden_kernel, chips, per),
         out_shape=struct((rows * block, channels)),
-        in_specs=[vmem()] * (6 + len(crossed)),
+        in_specs=[vmem()] * (7 + len(crossed)),
         out_specs=vmem(),
         compiler_params=params(24),
         cost_estimate=pl.CostEstimate(
             flops=6 * 256 * rows * width * channels, transcendentals=field.size, bytes_accessed=4 * field.size
         ),
         name="hidden",
-    )(field, got, mixed, trig, local, layer, *crossed)
+    )(high, low, got, mixed, trig, local, layer, *crossed)
 
     bias = conv_bias.reshape(1, channels)
     firsts = list(range(1, rows - 1, 2))

time: 32.8 us -> 32.3 us (0.985)
  Pallas kernels: 10.2 us -> 9.4 us
    pallas_call x1, Pallas kernels: 0.78 us -> 0.31 us  [per_device(): pl.pallas_call(functools.partial(prepare_kernel, chips, per, total_lon),...]
    ppermute x3, waiting for transfers between devices: 0.01 us -> 0.41 us  [per_device(): parts[d] = lax.ppermute(send, 'lon', chip_moves(d, chips, flip_of(d)))]
    ppermute x3, waiting for transfers between devices: 4.03 us -> 3.65 us  [per_device(): gathered.append(lax.ppermute(own_mixed, 'lon', chip_moves(d, chips, 0)))]
  transfers between devices with their start and end apart: 12 -> 12, of which waited for: 4 -> 5; matrix products, arithmetic and copies ran while one was open for 0% -> 0% of each run, Pallas kernels for 20% -> 18%
where the time goes in v4:
time: 32.3 us; the launch traced here: 32.1 us
  starting transfers between devices  16 us (50%)
  Pallas kernels  9.4 us (29%)
  waiting for transfers between devices  6.37 us (20%)
    ppermute x3, starting transfers between devices, per_device(): parts[d] = lax.ppermute(send, 'lon', chip_moves(d, chips, flip_of(d)))  5.41 us
    ppermute x3, starting transfers between devices, per_device(): gathered.append(lax.ppermute(own_mixed, 'lon', chip_moves(d, chips, 0)))  4.39 us
    ppermute x3, waiting for transfers between devices, per_device(): gathered.append(lax.ppermute(own_mixed, 'lon', chip_moves(d, chips, 0)))  3.65 us
    pallas_call x1, Pallas kernels, per_device(): pl.pallas_call(functools.partial(inner_kernel, groups), out_shape=struct(...  3.57 us
    pallas_call x1, Pallas kernels, per_device(): pl.pallas_call(functools.partial(forward_kernel, chips, per, total_lon),...  2.07 us
    pallas_call x1, Pallas kernels, per_device(): pl.pallas_call(functools.partial(outer_kernel, bands), out_shape=struct((...  1.71 us
    ppermute x1, starting transfers between devices, per_device(): early_first = lax.ppermute(early_first, 'lat', evens)  1.6 us
    ppermute x1, starting transfers between devices, per_device(): late_first = lax.ppermute(late_first, 'lat', evens)  1.56 us
  transfers between devices with their start and end apart: 12, of which 5 were waited for; matrix products, arithmetic and copies ran while one was open for 0% of the time, Pallas kernels for 18%

profile of v4, /device:TPU:0, one launch (start us, length us, event | category | flops | bytes accessed | tf_op | source)
XLA Modules:
  0.0 32.1 jit_solution(9306709044501125055)
XLA Ops:
  0.0 0.0 copy-start
  0.0 2.1 %forward.1 = (f32[9,16,256]{2,1,0:T(8,128)S(1)}, f32[8,16,256]{2,1,0:T(8,128)S(1)}, f32[1,16,256]{2,1,0:T(8,128)S(1)}, f32[264,128]{1,0:T(8,128)S(1)}, f32[264,1...) custom-call(s32[16]{0:T(128)} %modes_hbm.1, f32[16,256,128]{2,1,0:T(8,128)} %field_hbm.1, ...), custom_call_target="tpu_custom_call" | custom-call | tf_op jit(solution)/shard_map/forward/pallas_call | solution.py:405
  2.1 0.0 copy-start.1
  2.1 0.0 copy-start.2
  2.1 0.0 copy-start.3
  2.1 0.0 copy-start.4
  2.1 0.6 %collective-permute-start = (f32[144,256]{1,0:T(8,128)S(1)}, f32[144,256]{1,0:T(8,128)S(1)}, u32[]{:S(2)}, u32[]{:S(2)}) collective-permute-start(f32[144,256]{1,0:T(8,128)S(1)} %bitcast.16), channel_id=1, source_target_pairs={{0,1},{1,0},{2,3},{3,2},{4,5},{5,4},{6,7},{7,6},{8,9},{9,8},{10,11... | collective-permute-start | bytes 442376 | tf_op jit(solution)/shard_map/ppermute | solution.py:454
  2.7 1.0 %collective-permute-done.got_ref = f32[144,256]{1,0:T(8,128)S(1)} collective-permute-done((f32[144,256]{1,0:T(8,128)S(1)}, f32[144,256]{1,0:T(8,128)S(1)}, u32[]{:S(2)}, u32[]{:S(2)}) %collective-permute-start) | collective-permute-done | bytes 147488 | tf_op jit(solution)/shard_map/ppermute | solution.py:454
  3.8 4.8 %collective-permute-start.3 = (f32[48,256]{1,0:T(8,128)S(1)}, f32[48,256]{1,0:T(8,128)S(1)}, u32[]{:S(2)}, u32[]{:S(2)}) collective-permute-start(f32[48,256]{1,0:T(8,128)S(1)} %get-tuple-element.32), channel_id=1, source_target_pairs={{0,7},{1,6},{2,5},{3,4},{4,3},{5,2},{6,1},{7,0},{8,15},{9,14},{10,... | collective-permute-start | bytes 147464 | tf_op jit(solution)/shard_map/ppermute | solution.py:462
  8.5 0.0 collective-permute-start.1
  8.5 0.6 %collective-permute-start.2 = (f32[32,256]{1,0:T(8,128)S(1)}, f32[32,256]{1,0:T(8,128)S(1)}, u32[]{:S(2)}, u32[]{:S(2)}) collective-permute-start(f32[32,256]{1,0:T(8,128)S(1)} %get-tuple-element.30), channel_id=1, source_target_pairs={{0,4},{1,5},{2,6},{3,7},{4,0},{5,1},{6,2},{7,3},{8,12},{9,13},{10,... | collective-permute-start | bytes 98312 | tf_op jit(solution)/shard_map/ppermute | solution.py:462
  9.2 1.6 %collective-permute-start.8 = (f32[264,128]{1,0:T(8,128)S(1)}, f32[264,128]{1,0:T(8,128)S(1)}, u32[]{:S(2)}, u32[]{:S(2)}) collective-permute-start(f32[264,128]{1,0:T(8,128)S(1)} %get-tuple-element.25), channel_id=1, source_target_pairs={{0,8},{16,24},{8,0},{24,16},{1,9},{17,25},{9,1},{25,17},{2,10},{18... | collective-permute-start | bytes 405512 | tf_op jit(solution)/shard_map/ppermute | solution.py:469
  10.8 0.0 copy-start.5
  10.8 1.5 %collective-permute-start.9 = (f32[264,128]{1,0:T(8,128)S(1)}, f32[264,128]{1,0:T(8,128)S(1)}, u32[]{:S(2)}, u32[]{:S(2)}) collective-permute-start(f32[264,128]{1,0:T(8,128)S(1)} %get-tuple-element.26), channel_id=1, source_target_pairs={{8,16},{0,24},{16,8},{24,0},{9,17},{1,25},{17,9},{25,1},{10,18},{2... | collective-permute-start | bytes 405512 | tf_op jit(solution)/shard_map/ppermute | solution.py:470
  12.3 0.0 copy-done
  12.3 0.3 filters.1.filter_ref
  12.6 0.0 copy-done.1
  12.6 0.0 copy-done.2
  12.6 0.0 copy-done.3
  12.6 0.0 copy-done.4
  12.6 0.3 prepare.1
  12.9 0.4 %collective-permute-done.2.refs_2_ = f32[32,256]{1,0:T(8,128)S(1)} collective-permute-done((f32[32,256]{1,0:T(8,128)S(1)}, f32[32,256]{1,0:T(8,128)S(1)}, u32[]{:S(2)}, u32[]{:S(2)}) %collective-permute-start.2) | collective-permute-done | bytes 32800 | tf_op jit(solution)/shard_map/ppermute | solution.py:462
  13.3 0.0 collective-permute-done.3.refs_3_.refs_1_
  13.3 0.0 collective-permute-done.1.refs_1_.refs_0_
  13.3 0.2 mix.1
  13.6 3.2 %collective-permute-start.6 = (f32[32,256]{1,0:T(8,128)S(1)}, f32[32,256]{1,0:T(8,128)S(1)}, u32[]{:S(2)}, u32[]{:S(2)}) collective-permute-start(f32[32,256]{1,0:T(8,128)S(1)} %mix.1), channel_id=1, source_target_pairs={{0,6},{1,7},{2,4},{3,5},{4,2},{5,3},{6,0},{7,1},{8,14},{9,15},{10,... | collective-permute-start | bytes 98312 | tf_op jit(solution)/shard_map/ppermute | solution.py:482
  16.8 0.2 collective-permute-start.5
  17.0 0.9 %collective-permute-start.4 = (f32[32,256]{1,0:T(8,128)S(1)}, f32[32,256]{1,0:T(8,128)S(1)}, u32[]{:S(2)}, u32[]{:S(2)}) collective-permute-start(f32[32,256]{1,0:T(8,128)S(1)} %mix.1), channel_id=1, source_target_pairs={{0,2},{1,3},{2,0},{3,1},{4,6},{5,7},{6,4},{7,5},{8,10},{9,11},{10,... | collective-permute-start | bytes 98312 | tf_op jit(solution)/shard_map/ppermute | solution.py:482
  18.0 1.5 %collective-permute-done.6 = f32[32,256]{1,0:T(8,128)S(1)} collective-permute-done((f32[32,256]{1,0:T(8,128)S(1)}, f32[32,256]{1,0:T(8,128)S(1)}, u32[]{:S(2)}, u32[]{:S(2)}) %collective-permute-start.6) | collective-permute-done | bytes 32800 | tf_op jit(solution)/shard_map/ppermute | solution.py:482
  19.5 2.1 %collective-permute-done.5 = f32[32,256]{1,0:T(8,128)S(1)} collective-permute-done((f32[32,256]{1,0:T(8,128)S(1)}, f32[32,256]{1,0:T(8,128)S(1)}, u32[]{:S(2)}, u32[]{:S(2)}) %collective-permute-start.5) | collective-permute-done | bytes 32800 | tf_op jit(solution)/shard_map/ppermute | solution.py:482
  21.6 0.0 collective-permute-done.4
  21.6 0.1 collective-permute-start.7
  21.7 1.3 %collective-permute-done.7 = f32[128,256]{1,0:T(8,128)S(1)} collective-permute-done((f32[128,256]{1,0:T(8,128)S(1)}, f32[128,256]{1,0:T(8,128)S(1)}, u32[]{:S(2)}, u32[]{:S(2)}) %collective-permute-start.7) | collective-permute-done | bytes 131104 | tf_op jit(solution)/shard_map/ppermute | solution.py:484
  23.1 1.6 %collective-permute-start.10 = (f32[24,256]{1,0:T(8,128)S(1)}, f32[24,256]{1,0:T(8,128)S(1)}, u32[]{:S(2)}, u32[]{:S(2)}) collective-permute-start(f32[24,256]{1,0:T(8,128)S(1)} %get-tuple-element.27), channel_id=1, source_target_pairs={{0,8},{16,24},{8,0},{24,16},{1,9},{17,25},{9,1},{25,17},{2,10},{18... | collective-permute-start | bytes 73736 | tf_op jit(solution)/shard_map/ppermute | solution.py:496
  24.7 1.0 %collective-permute-start.11 = (f32[24,256]{1,0:T(8,128)S(1)}, f32[24,256]{1,0:T(8,128)S(1)}, u32[]{:S(2)}, u32[]{:S(2)}) collective-permute-start(f32[24,256]{1,0:T(8,128)S(1)} %get-tuple-element.28), channel_id=1, source_target_pairs={{8,16},{0,24},{16,8},{24,0},{9,17},{1,25},{17,9},{25,1},{10,18},{2... | collective-permute-start | bytes 73736 | tf_op jit(solution)/shard_map/ppermute | solution.py:497
  25.6 0.0 copy-done.5
  25.6 0.0 copy-start.6
  25.6 1.2 %hidden.1.hidden_ref = f32[4224,128]{1,0:T(8,128)S(1)} custom-call(bf16[16,256,128]{2,1,0:T(8,128)(2,1)S(1)} %get-tuple-element.17.high_ref, bf16[16,256,128]{2,1,0:T(8,128)(2,1)S(1)} %get-tuple-element.18.low_ref, f32[144,256]{1,0:T(8,128)S(1)} %collective-permute-done.got_ref, f32[16,16,256]{2,1,0:T(8,128)S(1)} %bitcast.9, ...), custom_call_target="tpu_custom_call" | custom-call | flops 805306368 | bytes 2097152 | tf_op jit(solution)/shard_map/hidden/pallas_call | solution.py:499
  26.8 0.0 copy-done.6
  26.8 3.6 %inner.1.inner_ref = f32[14,256,128]{2,1,0:T(8,128)S(1)} custom-call(f32[4224,128]{1,0:T(8,128)S(1)} %hidden.1.hidden_ref, s32[16,256]{1,0:T(8,128)S(1)} %copy-done.2, f32[1,128]{1,0:T(1,128)S(1)} %bitcast.14, bf16[5,256,768]{2,1,0:T(8,128)(2,1)S(1)} %filters.1.filter_ref), custom_call_target="tpu_custom_call" | custom-call | flops 3221225472 | bytes 2097152 | tf_op jit(solution)/shard_map/inner/pallas_call | solution.py:517
  30.4 0.0 collective-permute-done.8.early_first
  30.4 0.0 collective-permute-done.9.early_second
  30.4 0.0 collective-permute-done.10.late_first
  30.4 0.0 collective-permute-done.11.late_second
  30.4 1.7 %outer.1 = f32[16,256,128]{2,1,0:T(8,128)} custom-call(f32[4224,128]{1,0:T(8,128)S(1)} %hidden.1.hidden_ref, f32[264,128]{1,0:T(8,128)S(1)} %collective-permute-done.8.early_first, f32[264,128]{1,0:T(8,128)S(1)} %collective-permute-done.9.early_second, f32[24,256]{1,0:T(8,128)S(1)} %collective-permute-done.10.late_first, ...), custom_call_target="tpu_custom_call" | custom-call | tf_op jit(solution)/shard_map/outer/pallas_call | solution.py:526
  (10 shorter events, 0.1 us)
Async XLA Ops:
  0.0 12.3 %copy-start = (f32[3,3,128,128]{3,2,1,0:T(8,128)S(1)}, f32[3,3,128,128]{3,2,1,0:T(8,128)}, u32[]{:S(2)}) copy-start(f32[3,3,128,128]{3,2,1,0:T(8,128)} %conv_ref.1) | copy-start | bytes 1769476
  2.1 10.5 %copy-start.1 = (f32[2,2,128,128]{3,2,1,0:T(8,128)S(1)}, f32[2,2,128,128]{3,2,1,0:T(8,128)}, u32[]{:S(2)}) copy-start(f32[2,2,128,128]{3,2,1,0:T(8,128)} %spectral_ref.1) | copy-start | bytes 786436
  2.1 10.5 %copy-start.2 = (s32[16,256]{1,0:T(8,128)S(1)}, s32[16,256]{1,0:T(8,128)}, u32[]{:S(2)}) copy-start(s32[16,256]{1,0:T(8,128)} %ocean_ref.5) | copy-start | bytes 49156
  2.1 10.5 %copy-start.3 = (f32[128,128]{1,0:T(8,128)S(1)}, f32[128,128]{1,0:T(8,128)}, u32[]{:S(2)}) copy-start(f32[128,128]{1,0:T(8,128)} %local_ref.1) | copy-start | bytes 196612
  2.1 10.5 %copy-start.4 = (s32[16]{0:T(128)S(1)}, s32[16]{0:T(128)}, u32[]{:S(2)}) copy-start(s32[16]{0:T(128)} %modes_hbm.1) | copy-start | bytes 196
  2.1 1.6 %collective-permute-start = (f32[144,256]{1,0:T(8,128)S(1)}, f32[144,256]{1,0:T(8,128)S(1)}, u32[]{:S(2)}, u32[]{:S(2)}) collective-permute-start(f32[144,256]{1,0:T(8,128)S(1)} %bitcast.16), channel_id=1, source_target_pairs={{0,1},{1,0},{2,3},{3,2},{4,5},{5,4},{6,7},{7,6},{8,9},{9,8},{10,11... | collective-permute-start | bytes 442376 | tf_op jit(solution)/shard_map/ppermute | solution.py:454
  3.8 9.6 %collective-permute-start.3 = (f32[48,256]{1,0:T(8,128)S(1)}, f32[48,256]{1,0:T(8,128)S(1)}, u32[]{:S(2)}, u32[]{:S(2)}) collective-permute-start(f32[48,256]{1,0:T(8,128)S(1)} %get-tuple-element.32), channel_id=1, source_target_pairs={{0,7},{1,6},{2,5},{3,4},{4,3},{5,2},{6,1},{7,0},{8,15},{9,14},{10,... | collective-permute-start | bytes 147464 | tf_op jit(solution)/shard_map/ppermute | solution.py:462
  8.5 4.8 %collective-permute-start.1 = (f32[48,256]{1,0:T(8,128)S(1)}, f32[48,256]{1,0:T(8,128)S(1)}, u32[]{:S(2)}, u32[]{:S(2)}) collective-permute-start(f32[48,256]{1,0:T(8,128)S(1)} %get-tuple-element.33), channel_id=1, source_target_pairs={{0,3},{1,2},{2,1},{3,0},{4,7},{5,6},{6,5},{7,4},{8,11},{9,10},{10,... | collective-permute-start | bytes 147464 | tf_op jit(solution)/shard_map/ppermute | solution.py:462
  8.5 4.8 %collective-permute-start.2 = (f32[32,256]{1,0:T(8,128)S(1)}, f32[32,256]{1,0:T(8,128)S(1)}, u32[]{:S(2)}, u32[]{:S(2)}) collective-permute-start(f32[32,256]{1,0:T(8,128)S(1)} %get-tuple-element.30), channel_id=1, source_target_pairs={{0,4},{1,5},{2,6},{3,7},{4,0},{5,1},{6,2},{7,3},{8,12},{9,13},{10,... | collective-permute-start | bytes 98312 | tf_op jit(solution)/shard_map/ppermute | solution.py:462
  9.2 21.2 %collective-permute-start.8 = (f32[264,128]{1,0:T(8,128)S(1)}, f32[264,128]{1,0:T(8,128)S(1)}, u32[]{:S(2)}, u32[]{:S(2)}) collective-permute-start(f32[264,128]{1,0:T(8,128)S(1)} %get-tuple-element.25), channel_id=1, source_target_pairs={{0,8},{16,24},{8,0},{24,16},{1,9},{17,25},{9,1},{25,17},{2,10},{18... | collective-permute-start | bytes 405512 | tf_op jit(solution)/shard_map/ppermute | solution.py:469
  10.8 14.9 %copy-start.5 = (f32[128]{0:T(128)S(1)}, f32[128]{0:T(128)}, u32[]{:S(2)}) copy-start(f32[128]{0:T(128)} %param.13) | copy-start | bytes 1540
  10.8 19.6 %collective-permute-start.9 = (f32[264,128]{1,0:T(8,128)S(1)}, f32[264,128]{1,0:T(8,128)S(1)}, u32[]{:S(2)}, u32[]{:S(2)}) collective-permute-start(f32[264,128]{1,0:T(8,128)S(1)} %get-tuple-element.26), channel_id=1, source_target_pairs={{8,16},{0,24},{16,8},{24,0},{9,17},{1,25},{17,9},{25,1},{10,18},{2... | collective-permute-start | bytes 405512 | tf_op jit(solution)/shard_map/ppermute | solution.py:470
  13.6 5.9 %collective-permute-start.6 = (f32[32,256]{1,0:T(8,128)S(1)}, f32[32,256]{1,0:T(8,128)S(1)}, u32[]{:S(2)}, u32[]{:S(2)}) collective-permute-start(f32[32,256]{1,0:T(8,128)S(1)} %mix.1), channel_id=1, source_target_pairs={{0,6},{1,7},{2,4},{3,5},{4,2},{5,3},{6,0},{7,1},{8,14},{9,15},{10,... | collective-permute-start | bytes 98312 | tf_op jit(solution)/shard_map/ppermute | solution.py:482
  16.8 4.8 %collective-permute-start.5 = (f32[32,256]{1,0:T(8,128)S(1)}, f32[32,256]{1,0:T(8,128)S(1)}, u32[]{:S(2)}, u32[]{:S(2)}) collective-permute-start(f32[32,256]{1,0:T(8,128)S(1)} %mix.1), channel_id=1, source_target_pairs={{0,4},{1,5},{2,6},{3,7},{4,0},{5,1},{6,2},{7,3},{8,12},{9,13},{10,... | collective-permute-start | bytes 98312 | tf_op jit(solution)/shard_map/ppermute | solution.py:482
  17.0 4.6 %collective-permute-start.4 = (f32[32,256]{1,0:T(8,128)S(1)}, f32[32,256]{1,0:T(8,128)S(1)}, u32[]{:S(2)}, u32[]{:S(2)}) collective-permute-start(f32[32,256]{1,0:T(8,128)S(1)} %mix.1), channel_id=1, source_target_pairs={{0,2},{1,3},{2,0},{3,1},{4,6},{5,7},{6,4},{7,5},{8,10},{9,11},{10,... | collective-permute-start | bytes 98312 | tf_op jit(solution)/shard_map/ppermute | solution.py:482
  21.6 1.4 %collective-permute-start.7 = (f32[128,256]{1,0:T(8,128)S(1)}, f32[128,256]{1,0:T(8,128)S(1)}, u32[]{:S(2)}, u32[]{:S(2)}) collective-permute-start(f32[128,256]{1,0:T(8,128)S(1)} %pad_maximum_fusion), channel_id=1, source_target_pairs={{0,1},{1,0},{2,3},{3,2},{4,5},{5,4},{6,7},{7,6},{8,9},{9,8},{10,11... | collective-permute-start | bytes 393224 | tf_op jit(solution)/shard_map/ppermute | solution.py:484
  23.1 7.3 %collective-permute-start.10 = (f32[24,256]{1,0:T(8,128)S(1)}, f32[24,256]{1,0:T(8,128)S(1)}, u32[]{:S(2)}, u32[]{:S(2)}) collective-permute-start(f32[24,256]{1,0:T(8,128)S(1)} %get-tuple-element.27), channel_id=1, source_target_pairs={{0,8},{16,24},{8,0},{24,16},{1,9},{17,25},{9,1},{25,17},{2,10},{18... | collective-permute-start | bytes 73736 | tf_op jit(solution)/shard_map/ppermute | solution.py:496
  24.7 5.8 %collective-permute-start.11 = (f32[24,256]{1,0:T(8,128)S(1)}, f32[24,256]{1,0:T(8,128)S(1)}, u32[]{:S(2)}, u32[]{:S(2)}) collective-permute-start(f32[24,256]{1,0:T(8,128)S(1)} %get-tuple-element.28), channel_id=1, source_target_pairs={{8,16},{0,24},{16,8},{24,0},{9,17},{1,25},{17,9},{25,1},{10,18},{2... | collective-permute-start | bytes 73736 | tf_op jit(solution)/shard_map/ppermute | solution.py:497
  25.6 1.2 %copy-start.6 = (f32[128]{0:T(128)S(1)}, f32[128]{0:T(128)}, u32[]{:S(2)}) copy-start(f32[128]{0:T(128)} %param.15) | copy-start | bytes 1540

commit v5 on v4

--- a/solution.py
+++ b/solution.py
@@ -174,7 +174,11 @@
         right = slice((3 + col) * channels, (4 + col) * channels)
         low, mid, up = (0.5 * conv_ref[row, col] for row in range(3))
         outer = 0.5 * (low + up)
-        for k, taps in enumerate((low, outer + 0.5 * mid, outer - 0.5 * mid, up, mid)):
+        even4, even6 = (low + 4.0 * up) * (1.0 / 24.0), (low + up) * (-1.0 / 6.0)
+        odd4, odd6 = mid * (1.0 / 12.0), mid * (1.0 / 6.0)
+        quads = (0.25 * low, even6 - odd6, even6 + odd6, even4 + odd4, even4 - odd4, up)
+        pairs = (low, outer + 0.5 * mid, outer - 0.5 * mid, up, mid)
+        for k, taps in enumerate(pairs + quads[:-1]):
             top, bottom = split(taps)
             out_ref[k, :channels, left] = top
             out_ref[k, :channels, right] = bottom
@@ -304,21 +308,39 @@
     channels = hidden_ref.shape[1]
     block = width + TAIL
     wet = ocean_ref[...].astype(F32).T
-    for group in groups:
-        terms = [[], [], [], []]
-        for first in group:
-            d = [hidden_ref[(first - 1 + k) * block : (first + k) * block, :] for k in range(4)]
-            terms[0].append(d[0] - d[2])
-            terms[1].append(d[1] + d[2])
-            terms[2].append(d[2] - d[1])
-            terms[3].append(d[1] - d[3])
-        m = [product(terms[k], filter_ref[k], channels) for k in range(4)]
-        pair = (m[0] + m[1] + m[2], m[1] - m[2] - m[3])
-        for g, first in enumerate(group):
-            for r in range(2):
-                t = columns(pair[r][g * block : (g + 1) * block], channels, width)
+
+    def rows_of(first, count):
+        return [hidden_ref[(first - 1 + k) * block : (first + k) * block, :] for k in range(count)]
+
+    def write(sums, firsts):
+        for g, first in enumerate(firsts):
+            for r, t in enumerate(sums):
+                t = columns(t[g * block : (g + 1) * block], channels, width)
                 row = first + r
                 out_ref[row - 1] = (t + bias_ref[...]) * wet[:, row : row + 1]
+
+    quads, pairs = groups
+    if quads:
+        terms = [[] for _ in range(6)]
+        for first in quads:
+            d = rows_of(first, 6)
+            a, b = d[4] - 4.0 * d[2], d[3] - 4.0 * d[1]
+            p, q = d[4] - d[2], 2.0 * (d[3] - d[1])
+            for k, term in enumerate(
+                (4.0 * d[0] - 5.0 * d[2] + d[4], a + b, a - b, p + q, p - q, 4.0 * d[1] - 5.0 * d[3] + d[5])
+            ):
+                terms[k].append(term)
+        m = [product(terms[k], filter_ref[index], channels) for k, index in enumerate((5, 6, 7, 8, 9, 3))]
+        sum1, dif1, sum2, dif2 = m[1] + m[2], m[1] - m[2], m[3] + m[4], m[3] - m[4]
+        write((m[0] + sum1 + sum2, dif1 + 2.0 * dif2, sum1 + 4.0 * sum2, dif1 + 8.0 * dif2 + m[5]), quads)
+    if pairs:
+        terms = [[] for _ in range(4)]
+        for first in pairs:
+            d = rows_of(first, 4)
+            for k, term in enumerate((d[0] - d[2], d[1] + d[2], d[2] - d[1], d[1] - d[3])):
+                terms[k].append(term)
+        m = [product(terms[k], filter_ref[k], channels) for k in range(4)]
+        write((m[0] + m[1] + m[2], m[1] - m[2] - m[3]), pairs)
 
 
 def outer_kernel(
@@ -444,7 +466,7 @@
     )(modes.reshape(1, total_modes), local_weight, spectral_weight, ocean)
     filters = pl.pallas_call(
         filter_kernel,
-        out_shape=struct((5, 2 * channels, 6 * channels), BF16),
+        out_shape=struct((10, 2 * channels, 6 * channels), BF16),
         in_specs=[vmem()],
         out_specs=vmem(),
         compiler_params=params(16),
@@ -509,10 +531,8 @@
     )(high, low, got, mixed, trig, local, layer, *crossed)
 
     bias = conv_bias.reshape(1, channels)
-    firsts = list(range(1, rows - 1, 2))
-    groups = [firsts[k : k + 2] for k in range(0, len(firsts), 2)]
-    if len(groups) > 1 and len(groups[-1]) == 1:
-        groups[-2:] = [groups[-2] + groups[-1]]
+    whole = (rows - 2) // 4 * 4
+    groups = (list(range(1, whole, 4)), list(range(1 + whole, rows - 1, 2)))
     flops = 2 * 6 * 4 * rows * width * channels * channels
     inner = pl.pallas_call(
         functools.partial(inner_kernel, groups),

time: 32.3 us -> 32.2 us (level)
    ppermute x3, waiting for transfers between devices: 0.41 us -> 0.01 us  [per_device(): parts[d] = lax.ppermute(send, 'lon', chip_moves(d, chips, flip_of(d)))]
    ppermute x3, waiting for transfers between devices: 3.65 us -> 4.03 us  [per_device(): gathered.append(lax.ppermute(own_mixed, 'lon', chip_moves(d, chips, 0)))]
    pallas_call x1, Pallas kernels: 0.32 us -> 0.68 us  [per_device(): pl.pallas_call(filter_kernel, out_shape=struct((10, 2 * channels, 6 * cha...]
  transfers between devices with their start and end apart: 12 -> 12, of which waited for: 5 -> 4; matrix products, arithmetic and copies ran while one was open for 0% -> 0% of each run, Pallas kernels for 18% -> 18%
where the time goes in v5:
time: 32.2 us; the launch traced here: 32.1 us
  starting transfers between devices  15.9 us (49%)
  Pallas kernels  9.54 us (30%)
  waiting for transfers between devices  6.35 us (20%)
    ppermute x3, starting transfers between devices, per_device(): parts[d] = lax.ppermute(send, 'lon', chip_moves(d, chips, flip_of(d)))  5.41 us
    ppermute x3, starting transfers between devices, per_device(): gathered.append(lax.ppermute(own_mixed, 'lon', chip_moves(d, chips, 0)))  4.39 us
    ppermute x3, waiting for transfers between devices, per_device(): gathered.append(lax.ppermute(own_mixed, 'lon', chip_moves(d, chips, 0)))  4.03 us
    pallas_call x1, Pallas kernels, per_device(): pl.pallas_call(functools.partial(inner_kernel, groups), out_shape=struct(...  3.35 us
    pallas_call x1, Pallas kernels, per_device(): pl.pallas_call(functools.partial(forward_kernel, chips, per, total_lon),...  2.07 us
    pallas_call x1, Pallas kernels, per_device(): pl.pallas_call(functools.partial(outer_kernel, bands), out_shape=struct((...  1.71 us
    ppermute x1, starting transfers between devices, per_device(): early_first = lax.ppermute(early_first, 'lat', evens)  1.6 us
    ppermute x1, starting transfers between devices, per_device(): late_first = lax.ppermute(late_first, 'lat', evens)  1.56 us
  transfers between devices with their start and end apart: 12, of which 4 were waited for; matrix products, arithmetic and copies ran while one was open for 0% of the time, Pallas kernels for 18%

profile of v5, /device:TPU:0, one launch (start us, length us, event | category | flops | bytes accessed | tf_op | source)
XLA Modules:
  0.0 32.1 jit_solution(7004458215398837062)
XLA Ops:
  0.0 0.0 copy-start
  0.0 2.1 %forward.1 = (f32[9,16,256]{2,1,0:T(8,128)S(1)}, f32[8,16,256]{2,1,0:T(8,128)S(1)}, f32[1,16,256]{2,1,0:T(8,128)S(1)}, f32[264,128]{1,0:T(8,128)S(1)}, f32[264,1...) custom-call(s32[16]{0:T(128)} %modes_hbm.1, f32[16,256,128]{2,1,0:T(8,128)} %field_hbm.1, ...), custom_call_target="tpu_custom_call" | custom-call | tf_op jit(solution)/shard_map/forward/pallas_call | solution.py:427
  2.1 0.6 %collective-permute-start = (f32[144,256]{1,0:T(8,128)S(1)}, f32[144,256]{1,0:T(8,128)S(1)}, u32[]{:S(2)}, u32[]{:S(2)}) collective-permute-start(f32[144,256]{1,0:T(8,128)S(1)} %bitcast.16), channel_id=1, source_target_pairs={{0,1},{1,0},{2,3},{3,2},{4,5},{5,4},{6,7},{7,6},{8,9},{9,8},{10,11... | collective-permute-start | bytes 442376 | tf_op jit(solution)/shard_map/ppermute | solution.py:476
  2.6 1.0 %collective-permute-done.got_ref = f32[144,256]{1,0:T(8,128)S(1)} collective-permute-done((f32[144,256]{1,0:T(8,128)S(1)}, f32[144,256]{1,0:T(8,128)S(1)}, u32[]{:S(2)}, u32[]{:S(2)}) %collective-permute-start) | collective-permute-done | bytes 147488 | tf_op jit(solution)/shard_map/ppermute | solution.py:476
  3.7 4.8 %collective-permute-start.3 = (f32[48,256]{1,0:T(8,128)S(1)}, f32[48,256]{1,0:T(8,128)S(1)}, u32[]{:S(2)}, u32[]{:S(2)}) collective-permute-start(f32[48,256]{1,0:T(8,128)S(1)} %get-tuple-element.32), channel_id=1, source_target_pairs={{0,7},{1,6},{2,5},{3,4},{4,3},{5,2},{6,1},{7,0},{8,15},{9,14},{10,... | collective-permute-start | bytes 147464 | tf_op jit(solution)/shard_map/ppermute | solution.py:484
  8.5 0.0 collective-permute-start.1
  8.5 0.6 %collective-permute-start.2 = (f32[32,256]{1,0:T(8,128)S(1)}, f32[32,256]{1,0:T(8,128)S(1)}, u32[]{:S(2)}, u32[]{:S(2)}) collective-permute-start(f32[32,256]{1,0:T(8,128)S(1)} %get-tuple-element.30), channel_id=1, source_target_pairs={{0,4},{1,5},{2,6},{3,7},{4,0},{5,1},{6,2},{7,3},{8,12},{9,13},{10,... | collective-permute-start | bytes 98312 | tf_op jit(solution)/shard_map/ppermute | solution.py:484
  9.1 1.6 %collective-permute-start.8 = (f32[264,128]{1,0:T(8,128)S(1)}, f32[264,128]{1,0:T(8,128)S(1)}, u32[]{:S(2)}, u32[]{:S(2)}) collective-permute-start(f32[264,128]{1,0:T(8,128)S(1)} %get-tuple-element.25), channel_id=1, source_target_pairs={{0,8},{16,24},{8,0},{24,16},{1,9},{17,25},{9,1},{25,17},{2,10},{18... | collective-permute-start | bytes 405512 | tf_op jit(solution)/shard_map/ppermute | solution.py:491
  10.7 0.0 copy-start.1
  10.7 0.0 copy-start.2
  10.7 0.0 copy-start.3
  10.7 0.0 copy-start.4
  10.7 1.6 %collective-permute-start.9 = (f32[264,128]{1,0:T(8,128)S(1)}, f32[264,128]{1,0:T(8,128)S(1)}, u32[]{:S(2)}, u32[]{:S(2)}) collective-permute-start(f32[264,128]{1,0:T(8,128)S(1)} %get-tuple-element.26), channel_id=1, source_target_pairs={{8,16},{0,24},{16,8},{24,0},{9,17},{1,25},{17,9},{25,1},{10,18},{2... | collective-permute-start | bytes 405512 | tf_op jit(solution)/shard_map/ppermute | solution.py:492
  12.3 0.0 copy-done
  12.3 0.7 %filters.1.filter_ref = bf16[10,256,768]{2,1,0:T(8,128)(2,1)S(1)} custom-call(f32[3,3,128,128]{3,2,1,0:T(8,128)S(1)} %copy-done), custom_call_target="tpu_custom_call" | custom-call | tf_op jit(solution)/shard_map/filters/pallas_call | solution.py:467
  13.0 0.0 copy-start.5
  13.0 0.0 copy-done.1
  13.0 0.0 copy-done.2
  13.0 0.0 copy-done.3
  13.0 0.0 copy-done.4
  13.0 0.3 prepare.1
  13.3 0.0 collective-permute-done.2.refs_2_
  13.3 0.0 collective-permute-done.3.refs_3_.refs_1_
  13.4 0.0 collective-permute-done.1.refs_1_.refs_0_
  13.4 0.2 mix.1
  13.6 3.6 %collective-permute-start.6 = (f32[32,256]{1,0:T(8,128)S(1)}, f32[32,256]{1,0:T(8,128)S(1)}, u32[]{:S(2)}, u32[]{:S(2)}) collective-permute-start(f32[32,256]{1,0:T(8,128)S(1)} %mix.1), channel_id=1, source_target_pairs={{0,6},{1,7},{2,4},{3,5},{4,2},{5,3},{6,0},{7,1},{8,14},{9,15},{10,... | collective-permute-start | bytes 98312 | tf_op jit(solution)/shard_map/ppermute | solution.py:504
  17.2 0.0 collective-permute-start.5
  17.2 0.8 %collective-permute-start.4 = (f32[32,256]{1,0:T(8,128)S(1)}, f32[32,256]{1,0:T(8,128)S(1)}, u32[]{:S(2)}, u32[]{:S(2)}) collective-permute-start(f32[32,256]{1,0:T(8,128)S(1)} %mix.1), channel_id=1, source_target_pairs={{0,2},{1,3},{2,0},{3,1},{4,6},{5,7},{6,4},{7,5},{8,10},{9,11},{10,... | collective-permute-start | bytes 98312 | tf_op jit(solution)/shard_map/ppermute | solution.py:504
  18.0 1.5 %collective-permute-done.6 = f32[32,256]{1,0:T(8,128)S(1)} collective-permute-done((f32[32,256]{1,0:T(8,128)S(1)}, f32[32,256]{1,0:T(8,128)S(1)}, u32[]{:S(2)}, u32[]{:S(2)}) %collective-permute-start.6) | collective-permute-done | bytes 32800 | tf_op jit(solution)/shard_map/ppermute | solution.py:504
  19.5 2.5 %collective-permute-done.5 = f32[32,256]{1,0:T(8,128)S(1)} collective-permute-done((f32[32,256]{1,0:T(8,128)S(1)}, f32[32,256]{1,0:T(8,128)S(1)}, u32[]{:S(2)}, u32[]{:S(2)}) %collective-permute-start.5) | collective-permute-done | bytes 32800 | tf_op jit(solution)/shard_map/ppermute | solution.py:504
  22.0 0.0 collective-permute-done.4
  22.0 0.1 collective-permute-start.7
  22.1 1.3 %collective-permute-done.7 = f32[128,256]{1,0:T(8,128)S(1)} collective-permute-done((f32[128,256]{1,0:T(8,128)S(1)}, f32[128,256]{1,0:T(8,128)S(1)}, u32[]{:S(2)}, u32[]{:S(2)}) %collective-permute-start.7) | collective-permute-done | bytes 131104 | tf_op jit(solution)/shard_map/ppermute | solution.py:506
  23.5 1.6 %collective-permute-start.10 = (f32[24,256]{1,0:T(8,128)S(1)}, f32[24,256]{1,0:T(8,128)S(1)}, u32[]{:S(2)}, u32[]{:S(2)}) collective-permute-start(f32[24,256]{1,0:T(8,128)S(1)} %get-tuple-element.27), channel_id=1, source_target_pairs={{0,8},{16,24},{8,0},{24,16},{1,9},{17,25},{9,1},{25,17},{2,10},{18... | collective-permute-start | bytes 73736 | tf_op jit(solution)/shard_map/ppermute | solution.py:518
  25.1 0.7 %collective-permute-start.11 = (f32[24,256]{1,0:T(8,128)S(1)}, f32[24,256]{1,0:T(8,128)S(1)}, u32[]{:S(2)}, u32[]{:S(2)}) collective-permute-start(f32[24,256]{1,0:T(8,128)S(1)} %get-tuple-element.28), channel_id=1, source_target_pairs={{8,16},{0,24},{16,8},{24,0},{9,17},{1,25},{17,9},{25,1},{10,18},{2... | collective-permute-start | bytes 73736 | tf_op jit(solution)/shard_map/ppermute | solution.py:519
  25.8 0.0 copy-done.5
  25.8 0.0 copy-start.6
  25.8 1.2 %hidden.1.hidden_ref = f32[4224,128]{1,0:T(8,128)S(1)} custom-call(bf16[16,256,128]{2,1,0:T(8,128)(2,1)S(1)} %get-tuple-element.17.high_ref, bf16[16,256,128]{2,1,0:T(8,128)(2,1)S(1)} %get-tuple-element.18.low_ref, f32[144,256]{1,0:T(8,128)S(1)} %collective-permute-done.got_ref, f32[16,16,256]{2,1,0:T(8,128)S(1)} %bitcast.9, ...), custom_call_target="tpu_custom_call" | custom-call | flops 805306368 | bytes 2097152 | tf_op jit(solution)/shard_map/hidden/pallas_call | solution.py:521
  27.0 0.0 copy-done.6
  27.0 3.3 %inner.1.inner_ref = f32[14,256,128]{2,1,0:T(8,128)S(1)} custom-call(f32[4224,128]{1,0:T(8,128)S(1)} %hidden.1.hidden_ref, s32[16,256]{1,0:T(8,128)S(1)} %copy-done.2, f32[1,128]{1,0:T(1,128)S(1)} %bitcast.14, bf16[10,256,768]{2,1,0:T(8,128)(2,1)S(1)} %filters.1.filter_ref), custom_call_target="tpu_custom_call" | custom-call | flops 3221225472 | bytes 2097152 | tf_op jit(solution)/shard_map/inner/pallas_call | solution.py:537
  30.3 0.0 collective-permute-done.8.early_first
  30.3 0.0 collective-permute-done.9.early_second
  30.3 0.0 collective-permute-done.10.late_first
  30.3 0.0 collective-permute-done.11.late_second
  30.4 1.7 %outer.1 = f32[16,256,128]{2,1,0:T(8,128)} custom-call(f32[4224,128]{1,0:T(8,128)S(1)} %hidden.1.hidden_ref, f32[264,128]{1,0:T(8,128)S(1)} %collective-permute-done.8.early_first, f32[264,128]{1,0:T(8,128)S(1)} %collective-permute-done.9.early_second, f32[24,256]{1,0:T(8,128)S(1)} %collective-permute-done.10.late_first, ...), custom_call_target="tpu_custom_call" | custom-call | tf_op jit(solution)/shard_map/outer/pallas_call | solution.py:546
  (10 shorter events, 0.1 us)
Async XLA Ops:
  0.0 12.3 %copy-start = (f32[3,3,128,128]{3,2,1,0:T(8,128)S(1)}, f32[3,3,128,128]{3,2,1,0:T(8,128)}, u32[]{:S(2)}) copy-start(f32[3,3,128,128]{3,2,1,0:T(8,128)} %conv_ref.1) | copy-start | bytes 1769476
  2.1 1.6 %collective-permute-start = (f32[144,256]{1,0:T(8,128)S(1)}, f32[144,256]{1,0:T(8,128)S(1)}, u32[]{:S(2)}, u32[]{:S(2)}) collective-permute-start(f32[144,256]{1,0:T(8,128)S(1)} %bitcast.16), channel_id=1, source_target_pairs={{0,1},{1,0},{2,3},{3,2},{4,5},{5,4},{6,7},{7,6},{8,9},{9,8},{10,11... | collective-permute-start | bytes 442376 | tf_op jit(solution)/shard_map/ppermute | solution.py:476
  3.7 9.6 %collective-permute-start.3 = (f32[48,256]{1,0:T(8,128)S(1)}, f32[48,256]{1,0:T(8,128)S(1)}, u32[]{:S(2)}, u32[]{:S(2)}) collective-permute-start(f32[48,256]{1,0:T(8,128)S(1)} %get-tuple-element.32), channel_id=1, source_target_pairs={{0,7},{1,6},{2,5},{3,4},{4,3},{5,2},{6,1},{7,0},{8,15},{9,14},{10,... | collective-permute-start | bytes 147464 | tf_op jit(solution)/shard_map/ppermute | solution.py:484
  8.5 4.9 %collective-permute-start.1 = (f32[48,256]{1,0:T(8,128)S(1)}, f32[48,256]{1,0:T(8,128)S(1)}, u32[]{:S(2)}, u32[]{:S(2)}) collective-permute-start(f32[48,256]{1,0:T(8,128)S(1)} %get-tuple-element.33), channel_id=1, source_target_pairs={{0,3},{1,2},{2,1},{3,0},{4,7},{5,6},{6,5},{7,4},{8,11},{9,10},{10,... | collective-permute-start | bytes 147464 | tf_op jit(solution)/shard_map/ppermute | solution.py:484
  8.5 4.9 %collective-permute-start.2 = (f32[32,256]{1,0:T(8,128)S(1)}, f32[32,256]{1,0:T(8,128)S(1)}, u32[]{:S(2)}, u32[]{:S(2)}) collective-permute-start(f32[32,256]{1,0:T(8,128)S(1)} %get-tuple-element.30), channel_id=1, source_target_pairs={{0,4},{1,5},{2,6},{3,7},{4,0},{5,1},{6,2},{7,3},{8,12},{9,13},{10,... | collective-permute-start | bytes 98312 | tf_op jit(solution)/shard_map/ppermute | solution.py:484
  9.1 21.2 %collective-permute-start.8 = (f32[264,128]{1,0:T(8,128)S(1)}, f32[264,128]{1,0:T(8,128)S(1)}, u32[]{:S(2)}, u32[]{:S(2)}) collective-permute-start(f32[264,128]{1,0:T(8,128)S(1)} %get-tuple-element.25), channel_id=1, source_target_pairs={{0,8},{16,24},{8,0},{24,16},{1,9},{17,25},{9,1},{25,17},{2,10},{18... | collective-permute-start | bytes 405512 | tf_op jit(solution)/shard_map/ppermute | solution.py:491
  10.7 2.3 %copy-start.1 = (f32[2,2,128,128]{3,2,1,0:T(8,128)S(1)}, f32[2,2,128,128]{3,2,1,0:T(8,128)}, u32[]{:S(2)}) copy-start(f32[2,2,128,128]{3,2,1,0:T(8,128)} %spectral_ref.1) | copy-start | bytes 786436
  10.7 2.3 %copy-start.2 = (s32[16,256]{1,0:T(8,128)S(1)}, s32[16,256]{1,0:T(8,128)}, u32[]{:S(2)}) copy-start(s32[16,256]{1,0:T(8,128)} %ocean_ref.5) | copy-start | bytes 49156
  10.7 2.3 %copy-start.3 = (f32[128,128]{1,0:T(8,128)S(1)}, f32[128,128]{1,0:T(8,128)}, u32[]{:S(2)}) copy-start(f32[128,128]{1,0:T(8,128)} %local_ref.1) | copy-start | bytes 196612
  10.7 2.3 %copy-start.4 = (s32[16]{0:T(128)S(1)}, s32[16]{0:T(128)}, u32[]{:S(2)}) copy-start(s32[16]{0:T(128)} %modes_hbm.1) | copy-start | bytes 196
  10.7 19.6 %collective-permute-start.9 = (f32[264,128]{1,0:T(8,128)S(1)}, f32[264,128]{1,0:T(8,128)S(1)}, u32[]{:S(2)}, u32[]{:S(2)}) collective-permute-start(f32[264,128]{1,0:T(8,128)S(1)} %get-tuple-element.26), channel_id=1, source_target_pairs={{8,16},{0,24},{16,8},{24,0},{9,17},{1,25},{17,9},{25,1},{10,18},{2... | collective-permute-start | bytes 405512 | tf_op jit(solution)/shard_map/ppermute | solution.py:492
  13.0 12.8 %copy-start.5 = (f32[128]{0:T(128)S(1)}, f32[128]{0:T(128)}, u32[]{:S(2)}) copy-start(f32[128]{0:T(128)} %param.13) | copy-start | bytes 1540
  13.6 5.9 %collective-permute-start.6 = (f32[32,256]{1,0:T(8,128)S(1)}, f32[32,256]{1,0:T(8,128)S(1)}, u32[]{:S(2)}, u32[]{:S(2)}) collective-permute-start(f32[32,256]{1,0:T(8,128)S(1)} %mix.1), channel_id=1, source_target_pairs={{0,6},{1,7},{2,4},{3,5},{4,2},{5,3},{6,0},{7,1},{8,14},{9,15},{10,... | collective-permute-start | bytes 98312 | tf_op jit(solution)/shard_map/ppermute | solution.py:504
  17.2 4.8 %collective-permute-start.5 = (f32[32,256]{1,0:T(8,128)S(1)}, f32[32,256]{1,0:T(8,128)S(1)}, u32[]{:S(2)}, u32[]{:S(2)}) collective-permute-start(f32[32,256]{1,0:T(8,128)S(1)} %mix.1), channel_id=1, source_target_pairs={{0,4},{1,5},{2,6},{3,7},{4,0},{5,1},{6,2},{7,3},{8,12},{9,13},{10,... | collective-permute-start | bytes 98312 | tf_op jit(solution)/shard_map/ppermute | solution.py:504
  17.2 4.8 %collective-permute-start.4 = (f32[32,256]{1,0:T(8,128)S(1)}, f32[32,256]{1,0:T(8,128)S(1)}, u32[]{:S(2)}, u32[]{:S(2)}) collective-permute-start(f32[32,256]{1,0:T(8,128)S(1)} %mix.1), channel_id=1, source_target_pairs={{0,2},{1,3},{2,0},{3,1},{4,6},{5,7},{6,4},{7,5},{8,10},{9,11},{10,... | collective-permute-start | bytes 98312 | tf_op jit(solution)/shard_map/ppermute | solution.py:504
  22.0 1.4 %collective-permute-start.7 = (f32[128,256]{1,0:T(8,128)S(1)}, f32[128,256]{1,0:T(8,128)S(1)}, u32[]{:S(2)}, u32[]{:S(2)}) collective-permute-start(f32[128,256]{1,0:T(8,128)S(1)} %pad_maximum_fusion), channel_id=1, source_target_pairs={{0,1},{1,0},{2,3},{3,2},{4,5},{5,4},{6,7},{7,6},{8,9},{9,8},{10,11... | collective-permute-start | bytes 393224 | tf_op jit(solution)/shard_map/ppermute | solution.py:506
  23.5 6.8 %collective-permute-start.10 = (f32[24,256]{1,0:T(8,128)S(1)}, f32[24,256]{1,0:T(8,128)S(1)}, u32[]{:S(2)}, u32[]{:S(2)}) collective-permute-start(f32[24,256]{1,0:T(8,128)S(1)} %get-tuple-element.27), channel_id=1, source_target_pairs={{0,8},{16,24},{8,0},{24,16},{1,9},{17,25},{9,1},{25,17},{2,10},{18... | collective-permute-start | bytes 73736 | tf_op jit(solution)/shard_map/ppermute | solution.py:518
  25.1 5.3 %collective-permute-start.11 = (f32[24,256]{1,0:T(8,128)S(1)}, f32[24,256]{1,0:T(8,128)S(1)}, u32[]{:S(2)}, u32[]{:S(2)}) collective-permute-start(f32[24,256]{1,0:T(8,128)S(1)} %get-tuple-element.28), channel_id=1, source_target_pairs={{8,16},{0,24},{16,8},{24,0},{9,17},{1,25},{17,9},{25,1},{10,18},{2... | collective-permute-start | bytes 73736 | tf_op jit(solution)/shard_map/ppermute | solution.py:519
  25.8 1.2 %copy-start.6 = (f32[128]{0:T(128)S(1)}, f32[128]{0:T(128)}, u32[]{:S(2)}) copy-start(f32[128]{0:T(128)} %param.15) | copy-start | bytes 1540

commit v6 on v5

--- a/solution.py
+++ b/solution.py
@@ -67,13 +67,12 @@
     high_ref, low_ref,     modes_ref, field_ref, ocean_ref, small_sem, field_sem,
 ):
     rows, width, channels = field_ref.shape
-    chunks = field_sem.shape[0]
-    step = rows // chunks
+    starts = [0, rows * 3 // 4]
     first_copy = pltpu.make_async_copy(modes_hbm, modes_ref, small_sem.at[0])
     first_copy.start()
     copies = []
-    for k in range(chunks):
-        part = pl.ds(k * step, step)
+    for k, (start, stop) in enumerate(zip(starts, starts[1:] + [rows])):
+        part = pl.ds(start, stop - start)
         copies.append(pltpu.make_async_copy(field_hbm.at[part], field_ref.at[part], field_sem.at[k]))
         copies[-1].start()
     ocean_copy = pltpu.make_async_copy(ocean_hbm, ocean_ref, small_sem.at[1])
@@ -94,8 +93,8 @@
     table = jnp.concatenate([jnp.cos(theta) * scale, -jnp.sin(theta) * scale], 0)
     lhs = jnp.concatenate(split(table), 0)
     for i in range(rows):
-        if i % step == 0:
-            copies[i // step].wait()
+        if i in starts:
+            copies[starts.index(i)].wait()
         high, low = split(field_ref[i])
         high_ref[i] = high
         low_ref[i] = low

time: 32.2 us -> 32.4 us (level)
  no operation moved by 1% of the time
where the time goes in v6:
time: 32.4 us; the launch traced here: 32.3 us
  starting transfers between devices  15.9 us (49%)
  Pallas kernels  9.72 us (30%)
  waiting for transfers between devices  6.35 us (20%)
    ppermute x3, starting transfers between devices, per_device(): parts[d] = lax.ppermute(send, 'lon', chip_moves(d, chips, flip_of(d)))  5.41 us
    ppermute x3, starting transfers between devices, per_device(): gathered.append(lax.ppermute(own_mixed, 'lon', chip_moves(d, chips, 0)))  4.39 us
    ppermute x3, waiting for transfers between devices, per_device(): gathered.append(lax.ppermute(own_mixed, 'lon', chip_moves(d, chips, 0)))  4.03 us
    pallas_call x1, Pallas kernels, per_device(): pl.pallas_call(functools.partial(inner_kernel, groups), out_shape=struct(...  3.35 us
    pallas_call x1, Pallas kernels, per_device(): pl.pallas_call(functools.partial(forward_kernel, chips, per, total_lon),...  2.26 us
    pallas_call x1, Pallas kernels, per_device(): pl.pallas_call(functools.partial(outer_kernel, bands), out_shape=struct((...  1.71 us
    ppermute x1, starting transfers between devices, per_device(): early_first = lax.ppermute(early_first, 'lat', evens)  1.6 us
    ppermute x1, starting transfers between devices, per_device(): early_second = lax.ppermute(early_second, 'lat', odds)  1.56 us
  transfers between devices with their start and end apart: 12, of which 4 were waited for; matrix products, arithmetic and copies ran while one was open for 0% of the time, Pallas kernels for 18%

profile of v6, /device:TPU:0, one launch (start us, length us, event | category | flops | bytes accessed | tf_op | source)
XLA Modules:
  0.0 32.3 jit_solution(276696176928302107)
XLA Ops:
  0.0 0.0 copy-start
  0.0 2.3 %forward.1 = (f32[9,16,256]{2,1,0:T(8,128)S(1)}, f32[8,16,256]{2,1,0:T(8,128)S(1)}, f32[1,16,256]{2,1,0:T(8,128)S(1)}, f32[264,128]{1,0:T(8,128)S(1)}, f32[264,1...) custom-call(s32[16]{0:T(128)} %modes_hbm.1, f32[16,256,128]{2,1,0:T(8,128)} %field_hbm.1, ...), custom_call_target="tpu_custom_call" | custom-call | tf_op jit(solution)/shard_map/forward/pallas_call | solution.py:426
  2.3 0.6 %collective-permute-start = (f32[144,256]{1,0:T(8,128)S(1)}, f32[144,256]{1,0:T(8,128)S(1)}, u32[]{:S(2)}, u32[]{:S(2)}) collective-permute-start(f32[144,256]{1,0:T(8,128)S(1)} %bitcast.16), channel_id=1, source_target_pairs={{0,1},{1,0},{2,3},{3,2},{4,5},{5,4},{6,7},{7,6},{8,9},{9,8},{10,11... | collective-permute-start | bytes 442376 | tf_op jit(solution)/shard_map/ppermute | solution.py:475
  2.8 1.0 %collective-permute-done.got_ref = f32[144,256]{1,0:T(8,128)S(1)} collective-permute-done((f32[144,256]{1,0:T(8,128)S(1)}, f32[144,256]{1,0:T(8,128)S(1)}, u32[]{:S(2)}, u32[]{:S(2)}) %collective-permute-start) | collective-permute-done | bytes 147488 | tf_op jit(solution)/shard_map/ppermute | solution.py:475
  3.9 4.8 %collective-permute-start.3 = (f32[48,256]{1,0:T(8,128)S(1)}, f32[48,256]{1,0:T(8,128)S(1)}, u32[]{:S(2)}, u32[]{:S(2)}) collective-permute-start(f32[48,256]{1,0:T(8,128)S(1)} %get-tuple-element.32), channel_id=1, source_target_pairs={{0,7},{1,6},{2,5},{3,4},{4,3},{5,2},{6,1},{7,0},{8,15},{9,14},{10,... | collective-permute-start | bytes 147464 | tf_op jit(solution)/shard_map/ppermute | solution.py:483
  8.7 0.0 collective-permute-start.1
  8.7 0.6 %collective-permute-start.2 = (f32[32,256]{1,0:T(8,128)S(1)}, f32[32,256]{1,0:T(8,128)S(1)}, u32[]{:S(2)}, u32[]{:S(2)}) collective-permute-start(f32[32,256]{1,0:T(8,128)S(1)} %get-tuple-element.30), channel_id=1, source_target_pairs={{0,4},{1,5},{2,6},{3,7},{4,0},{5,1},{6,2},{7,3},{8,12},{9,13},{10,... | collective-permute-start | bytes 98312 | tf_op jit(solution)/shard_map/ppermute | solution.py:483
  9.3 1.6 %collective-permute-start.8 = (f32[264,128]{1,0:T(8,128)S(1)}, f32[264,128]{1,0:T(8,128)S(1)}, u32[]{:S(2)}, u32[]{:S(2)}) collective-permute-start(f32[264,128]{1,0:T(8,128)S(1)} %get-tuple-element.25), channel_id=1, source_target_pairs={{0,8},{16,24},{8,0},{24,16},{1,9},{17,25},{9,1},{25,17},{2,10},{18... | collective-permute-start | bytes 405512 | tf_op jit(solution)/shard_map/ppermute | solution.py:490
  10.9 0.0 copy-start.1
  10.9 0.0 copy-start.2
  10.9 0.0 copy-start.3
  10.9 0.0 copy-start.4
  10.9 1.6 %collective-permute-start.9 = (f32[264,128]{1,0:T(8,128)S(1)}, f32[264,128]{1,0:T(8,128)S(1)}, u32[]{:S(2)}, u32[]{:S(2)}) collective-permute-start(f32[264,128]{1,0:T(8,128)S(1)} %get-tuple-element.26), channel_id=1, source_target_pairs={{8,16},{0,24},{16,8},{24,0},{9,17},{1,25},{17,9},{25,1},{10,18},{2... | collective-permute-start | bytes 405512 | tf_op jit(solution)/shard_map/ppermute | solution.py:491
  12.5 0.0 copy-done
  12.5 0.7 %filters.1.filter_ref = bf16[10,256,768]{2,1,0:T(8,128)(2,1)S(1)} custom-call(f32[3,3,128,128]{3,2,1,0:T(8,128)S(1)} %copy-done), custom_call_target="tpu_custom_call" | custom-call | tf_op jit(solution)/shard_map/filters/pallas_call | solution.py:466
  13.2 0.0 copy-start.5
  13.2 0.0 copy-done.1
  13.2 0.0 copy-done.2
  13.2 0.0 copy-done.3
  13.2 0.0 copy-done.4
  13.2 0.3 prepare.1
  13.5 0.0 collective-permute-done.2.refs_2_
  13.5 0.0 collective-permute-done.3.refs_3_.refs_1_
  13.6 0.0 collective-permute-done.1.refs_1_.refs_0_
  13.6 0.2 mix.1
  13.8 3.6 %collective-permute-start.6 = (f32[32,256]{1,0:T(8,128)S(1)}, f32[32,256]{1,0:T(8,128)S(1)}, u32[]{:S(2)}, u32[]{:S(2)}) collective-permute-start(f32[32,256]{1,0:T(8,128)S(1)} %mix.1), channel_id=1, source_target_pairs={{0,6},{1,7},{2,4},{3,5},{4,2},{5,3},{6,0},{7,1},{8,14},{9,15},{10,... | collective-permute-start | bytes 98312 | tf_op jit(solution)/shard_map/ppermute | solution.py:503
  17.4 0.0 collective-permute-start.5
  17.4 0.8 %collective-permute-start.4 = (f32[32,256]{1,0:T(8,128)S(1)}, f32[32,256]{1,0:T(8,128)S(1)}, u32[]{:S(2)}, u32[]{:S(2)}) collective-permute-start(f32[32,256]{1,0:T(8,128)S(1)} %mix.1), channel_id=1, source_target_pairs={{0,2},{1,3},{2,0},{3,1},{4,6},{5,7},{6,4},{7,5},{8,10},{9,11},{10,... | collective-permute-start | bytes 98312 | tf_op jit(solution)/shard_map/ppermute | solution.py:503
  18.2 1.5 %collective-permute-done.6 = f32[32,256]{1,0:T(8,128)S(1)} collective-permute-done((f32[32,256]{1,0:T(8,128)S(1)}, f32[32,256]{1,0:T(8,128)S(1)}, u32[]{:S(2)}, u32[]{:S(2)}) %collective-permute-start.6) | collective-permute-done | bytes 32800 | tf_op jit(solution)/shard_map/ppermute | solution.py:503
  19.7 2.5 %collective-permute-done.5 = f32[32,256]{1,0:T(8,128)S(1)} collective-permute-done((f32[32,256]{1,0:T(8,128)S(1)}, f32[32,256]{1,0:T(8,128)S(1)}, u32[]{:S(2)}, u32[]{:S(2)}) %collective-permute-start.5) | collective-permute-done | bytes 32800 | tf_op jit(solution)/shard_map/ppermute | solution.py:503
  22.2 0.0 collective-permute-done.4
  22.2 0.1 collective-permute-start.7
  22.3 1.3 %collective-permute-done.7 = f32[128,256]{1,0:T(8,128)S(1)} collective-permute-done((f32[128,256]{1,0:T(8,128)S(1)}, f32[128,256]{1,0:T(8,128)S(1)}, u32[]{:S(2)}, u32[]{:S(2)}) %collective-permute-start.7) | collective-permute-done | bytes 131104 | tf_op jit(solution)/shard_map/ppermute | solution.py:505
  23.7 1.6 %collective-permute-start.10 = (f32[24,256]{1,0:T(8,128)S(1)}, f32[24,256]{1,0:T(8,128)S(1)}, u32[]{:S(2)}, u32[]{:S(2)}) collective-permute-start(f32[24,256]{1,0:T(8,128)S(1)} %get-tuple-element.27), channel_id=1, source_target_pairs={{0,8},{16,24},{8,0},{24,16},{1,9},{17,25},{9,1},{25,17},{2,10},{18... | collective-permute-start | bytes 73736 | tf_op jit(solution)/shard_map/ppermute | solution.py:517
  25.2 0.7 %collective-permute-start.11 = (f32[24,256]{1,0:T(8,128)S(1)}, f32[24,256]{1,0:T(8,128)S(1)}, u32[]{:S(2)}, u32[]{:S(2)}) collective-permute-start(f32[24,256]{1,0:T(8,128)S(1)} %get-tuple-element.28), channel_id=1, source_target_pairs={{8,16},{0,24},{16,8},{24,0},{9,17},{1,25},{17,9},{25,1},{10,18},{2... | collective-permute-start | bytes 73736 | tf_op jit(solution)/shard_map/ppermute | solution.py:518
  26.0 0.0 copy-done.5
  26.0 0.0 copy-start.6
  26.0 1.2 %hidden.1.hidden_ref = f32[4224,128]{1,0:T(8,128)S(1)} custom-call(bf16[16,256,128]{2,1,0:T(8,128)(2,1)S(1)} %get-tuple-element.17.high_ref, bf16[16,256,128]{2,1,0:T(8,128)(2,1)S(1)} %get-tuple-element.18.low_ref, f32[144,256]{1,0:T(8,128)S(1)} %collective-permute-done.got_ref, f32[16,16,256]{2,1,0:T(8,128)S(1)} %bitcast.9, ...), custom_call_target="tpu_custom_call" | custom-call | flops 805306368 | bytes 2097152 | tf_op jit(solution)/shard_map/hidden/pallas_call | solution.py:520
  27.1 0.0 copy-done.6
  27.2 3.3 %inner.1.inner_ref = f32[14,256,128]{2,1,0:T(8,128)S(1)} custom-call(f32[4224,128]{1,0:T(8,128)S(1)} %hidden.1.hidden_ref, s32[16,256]{1,0:T(8,128)S(1)} %copy-done.2, f32[1,128]{1,0:T(1,128)S(1)} %bitcast.14, bf16[10,256,768]{2,1,0:T(8,128)(2,1)S(1)} %filters.1.filter_ref), custom_call_target="tpu_custom_call" | custom-call | flops 3221225472 | bytes 2097152 | tf_op jit(solution)/shard_map/inner/pallas_call | solution.py:536
  30.5 0.0 collective-permute-done.8.early_first
  30.5 0.0 collective-permute-done.9.early_second
  30.5 0.0 collective-permute-done.10.late_first
  30.5 0.0 collective-permute-done.11.late_second
  30.5 1.7 %outer.1 = f32[16,256,128]{2,1,0:T(8,128)} custom-call(f32[4224,128]{1,0:T(8,128)S(1)} %hidden.1.hidden_ref, f32[264,128]{1,0:T(8,128)S(1)} %collective-permute-done.8.early_first, f32[264,128]{1,0:T(8,128)S(1)} %collective-permute-done.9.early_second, f32[24,256]{1,0:T(8,128)S(1)} %collective-permute-done.10.late_first, ...), custom_call_target="tpu_custom_call" | custom-call | tf_op jit(solution)/shard_map/outer/pallas_call | solution.py:545
  (10 shorter events, 0.1 us)
Async XLA Ops:
  0.0 12.5 %copy-start = (f32[3,3,128,128]{3,2,1,0:T(8,128)S(1)}, f32[3,3,128,128]{3,2,1,0:T(8,128)}, u32[]{:S(2)}) copy-start(f32[3,3,128,128]{3,2,1,0:T(8,128)} %conv_ref.1) | copy-start | bytes 1769476
  2.3 1.6 %collective-permute-start = (f32[144,256]{1,0:T(8,128)S(1)}, f32[144,256]{1,0:T(8,128)S(1)}, u32[]{:S(2)}, u32[]{:S(2)}) collective-permute-start(f32[144,256]{1,0:T(8,128)S(1)} %bitcast.16), channel_id=1, source_target_pairs={{0,1},{1,0},{2,3},{3,2},{4,5},{5,4},{6,7},{7,6},{8,9},{9,8},{10,11... | collective-permute-start | bytes 442376 | tf_op jit(solution)/shard_map/ppermute | solution.py:475
  3.9 9.6 %collective-permute-start.3 = (f32[48,256]{1,0:T(8,128)S(1)}, f32[48,256]{1,0:T(8,128)S(1)}, u32[]{:S(2)}, u32[]{:S(2)}) collective-permute-start(f32[48,256]{1,0:T(8,128)S(1)} %get-tuple-element.32), channel_id=1, source_target_pairs={{0,7},{1,6},{2,5},{3,4},{4,3},{5,2},{6,1},{7,0},{8,15},{9,14},{10,... | collective-permute-start | bytes 147464 | tf_op jit(solution)/shard_map/ppermute | solution.py:483
  8.7 4.9 %collective-permute-start.1 = (f32[48,256]{1,0:T(8,128)S(1)}, f32[48,256]{1,0:T(8,128)S(1)}, u32[]{:S(2)}, u32[]{:S(2)}) collective-permute-start(f32[48,256]{1,0:T(8,128)S(1)} %get-tuple-element.33), channel_id=1, source_target_pairs={{0,3},{1,2},{2,1},{3,0},{4,7},{5,6},{6,5},{7,4},{8,11},{9,10},{10,... | collective-permute-start | bytes 147464 | tf_op jit(solution)/shard_map/ppermute | solution.py:483
  8.7 4.9 %collective-permute-start.2 = (f32[32,256]{1,0:T(8,128)S(1)}, f32[32,256]{1,0:T(8,128)S(1)}, u32[]{:S(2)}, u32[]{:S(2)}) collective-permute-start(f32[32,256]{1,0:T(8,128)S(1)} %get-tuple-element.30), channel_id=1, source_target_pairs={{0,4},{1,5},{2,6},{3,7},{4,0},{5,1},{6,2},{7,3},{8,12},{9,13},{10,... | collective-permute-start | bytes 98312 | tf_op jit(solution)/shard_map/ppermute | solution.py:483
  9.3 21.2 %collective-permute-start.8 = (f32[264,128]{1,0:T(8,128)S(1)}, f32[264,128]{1,0:T(8,128)S(1)}, u32[]{:S(2)}, u32[]{:S(2)}) collective-permute-start(f32[264,128]{1,0:T(8,128)S(1)} %get-tuple-element.25), channel_id=1, source_target_pairs={{0,8},{16,24},{8,0},{24,16},{1,9},{17,25},{9,1},{25,17},{2,10},{18... | collective-permute-start | bytes 405512 | tf_op jit(solution)/shard_map/ppermute | solution.py:490
  10.9 2.3 %copy-start.1 = (f32[2,2,128,128]{3,2,1,0:T(8,128)S(1)}, f32[2,2,128,128]{3,2,1,0:T(8,128)}, u32[]{:S(2)}) copy-start(f32[2,2,128,128]{3,2,1,0:T(8,128)} %spectral_ref.1) | copy-start | bytes 786436
  10.9 2.3 %copy-start.2 = (s32[16,256]{1,0:T(8,128)S(1)}, s32[16,256]{1,0:T(8,128)}, u32[]{:S(2)}) copy-start(s32[16,256]{1,0:T(8,128)} %ocean_ref.5) | copy-start | bytes 49156
  10.9 2.3 %copy-start.3 = (f32[128,128]{1,0:T(8,128)S(1)}, f32[128,128]{1,0:T(8,128)}, u32[]{:S(2)}) copy-start(f32[128,128]{1,0:T(8,128)} %local_ref.1) | copy-start | bytes 196612
  10.9 2.3 %copy-start.4 = (s32[16]{0:T(128)S(1)}, s32[16]{0:T(128)}, u32[]{:S(2)}) copy-start(s32[16]{0:T(128)} %modes_hbm.1) | copy-start | bytes 196
  10.9 19.6 %collective-permute-start.9 = (f32[264,128]{1,0:T(8,128)S(1)}, f32[264,128]{1,0:T(8,128)S(1)}, u32[]{:S(2)}, u32[]{:S(2)}) collective-permute-start(f32[264,128]{1,0:T(8,128)S(1)} %get-tuple-element.26), channel_id=1, source_target_pairs={{8,16},{0,24},{16,8},{24,0},{9,17},{1,25},{17,9},{25,1},{10,18},{2... | collective-permute-start | bytes 405512 | tf_op jit(solution)/shard_map/ppermute | solution.py:491
  13.2 12.8 %copy-start.5 = (f32[128]{0:T(128)S(1)}, f32[128]{0:T(128)}, u32[]{:S(2)}) copy-start(f32[128]{0:T(128)} %param.13) | copy-start | bytes 1540
  13.8 5.9 %collective-permute-start.6 = (f32[32,256]{1,0:T(8,128)S(1)}, f32[32,256]{1,0:T(8,128)S(1)}, u32[]{:S(2)}, u32[]{:S(2)}) collective-permute-start(f32[32,256]{1,0:T(8,128)S(1)} %mix.1), channel_id=1, source_target_pairs={{0,6},{1,7},{2,4},{3,5},{4,2},{5,3},{6,0},{7,1},{8,14},{9,15},{10,... | collective-permute-start | bytes 98312 | tf_op jit(solution)/shard_map/ppermute | solution.py:503
  17.4 4.8 %collective-permute-start.5 = (f32[32,256]{1,0:T(8,128)S(1)}, f32[32,256]{1,0:T(8,128)S(1)}, u32[]{:S(2)}, u32[]{:S(2)}) collective-permute-start(f32[32,256]{1,0:T(8,128)S(1)} %mix.1), channel_id=1, source_target_pairs={{0,4},{1,5},{2,6},{3,7},{4,0},{5,1},{6,2},{7,3},{8,12},{9,13},{10,... | collective-permute-start | bytes 98312 | tf_op jit(solution)/shard_map/ppermute | solution.py:503
  17.4 4.8 %collective-permute-start.4 = (f32[32,256]{1,0:T(8,128)S(1)}, f32[32,256]{1,0:T(8,128)S(1)}, u32[]{:S(2)}, u32[]{:S(2)}) collective-permute-start(f32[32,256]{1,0:T(8,128)S(1)} %mix.1), channel_id=1, source_target_pairs={{0,2},{1,3},{2,0},{3,1},{4,6},{5,7},{6,4},{7,5},{8,10},{9,11},{10,... | collective-permute-start | bytes 98312 | tf_op jit(solution)/shard_map/ppermute | solution.py:503
  22.2 1.4 %collective-permute-start.7 = (f32[128,256]{1,0:T(8,128)S(1)}, f32[128,256]{1,0:T(8,128)S(1)}, u32[]{:S(2)}, u32[]{:S(2)}) collective-permute-start(f32[128,256]{1,0:T(8,128)S(1)} %pad_maximum_fusion), channel_id=1, source_target_pairs={{0,1},{1,0},{2,3},{3,2},{4,5},{5,4},{6,7},{7,6},{8,9},{9,8},{10,11... | collective-permute-start | bytes 393224 | tf_op jit(solution)/shard_map/ppermute | solution.py:505
  23.7 6.8 %collective-permute-start.10 = (f32[24,256]{1,0:T(8,128)S(1)}, f32[24,256]{1,0:T(8,128)S(1)}, u32[]{:S(2)}, u32[]{:S(2)}) collective-permute-start(f32[24,256]{1,0:T(8,128)S(1)} %get-tuple-element.27), channel_id=1, source_target_pairs={{0,8},{16,24},{8,0},{24,16},{1,9},{17,25},{9,1},{25,17},{2,10},{18... | collective-permute-start | bytes 73736 | tf_op jit(solution)/shard_map/ppermute | solution.py:517
  25.2 5.3 %collective-permute-start.11 = (f32[24,256]{1,0:T(8,128)S(1)}, f32[24,256]{1,0:T(8,128)S(1)}, u32[]{:S(2)}, u32[]{:S(2)}) collective-permute-start(f32[24,256]{1,0:T(8,128)S(1)} %get-tuple-element.28), channel_id=1, source_target_pairs={{8,16},{0,24},{16,8},{24,0},{9,17},{1,25},{17,9},{25,1},{10,18},{2... | collective-permute-start | bytes 73736 | tf_op jit(solution)/shard_map/ppermute | solution.py:518
  26.0 1.2 %copy-start.6 = (f32[128]{0:T(128)S(1)}, f32[128]{0:T(128)}, u32[]{:S(2)}) copy-start(f32[128]{0:T(128)} %param.15) | copy-start | bytes 1540
